TPU v7x, 256 devices: a 4x2x16 block of a 4x16x16 slice. The times are simulated.
256 devices in a mesh: rep: 2 (over y), step: 32 (over z, core), patch: 4 (over x).
Axes of the slice: x: 4, y: 2, z: 16, core: 2. Of those that a mesh axis runs over, the one named last changes fastest.
The devices are a block of a 4x16x16 slice.
Arguments:
- latent_old: float32 [64, 1024, 64], P(('rep', 'step'), 'patch'), parts along dimension 0, may hold values from -6 to 6
- noise_start: float32 [2048, 64], P(('rep', 'patch')), parts along dimension 0, may hold values from -6 to 6
- step_index: int32 [64], P(('rep', 'step')), parts along dimension 0, may hold values from 0 to 998
- sigma_table: float32 [1000], replicated, may hold values from 0.02 to 1
- mod_weight: bfloat16 [256, 9216], replicated, may hold values from -0.375 to 0.375
- embed_weight: bfloat16 [64, 3072], replicated, may hold values from -0.75 to 0.75
- embed_bias: float32 [3072], replicated, may hold values from -3 to 3
- query_weight: bfloat16 [3072, 1536], P('step'), may hold values from -0.109375 to 0.109375
- query_gain: float32 [128], replicated, may hold values from 0.1 to 1.9
- stale_keys: bfloat16 [64, 1280, 1536], P(('rep', 'step'), 'patch'), parts along dimension 0, may hold values from -640 to 640
- stale_values: bfloat16 [64, 1280, 1536], P(('rep', 'step'), 'patch'), parts along dimension 0, may hold values from -6 to 6
- out_weight: bfloat16 [3072, 1536], P('step'), may hold values from -0.3125 to 0.3125
- final_weight: bfloat16 [3072, 64], replicated, may hold values from -0.109375 to 0.109375
Outputs:
- latent_new: float32 [64, 1024, 64], P(('rep', 'step'), 'patch'), parts along dimension 0
There are 2 independent parts, one for each index of `rep`. A program takes and returns all parts, laid end to end along the dimension named above; an argument that names none is the same for every part. Nothing has to cross between parts.
All inputs are finite; a program needn't handle non-finite values.
Results may differ from a plain program's by a relative error of at most 0.012.
The roundings to bfloat16 on the way count: a program that leaves them out, or rounds other values in their place, can miss the bound.
Values may be sent and summed in bfloat16 or wider, within the bound.
No kernel may reach another device: no remote copies, remote signals or barrier semaphores. Data moves between devices by JAX's collectives and lax.ppermute only.
A program may use at most 128 MiB of HBM per device.

v0:
```python
import math

import jax
import jax.numpy as jnp
from jax import lax
from jax.sharding import Mesh
from jax.sharding import PartitionSpec as P

D = 3072
HEAD = 128
FREQ = 256
STEP = ("step_0", "step_1")
REP_STEP = ("rep", "step_0", "step_1")


epsilon = 1e-06


def from_everyone(shard, axis):
    copies = jnp.broadcast_to(shard, (lax.axis_size(axis), *shard.shape))
    return lax.all_to_all(copies, axis, split_axis=0, concat_axis=0, tiled=True)


def in_order(pieces, dim):
    dims = list(pieces.shape[1:])
    dims[dim] *= pieces.shape[0]
    return jnp.moveaxis(pieces, 0, dim).reshape(dims)


def gather_directly(shard, axis, dim):
    pieces = from_everyone(shard, axis)
    return in_order(pieces, dim)


def side_by_side(arrays, axis, dim, along):
    ends, at = ([], 0)
    for a in arrays[:-1]:
        at += a.shape[along]
        ends.append(at)
    both = jnp.concatenate(arrays, axis=along)
    return tuple(jnp.split(gather_directly(both, axis, dim), ends, axis=along))


def neutral_like(shard, identity):
    return jnp.zeros_like(shard) + jnp.asarray(identity, shard.dtype)


def entering(shard, axes, combine, identity):
    before = start = neutral_like(shard, identity)
    running = shard
    for axis in reversed(axes):
        devices, here = (lax.axis_size(axis), lax.axis_index(axis))
        pieces = lax.all_gather(running.astype(jnp.bfloat16), axis)
        inside, running = (start, start)
        for k in range(devices):
            passed = k < here
            running = combine(running, pieces[k].astype(shard.dtype))
            inside = jnp.where(passed, running, inside)
        before = combine(inside, before)
    return before


def layer_norm(values_in):
    row_mean = jnp.mean(values_in, axis=-1, keepdims=True)
    centered = values_in - row_mean
    row_var = jnp.mean(centered * centered, axis=-1, keepdims=True)
    return centered * lax.rsqrt(row_var + epsilon)


def time_embed(sigma_now):
    half_count = FREQ // 2
    frequency = jnp.exp(
        -math.log(10000.0) * jnp.arange(half_count).astype(jnp.float32) / half_count
    )
    angles = 1000.0 * sigma_now * frequency
    return jnp.concatenate([jnp.cos(angles), jnp.sin(angles)])


def project_back(attended, weight_rows):
    return lax.dot_general(
        attended, weight_rows, (((1,), (1,)), ((), ())), preferred_element_type=jnp.float32
    )


def norm_queries(raw_queries, query_gain):
    token_count = raw_queries.shape[0]
    head_count = raw_queries.shape[1] // HEAD
    queries = raw_queries.reshape(token_count, head_count, HEAD)
    queries = (
        queries
        * lax.rsqrt(jnp.mean(queries * queries, axis=-1, keepdims=True) + epsilon)
        * query_gain
    )
    return queries.astype(jnp.bfloat16)


def empty_state(queries):
    token_count = queries.shape[0]
    head_count = queries.shape[1]
    return (
        jnp.full((head_count, token_count), -jnp.inf, jnp.float32),
        jnp.zeros((head_count, token_count), jnp.float32),
        jnp.zeros((head_count, token_count, HEAD), jnp.float32),
    )


def attend_block(queries, state_tuple, key_piece, value_piece):
    head_count = queries.shape[1]
    row_count = key_piece.shape[0]
    key_split = key_piece.reshape(row_count, head_count, HEAD)
    value_split = value_piece.reshape(row_count, head_count, HEAD)
    run_peak, run_total, run_sum = state_tuple
    scores = jnp.einsum(
        "qhd,khd->hqk", queries, key_split, preferred_element_type=jnp.float32
    ) / math.sqrt(HEAD)
    new_peak = jnp.max(scores, axis=-1)
    rescale = jnp.exp(run_peak - new_peak)
    exp_weights = jnp.exp(scores - new_peak[..., None])
    run_total = run_total * rescale + jnp.sum(exp_weights, axis=-1)
    run_sum = run_sum * rescale[..., None] + jnp.einsum(
        "hqk,khd->hqd",
        exp_weights.astype(jnp.bfloat16),
        value_split,
        preferred_element_type=jnp.float32,
    )
    return (new_peak, run_total, run_sum)


def finish_heads(state_tuple):
    final_peak, final_total, final_sum = state_tuple
    blended = final_sum / final_total[..., None]
    token_count = blended.shape[1]
    return jnp.transpose(blended, (1, 0, 2)).reshape(token_count, -1).astype(jnp.bfloat16)


def per_device(
    latent_old,
    noise_start,
    step_index,
    sigma_table,
    mod_weight,
    embed_weight,
    embed_bias,
    query_weight,
    query_gain,
    stale_keys,
    stale_values,
    out_weight,
    final_weight,
):
    step_slot = step_index[0]
    table_slots = jnp.arange(sigma_table.shape[0])
    sigma_now = jnp.sum(jnp.where(table_slots == step_slot, sigma_table, 0.0))
    sigma_next = jnp.sum(jnp.where(table_slots == step_slot + 1, sigma_table, 0.0))
    embedded = jax.nn.silu(time_embed(sigma_now)).astype(jnp.bfloat16)
    modulate = jnp.dot(embedded[None, :], mod_weight, preferred_element_type=jnp.float32)[0]
    width = D
    shift_vec = modulate[:width]
    scale_vec = modulate[width : 2 * width]
    gate_vec = modulate[2 * width :]
    latent = latent_old[0]
    token_count = latent.shape[0]
    hidden = (
        jnp.dot(latent.astype(jnp.bfloat16), embed_weight, preferred_element_type=jnp.float32)
        + embed_bias
    )
    normed = (layer_norm(hidden) * (1.0 + scale_vec) + shift_vec).astype(jnp.bfloat16)
    raw_queries = jnp.dot(
        normed,
        lax.all_gather(query_weight, STEP, axis=0, tiled=True),
        preferred_element_type=jnp.float32,
    )
    queries = norm_queries(raw_queries, query_gain)
    pieces = side_by_side((stale_keys[0], stale_values[0]), "patch", 0, 1)
    final_state = attend_block(queries, empty_state(queries), pieces[0], pieces[1])
    attended = finish_heads(final_state)
    branch = project_back(attended, lax.all_gather(out_weight, STEP, axis=0, tiled=True))
    mixed = hidden + gate_vec * branch
    velocity = jnp.dot(
        layer_norm(mixed).astype(jnp.bfloat16), final_weight, preferred_element_type=jnp.float32
    )
    drift_term = velocity * (sigma_next - sigma_now)
    flat_term = drift_term.reshape(-1, 128)

    def add_terms(earlier, later):
        return earlier + later

    prefix = entering(flat_term, STEP, add_terms, jnp.zeros_like(flat_term))
    result = noise_start + (prefix + flat_term).reshape(token_count, -1)
    return result[None]


def solution(mesh):
    torus = Mesh(
        mesh.devices.reshape(mesh.shape["rep"], 16, 2, mesh.shape["patch"]),
        ("rep", "step_0", "step_1", "patch"),
    )
    placed = (
        P(REP_STEP, "patch", None),
        P(("rep", "patch"), None),
        P(REP_STEP),
        P(),
        P(),
        P(),
        P(),
        P(STEP, None),
        P(),
        P(REP_STEP, "patch", None),
        P(REP_STEP, "patch", None),
        P(STEP, None),
        P(),
    )
    return jax.shard_map(
        per_device,
        mesh=torus,
        in_specs=placed,
        out_specs=P(REP_STEP, "patch", None),
        check_vma=False,
    )
```

profile of v0, /device:TPU:36, one launch (start us, length us, event | category | flops | bytes accessed | tf_op | source)
XLA Modules:
  0.0 225.6 jit_solution(14928748804721785456)
XLA Ops:
  6.5 0.0 copy-start
  6.6 0.0 all-gather.3.cloned.1.call-start
  6.6 0.7 all-gather.3.cloned.1.call-update
  7.3 0.1 all-gather.5.cloned.1.call-start
  7.4 0.7 all-gather.5.cloned.1.call-update
  8.1 1.7 pad_maximum_fusion
  9.8 4.1 %broadcast_in_dim.17 = bf16[4,320,3072]{2,1,0:T(8,128)(2,1)} broadcast(bf16[320,3072]{1,0:T(8,128)(2,1)S(1)} %pad_maximum_fusion), dimensions={1,2} | broadcast | bytes 9830400 | tf_op jit(solution)/shard_map/broadcast_in_dim | solution.py:20
  13.9 0.0 copy-start.7
  13.9 0.0 copy-start.6
  13.9 24.9 %all-to-all-start = ((bf16[4,320,3072]{2,1,0:T(8,128)(2,1)}), bf16[4,320,3072]{2,1,0:T(8,128)(2,1)}, u32[]{:S(2)}, u32[]{:S(2)}) async-start(bf16[4,320,3072]{2,1,0:T(8,128)(2,1)} %broadcast_in_dim.17), calls=%async_computation | async-start | bytes 15728640 | tf_op jit(solution)/shard_map/all_to_all | solution.py:21
  39.4 0.0 copy-done.7
  39.4 0.6 select_reduce_fusion
  41.9 0.0 copy-done
  42.0 0.0 copy-done.6
  42.0 1.5 fusion.46
  43.5 0.5 multiply_reduce_fusion.2
  44.0 3.2 %fusion.49 = f32[1,9216]{1,0:T(1,128)S(1)} fusion(bf16[256,1]{0,1:T(2,128)(2,1)S(1)} %reshape.197, bf16[256,9216]{1,0:T(8,128)(2,1)} %param.17), kind=kOutput, calls=%fused_computation.92 | convolution fusion | flops 4718592 | bytes 4755968 | tf_op jit(solution)/shard_map/dot_general | solution.py:156
  47.2 58.1 %all-to-all-done = bf16[4,320,3072]{2,1,0:T(8,128)(2,1)} async-done(((bf16[4,320,3072]{2,1,0:T(8,128)(2,1)}), bf16[4,320,3072]{2,1,0:T(8,128)(2,1)}, u32[]{:S(2)}, u32[]{:S(2)}) %all-to-all-start) | async-done | bytes 7864352 | tf_op jit(solution)/shard_map/all_to_all | solution.py:21
  105.3 5.5 %fusion.44 = (bf16[1280,1536]{1,0:T(8,128)(2,1)}, bf16[1280,1536]{1,0:T(8,128)(2,1)}) fusion(bf16[1280,3072]{1,0:T(8,128)(2,1)} %bitcast.6), kind=kLoop, calls=%fused_computation.87 | loop fusion | bytes 15728640 | tf_op jit(solution)/shard_map/split | solution.py:41
  110.9 6.3 %copy.31 = bf16[1280,1536]{0,1:T(8,128)(2,1)} copy(bf16[1280,1536]{1,0:T(8,128)(2,1)} %get-tuple-element.8) | data formatting | bytes 7864320 | tf_op jit(solution)/shard_map/split | solution.py:41
  117.2 6.2 %copy.28 = bf16[1280,1536]{0,1:T(8,128)(2,1)} copy(bf16[1280,1536]{1,0:T(8,128)(2,1)} %get-tuple-element.7) | data formatting | bytes 7864320 | tf_op jit(solution)/shard_map/split | solution.py:41
  123.4 0.0 all-gather.3.cloned.1.call-done
  123.4 0.0 copy-start.3
  123.4 0.0 copy-start.8
  123.4 6.9 %fusion.7 = f32[256,1536]{0,1:T(8,128)S(1)} fusion(bf16[3072,1536]{1,0:T(8,128)(2,1)} %all-gather.3.cloned.1.call-done, f32[256,3072]{1,0:T(8,128)S(1)} %get-tuple-element.15, f32[3072]{0:T(1024)S(1)} %get-tuple-element.12, f32[3072]{0:T(1024)S(1)} %get-tuple-element.13, f32[256]{0:T(256)S(1)} %add_rsqrt_fusion.2, f32[256]{0:T(256)S(1)} %broadcast_multiply_fusion.1), kind=kOutput, calls=%fused_computation.15 | convolution fusion | flops 2419851264 | bytes 14182400 | tf_op jit(solution)/shard_map/dot_general | solution.py:168
  130.3 0.1 multiply_reduce_fusion.3
  130.5 0.0 copy-done.3
  130.5 0.0 copy-done.8
  130.5 2.4 %multiply_reduce_fusion = (f32[12,256]{1,0:T(8,128)S(1)}, f32[12,256,1280]{2,1,0:T(8,128)S(1)}) fusion(bf16[1280,12,128]{0,2,1:T(8,128)(2,1)S(1)} %bitcast.39, f32[256,12,128]{0,2,1:T(8,128)S(1)} %bitcast.41, f32[128]{0:T(128)S(1)} %copy-done.8, f32[256,12]{0,1:T(8,128)S(1)} %add_rsqrt_fusion), kind=kOutput, calls=%fused_computation.1 | convolution fusion | flops 1015673856 | bytes 21258752 | tf_op jit(solution)/shard_map/qhd,khd->hqk/dot_general | solution.py:113
  132.9 0.0 copy-start.2
  132.9 3.3 %fusion = f32[12,256]{1,0:T(8,128)S(1)} fusion(f32[12,256,1280]{2,1,0:T(8,128)S(1)} %get-tuple-element.17, f32[12,256]{1,0:T(8,128)S(1)} %get-tuple-element.16), kind=kLoop, calls=%fused_computation.2 | loop fusion | flops 11793408 | bytes 15753216 | tf_op jit(solution)/shard_map/reduce_sum | solution.py:119
  136.3 2.2 copy-done.2
  138.5 11.0 %fusion.10 = bf16[256,12,128]{0,2,1:T(8,128)(2,1)} fusion(bf16[1280,12,128]{0,2,1:T(8,128)(2,1)} %bitcast.42, f32[12,256,1280]{2,1,0:T(8,128)} %copy-done.2, f32[12,256]{1,0:T(8,128)S(1)} %get-tuple-element.16, f32[256,12]{0,1:T(8,128)S(1)} %bitcast_add_fusion.1, f32[256,12]{0,1:T(8,128)S(1)} %multiply_bitcast_fusion), kind=kOutput, calls=%fused_computation.19 | convolution fusion | flops 1019609088 | bytes 20484096 | tf_op jit(solution)/shard_map/hqk,khd->hqd/dot_general | solution.py:120
  149.5 27.1 %all-gather.5.cloned.1.call-done = bf16[3072,1536]{1,0:T(8,128)(2,1)} async-done(((bf16[96,1536]{1,0:T(8,128)(2,1)}), bf16[3072,1536]{1,0:T(8,128)(2,1)}) %all-gather.5.cloned.1.call-update) | async-done | bytes 9437200 | tf_op jit(solution)/shard_map/all_gather | solution.py:177
  176.6 5.6 %fusion.47 = (f32[256]{0:T(256)S(1)}, f32[256,3072]{1,0:T(8,128)S(1)}) fusion(f32[256,3072]{1,0:T(8,128)S(1)} %get-tuple-element.15, bf16[256,1536]{0,1:T(8,128)(2,1)} %bitcast.46, bf16[3072,1536]{1,0:T(8,128)(2,1)} %all-gather.5.cloned.1.call-done, f32[3072]{0:T(1024)S(1)} %get-tuple-element.11), kind=kOutput, calls=%fused_computation.90 | convolution fusion | flops 2418278144 | bytes 16528384 | tf_op jit(solution)/shard_map/dot_general | solution.py:80
  182.2 0.0 copy-start.4
  182.3 0.5 multiply_reduce_fusion.1
  182.7 0.0 copy-start.1
  182.7 0.5 copy-done.4
  183.2 0.0 copy-start.5
  183.2 0.7 fusion.48
  183.9 0.1 copy.32
  184.0 0.1 convert_element_type.175
  184.1 1.9 all_gather.16
  186.1 31.1 %all_gather.17 = bf16[16,128,128]{2,1,0:T(8,128)(2,1)S(1)} all-gather(bf16[1,128,128]{2,1,0:T(8,128)(2,1)S(1)} %get-tuple-element.9), channel_id=1, replica_groups=mesh['rep'=2,'step_0'=16,'step_1'=2,'patch'=4] {'step_0'}, dimensions={0}, use_global_device_ids=true | all-gather | bytes 557056 | tf_op jit(solution)/shard_map/all_gather | solution.py:53
  217.2 0.1 convert_add_fusion.2
  217.3 0.1 select_n.183
  217.4 0.1 copy.37
  217.4 0.1 reshape.194
  217.5 0.1 copy.33
  217.6 0.1 fusion.36
  217.7 0.1 reshape.196
  217.8 0.1 copy.36
  217.9 0.1 reshape.163
  218.0 0.1 copy.34
  218.1 0.0 copy-done.5
  218.1 0.7 add_bitcast_fusion
  218.7 0.0 copy-done.1
  (13 shorter events, 0.1 us)
Async XLA Ops:
  6.5 35.4 %copy-start = (bf16[64,3072]{1,0:T(8,128)(2,1)S(1)}, bf16[64,3072]{1,0:T(8,128)(2,1)}, u32[]{:S(2)}) copy-start(bf16[64,3072]{1,0:T(8,128)(2,1)} %param.18) | copy-start | bytes 1179652
  6.6 116.8 %all-gather.3.cloned.1.call-start = ((), (), s32[]{:S(2)}) async-start(), calls=%async_computation.1 | async-start | bytes 9732096 | tf_op jit(solution)/shard_map/all_gather | solution.py:170
  7.3 169.3 %all-gather.5.cloned.1.call-start = ((), (), s32[]{:S(2)}) async-start(), calls=%async_computation.2 | async-start | bytes 9732096 | tf_op jit(solution)/shard_map/all_gather | solution.py:177
  13.9 25.5 %copy-start.7 = (f32[1000]{0:T(1024)S(1)}, f32[1000]{0:T(1024)}, u32[]{:S(2)}) copy-start(f32[1000]{0:T(1024)} %param.16) | copy-start | bytes 12004
  13.9 28.1 %copy-start.6 = (f32[3072]{0:T(1024)S(1)}, f32[3072]{0:T(1024)}, u32[]{:S(2)}) copy-start(f32[3072]{0:T(1024)} %param.19) | copy-start | bytes 36868
  13.9 91.4 %all-to-all-start = ((bf16[4,320,3072]{2,1,0:T(8,128)(2,1)}), bf16[4,320,3072]{2,1,0:T(8,128)(2,1)}, u32[]{:S(2)}, u32[]{:S(2)}) async-start(bf16[4,320,3072]{2,1,0:T(8,128)(2,1)} %broadcast_in_dim.17), calls=%async_computation | async-start | bytes 15728640 | tf_op jit(solution)/shard_map/all_to_all | solution.py:21
  123.4 7.1 %copy-start.3 = (bf16[1280,1536]{0,1:T(8,128)(2,1)S(1)}, bf16[1280,1536]{0,1:T(8,128)(2,1)}, u32[]{:S(2)}) copy-start(bf16[1280,1536]{0,1:T(8,128)(2,1)} %copy.28) | copy-start | bytes 11796484
  123.4 7.1 %copy-start.8 = (f32[128]{0:T(128)S(1)}, f32[128]{0:T(128)}, u32[]{:S(2)}) copy-start(f32[128]{0:T(128)} %param.21) | copy-start | bytes 1540
  132.9 5.5 %copy-start.2 = (f32[12,256,1280]{2,1,0:T(8,128)}, f32[12,256,1280]{2,1,0:T(8,128)S(1)}, u32[]{:S(2)}) copy-start(f32[12,256,1280]{2,1,0:T(8,128)S(1)} %get-tuple-element.17) | copy-start | bytes 47185924
  182.2 1.0 copy-start.4
  182.7 36.0 %copy-start.1 = (bf16[64,3072]{1,0:T(8,128)(2,1)S(1)}, bf16[64,3072]{1,0:T(8,128)(2,1)}, u32[]{:S(2)}) copy-start(bf16[64,3072]{1,0:T(8,128)(2,1)} %param.18) | copy-start | bytes 1179652
  183.2 34.8 %copy-start.5 = (f32[256,64]{0,1:T(8,128)S(1)}, f32[256,64]{0,1:T(8,128)}, u32[]{:S(2)}) copy-start(f32[256,64]{0,1:T(8,128)} %param.14) | copy-start | bytes 196612
Sparse Core Ops, SparseCore 0:
  9.2 91.4 all-gather.2
  102.6 73.9 all-gather.4
where the time goes:
time: 226 us
  waiting for transfers between devices  86.8 us (38%)
  blocking collectives  33 us (15%)
  matrix products  31.3 us (14%)
  local copies, waits for them, and re-layouts  25.8 us (11%)
  starting transfers between devices  24.9 us (11%)
  between operations  16.2 us (7%)
  other arithmetic  7.65 us (3%)
    all_to_all x1, waiting for transfers between devices, from_everyone(): return lax.all_to_all(copies, axis, split_axis=0, concat_axis=0, tiled=True)  58.1 us
    all_gather x2, blocking collectives, entering(): pieces = lax.all_gather(running.astype(jnp.bfloat16), axis)  33 us
    all_gather x1, waiting for transfers between devices, per_device(): lax.all_gather(out_weight, STEP, axis=0, tiled=True)  27.1 us
    all_to_all x1, starting transfers between devices, from_everyone(): return lax.all_to_all(copies, axis, split_axis=0, concat_axis=0, tiled=True)  24.9 us
    split x3, local copies, waits for them, and re-layouts, side_by_side(): return tuple(jnp.split(gather_directly(both, axis, dim), ends, axis=along))  18.1 us
    dot_general x1, matrix products, attend_block(): jnp.einsum('hqk,khd->hqd', exp_weights.astype(jnp.bfloat16), value_split,...  11 us
    dot_general x1, matrix products, per_device(): jnp.dot(normed, lax.all_gather(query_weight, STEP, axis=0, tiled=True), p...  6.91 us
    dot_general x1, matrix products, project_back(): lax.dot_general(attended, weight_rows, (((1,), (1,)), ((), ())), preferre...  5.63 us
  transfers between devices with their start and end apart: 3, of which 2 were waited for; matrix products, arithmetic and copies ran while one was open for 24% of the time, Pallas kernels for 0%

commit v1 on v0

v1 whole, which is shorter than its diff:
```python
import functools
import math

import jax
import jax.numpy as jnp
from jax import lax
from jax.experimental import pallas as pl
from jax.experimental.pallas import tpu as pltpu
from jax.sharding import Mesh
from jax.sharding import PartitionSpec as P

HEAD = 128
CORES = 2
STEP = ("chip", "core")
REP_STEP = ("rep", "chip", "core")
epsilon = 1e-06


def shift(value, axis, distance, wrap):
    size = lax.axis_size(axis)
    pairs = [(i, (i + distance) % size) for i in range(size) if wrap or 0 <= i + distance < size]
    return lax.ppermute(value, axis, pairs)


def ring_gather(shard, axis):
    size, here = lax.axis_size(axis), lax.axis_index(axis)
    held = jnp.zeros((size, *shard.shape), shard.dtype)

    def put(held, piece, owner):
        return lax.dynamic_update_slice_in_dim(held, piece[None], lax.rem(owner + size, size), 0)

    held = put(held, shard, here)
    up = down = shard
    for hop in range(1, size // 2 + 1):
        up = shift(up, axis, 1, True)
        held = put(held, up, here - hop)
        if hop < size - size // 2:
            down = shift(down, axis, -1, True)
            held = put(held, down, here + hop)
    return held


def both_cores(own, axis):
    other = shift(own, axis, 1, True)
    first = lax.axis_index(axis) == 0
    return jnp.stack([jnp.where(first, own, other), jnp.where(first, other, own)], axis=1)


def layer_norm(values_in):
    row_mean = jnp.mean(values_in, axis=-1, keepdims=True)
    centered = values_in - row_mean
    row_var = jnp.mean(centered * centered, axis=-1, keepdims=True)
    return centered * lax.rsqrt(row_var + epsilon)


def time_embed(sigma_now, half_count):
    frequency = jnp.exp(
        -math.log(10000.0) * jnp.arange(half_count).astype(jnp.float32) / half_count
    )
    angles = 1000.0 * sigma_now * frequency
    return jnp.concatenate([jnp.cos(angles), jnp.sin(angles)])


def attention_body(query_ref, gain_ref, key_ref, value_ref, out_ref):
    raw = query_ref[...]
    normed = raw * lax.rsqrt(jnp.mean(raw * raw, axis=-1, keepdims=True) + epsilon) * gain_ref[...]
    scores = lax.dot_general(
        normed.astype(jnp.bfloat16),
        key_ref[...],
        (((1,), (1,)), ((), ())),
        preferred_element_type=jnp.float32,
    )
    peak = jnp.max(scores, axis=-1, keepdims=True)
    weights = jnp.exp((scores - peak) * (1.0 / math.sqrt(HEAD)))
    total = jnp.sum(weights, axis=-1, keepdims=True)
    blended = jnp.dot(
        weights.astype(jnp.bfloat16), value_ref[...], preferred_element_type=jnp.float32
    )
    out_ref[...] = (blended / total).astype(jnp.bfloat16)


def attention(raw_queries, query_gain, keys, values):
    tokens, width = raw_queries.shape
    key_count = keys.shape[0]
    tile = min(256, tokens)
    heads = width // HEAD
    work = tokens * key_count * width
    return pl.pallas_call(
        attention_body,
        grid=(heads, tokens // tile),
        in_specs=[
            pl.BlockSpec((tile, HEAD), lambda h, t: (t, h)),
            pl.BlockSpec((1, HEAD), lambda h, t: (0, 0)),
            pl.BlockSpec((key_count, HEAD), lambda h, t: (0, h)),
            pl.BlockSpec((key_count, HEAD), lambda h, t: (0, h)),
        ],
        out_specs=pl.BlockSpec((tile, HEAD), lambda h, t: (t, h)),
        out_shape=jax.ShapeDtypeStruct((tokens, width), jnp.bfloat16),
        cost_estimate=pl.CostEstimate(
            flops=4 * work,
            bytes_accessed=4 * key_count * width + 6 * tokens * width,
            transcendentals=work // HEAD,
        ),
        name="attention",
    )(raw_queries, query_gain.reshape(1, HEAD), keys, values)


def prefix_over_steps(drift):
    core = lax.axis_index("core")
    rows = drift.shape[0] // CORES
    sent = drift.astype(jnp.bfloat16)
    other = shift(sent, "core", 1, True).astype(jnp.float32)
    within = jnp.where(core == 1, other, jnp.zeros_like(other))
    chip_total = drift + other
    mine = lax.dynamic_slice_in_dim(chip_total, core * rows, rows, 0)
    group = 4
    sent = mine.astype(jnp.bfloat16)
    near = [shift(sent, "chip", d, False) for d in range(1, group)]
    before = functools.reduce(lambda a, b: a + b, [n.astype(jnp.float32) for n in near])
    window = (mine + before).astype(jnp.bfloat16)
    size = lax.axis_size("chip")
    far = [shift(window, "chip", d, False) for d in range(group, size, group)]
    before = functools.reduce(lambda a, b: a + b, [f.astype(jnp.float32) for f in far], before)
    halves = lax.all_gather(before.astype(jnp.bfloat16), "core", axis=0, tiled=True)
    return within + halves.astype(jnp.float32)


def per_device(
    latent_old,
    noise_start,
    step_index,
    sigma_table,
    mod_weight,
    embed_weight,
    embed_bias,
    query_weight,
    query_gain,
    stale_keys,
    stale_values,
    out_weight,
    final_weight,
):
    parts, part = lax.axis_size("patch"), lax.axis_index("patch")
    width = embed_weight.shape[1]
    columns = query_weight.shape[1] // parts
    latent = latent_old[0].astype(jnp.bfloat16)
    token_count, channels = latent.shape
    key_rows = stale_keys.shape[1]

    all_out_weight = lax.all_gather(out_weight, STEP, axis=0, tiled=True)

    def by_part(rows):
        return jnp.moveaxis(rows.reshape(rows.shape[0], parts, columns), 1, 0)

    spare = -(-latent.size // columns)
    spare += -spare % 16
    packed = jnp.pad(latent.reshape(-1), (0, spare * columns - latent.size))
    packed = jnp.broadcast_to(packed.reshape(1, spare, columns), (parts, spare, columns))
    sent = [by_part(stale_keys[0]), by_part(stale_values[0]), packed]
    got = lax.all_to_all(jnp.concatenate(sent, axis=1), "patch", 0, 0, tiled=True)
    keys = got[:, :key_rows].reshape(-1, columns)
    values = got[:, key_rows : 2 * key_rows].reshape(-1, columns)
    all_latent = got[:, 2 * key_rows :].reshape(parts, -1)[:, : latent.size]
    all_latent = all_latent.reshape(parts * token_count, channels)

    my_columns = lax.dynamic_slice_in_dim(query_weight, part * columns, columns, 1)
    gathered = both_cores(ring_gather(my_columns, "chip"), "core").reshape(-1, columns)

    step_slot = step_index[0]
    table_slots = jnp.arange(sigma_table.shape[0])
    sigma_now = jnp.sum(jnp.where(table_slots == step_slot, sigma_table, 0.0))
    sigma_next = jnp.sum(jnp.where(table_slots == step_slot + 1, sigma_table, 0.0))
    embedded = jax.nn.silu(time_embed(sigma_now, mod_weight.shape[0] // 2)).astype(jnp.bfloat16)
    modulate = jnp.dot(embedded[None, :], mod_weight, preferred_element_type=jnp.float32)[0]
    shift_vec = modulate[:width]
    scale_vec = modulate[width : 2 * width]
    gate_vec = modulate[2 * width :]

    def embed(rows):
        return jnp.dot(rows, embed_weight, preferred_element_type=jnp.float32) + embed_bias

    normed = (layer_norm(embed(all_latent)) * (1.0 + scale_vec) + shift_vec).astype(jnp.bfloat16)
    normed = lax.optimization_barrier(normed)
    raw_queries = jnp.dot(normed, gathered, preferred_element_type=jnp.float32)
    attended = attention(raw_queries, query_gain, keys, values)
    attended = lax.all_to_all(
        attended.reshape(parts, token_count, columns), "patch", 0, 0, tiled=True
    )
    attended = jnp.moveaxis(attended, 0, 1).reshape(token_count, -1)
    hidden = embed(latent)
    branch = lax.dot_general(
        attended, all_out_weight, (((1,), (1,)), ((), ())), preferred_element_type=jnp.float32
    )
    mixed = hidden + gate_vec * branch
    velocity = jnp.dot(
        layer_norm(mixed).astype(jnp.bfloat16), final_weight, preferred_element_type=jnp.float32
    )
    drift_term = (velocity * (sigma_next - sigma_now)).reshape(-1, HEAD)
    prefix = prefix_over_steps(drift_term)
    return (noise_start + (prefix + drift_term).reshape(token_count, -1))[None]


def solution(mesh):
    shape = mesh.shape
    torus = Mesh(
        mesh.devices.reshape(shape["rep"], shape["step"] // CORES, CORES, shape["patch"]),
        ("rep", "chip", "core", "patch"),
    )
    placed = (
        P(REP_STEP, "patch", None),
        P(("rep", "patch"), None),
        P(REP_STEP),
        P(),
        P(),
        P(),
        P(),
        P(STEP, None),
        P(),
        P(REP_STEP, "patch", None),
        P(REP_STEP, "patch", None),
        P(STEP, None),
        P(),
    )
    return jax.shard_map(
        per_device,
        mesh=torus,
        in_specs=placed,
        out_specs=P(REP_STEP, "patch", None),
        check_vma=False,
    )
```

time: 226 us -> 196 us (0.87)
  the two profiles are of different devices: /device:TPU:36 before, /device:TPU:33 now
where the time goes in v1:
time: 196 us; the launch traced here: 195 us
  starting transfers between devices  81 us (41%)
  waiting for transfers between devices  27.2 us (14%)
  local copies, waits for them, and re-layouts  25.1 us (13%)
  between operations  16.5 us (8%)
  matrix products  16.2 us (8%)
  Pallas kernels  13.8 us (7%)
  other arithmetic  11.2 us (6%)
  blocking collectives  4.11 us (2%)
    ppermute x23, starting transfers between devices, shift(): return lax.ppermute(value, axis, pairs)  70.2 us
    ppermute x23, waiting for transfers between devices, shift(): return lax.ppermute(value, axis, pairs)  15.6 us
    pallas_call x1, Pallas kernels, attention(): pl.pallas_call(attention_body, grid=(heads, tokens // tile), in_specs=[pl...  13.8 us
    dynamic_update_slice x16, local copies, waits for them, and re-layouts, put(): lax.dynamic_update_slice_in_dim(held, piece[None], lax.rem(owner + size,...  12.8 us
    all_to_all x1, waiting for transfers between devices, per_device(): lax.all_to_all(attended.reshape(parts, token_count, columns), 'patch', 0,...  10.8 us
    all_to_all x1, starting transfers between devices, per_device(): lax.all_to_all(attended.reshape(parts, token_count, columns), 'patch', 0,...  6.31 us
    dot_general x1, matrix products, per_device(): lax.dot_general(attended, all_out_weight, (((1,), (1,)), ((), ())), prefe...  5.26 us
    another operation x2, local copies, waits for them, and re-layouts, by_part(): return jnp.moveaxis(rows.reshape(rows.shape[0], parts, columns), 1, 0)  4.6 us
  transfers between devices with their start and end apart: 26, of which 13 were waited for; matrix products, arithmetic and copies ran while one was open for 22% of the time, Pallas kernels for 7%

profile of v1, /device:TPU:33, one launch (start us, length us, event | category | flops | bytes accessed | tf_op | source)
XLA Modules:
  0.0 195.0 jit_solution(2380305383867483790)
XLA Ops:
  6.6 0.7 all-gather.2.cloned.1.call-update
  7.4 1.5 bitcast_dynamic-update-slice_fusion.15
  9.0 3.3 %collective-permute-start = (bf16[96,384]{1,0:T(8,128)(2,1)}, bf16[96,384]{1,0:T(8,128)(2,1)}, u32[]{:S(2)}, u32[]{:S(2)}) collective-permute-start(bf16[96,384]{1,0:T(8,128)(2,1)} %get-tuple-element.8), channel_id=1, source_target_pairs={{0,8},{8,16},{16,24},{24,32},{32,40},{40,48},{48,56},{56,64},{64,7... | collective-permute-start | bytes 221192 | tf_op jit(solution)/shard_map/ppermute | solution.py:22
  12.3 19.6 %collective-permute-start.1 = (bf16[96,384]{1,0:T(8,128)(2,1)}, bf16[96,384]{1,0:T(8,128)(2,1)}, u32[]{:S(2)}, u32[]{:S(2)}) collective-permute-start(bf16[96,384]{1,0:T(8,128)(2,1)} %get-tuple-element.8), channel_id=1, source_target_pairs={{0,120},{8,0},{16,8},{24,16},{32,24},{40,32},{48,40},{56,48},{64,5... | collective-permute-start | bytes 221192 | tf_op jit(solution)/shard_map/ppermute | solution.py:22
  31.9 0.8 convert_element_type.61
  33.0 1.9 reshape_squeeze.7
  34.9 2.7 %reshape_squeeze.6 = bf16[320,4,384]{2,1,0:T(4,128)(2,1)} reshape(bf16[1,320,1536]{2,1,0:T(8,128)(2,1)} %param.22) | data formatting | bytes 1966080 | tf_op jit(solution)/shard_map/reshape;squeeze | solution.py:153
  37.6 1.5 copy_bitcast_fusion
  39.1 1.6 pad_maximum_fusion.1
  40.7 4.5 %all-to-all-start = ((bf16[4,688,384]{2,1,0:T(8,128)(2,1)}), bf16[4,688,384]{2,1,0:T(8,128)(2,1)S(1)}, u32[]{:S(2)}, u32[]{:S(2)}) async-start(bf16[4,688,384]{2,1,0:T(8,128)(2,1)} %pad_maximum_fusion.1), calls=%async_computation | async-start | bytes 4227072 | tf_op jit(solution)/shard_map/all_to_all | solution.py:160
  45.8 0.7 select_reduce_fusion
  47.2 3.2 %fusion.13 = f32[1,9216]{1,0:T(1,128)S(1)} fusion(bf16[256,1]{0,1:T(2,128)(2,1)S(1)} %reshape.82, bf16[256,9216]{1,0:T(8,128)(2,1)} %param.17), kind=kOutput, calls=%fused_computation.62 | convolution fusion | flops 4718592 | bytes 4755968 | tf_op jit(solution)/shard_map/dot_general | solution.py:174
  50.6 2.6 %collective-permute-start.3 = (bf16[96,384]{1,0:T(8,128)(2,1)}, bf16[96,384]{1,0:T(8,128)(2,1)S(1)}, u32[]{:S(2)}, u32[]{:S(2)}) collective-permute-start(bf16[96,384]{1,0:T(8,128)(2,1)} %collective-permute-done.1), channel_id=1, source_target_pairs={{0,120},{8,0},{16,8},{24,16},{32,24},{40,32},{48,40},{56,48},{64,5... | collective-permute-start | bytes 221192 | tf_op jit(solution)/shard_map/ppermute | solution.py:22
  53.3 1.5 bitcast_dynamic-update-slice_fusion.14
  54.8 1.5 bitcast_dynamic-update-slice_fusion.13
  56.3 1.0 collective-permute-done.2
  57.3 2.7 %collective-permute-start.5 = (bf16[96,384]{1,0:T(8,128)(2,1)S(1)}, bf16[96,384]{1,0:T(8,128)(2,1)S(1)}, u32[]{:S(2)}, u32[]{:S(2)}) collective-permute-start(bf16[96,384]{1,0:T(8,128)(2,1)S(1)} %collective-permute-done.3), channel_id=1, source_target_pairs={{0,120},{8,0},{16,8},{24,16},{32,24},{40,32},{48,40},{56,48},{64,5... | collective-permute-start | bytes 221192 | tf_op jit(solution)/shard_map/ppermute | solution.py:22
  60.6 0.6 bitcast_dynamic-update-slice_fusion.11
  61.2 1.7 collective-permute-done.4
  62.9 2.9 %collective-permute-start.7 = (bf16[96,384]{1,0:T(8,128)(2,1)S(1)}, bf16[96,384]{1,0:T(8,128)(2,1)S(1)}, u32[]{:S(2)}, u32[]{:S(2)}) collective-permute-start(bf16[96,384]{1,0:T(8,128)(2,1)S(1)} %collective-permute-done.5), channel_id=1, source_target_pairs={{0,120},{8,0},{16,8},{24,16},{32,24},{40,32},{48,40},{56,48},{64,5... | collective-permute-start | bytes 221192 | tf_op jit(solution)/shard_map/ppermute | solution.py:22
  65.8 0.6 bitcast_dynamic-update-slice_fusion.10
  66.5 0.6 bitcast_dynamic-update-slice_fusion.9
  67.1 1.7 collective-permute-done.6
  68.8 3.2 %collective-permute-start.9 = (bf16[96,384]{1,0:T(8,128)(2,1)S(1)}, bf16[96,384]{1,0:T(8,128)(2,1)S(1)}, u32[]{:S(2)}, u32[]{:S(2)}) collective-permute-start(bf16[96,384]{1,0:T(8,128)(2,1)S(1)} %collective-permute-done.7), channel_id=1, source_target_pairs={{0,120},{8,0},{16,8},{24,16},{32,24},{40,32},{48,40},{56,48},{64,5... | collective-permute-start | bytes 221192 | tf_op jit(solution)/shard_map/ppermute | solution.py:22
  72.0 0.6 bitcast_dynamic-update-slice_fusion.8
  72.6 0.6 bitcast_dynamic-update-slice_fusion.7
  73.2 1.5 collective-permute-done.8
  74.8 3.5 %collective-permute-start.11 = (bf16[96,384]{1,0:T(8,128)(2,1)S(1)}, bf16[96,384]{1,0:T(8,128)(2,1)S(1)}, u32[]{:S(2)}, u32[]{:S(2)}) collective-permute-start(bf16[96,384]{1,0:T(8,128)(2,1)S(1)} %collective-permute-done.9), channel_id=1, source_target_pairs={{0,120},{8,0},{16,8},{24,16},{32,24},{40,32},{48,40},{56,48},{64,5... | collective-permute-start | bytes 221192 | tf_op jit(solution)/shard_map/ppermute | solution.py:22
  78.9 0.6 bitcast_dynamic-update-slice_fusion.5
  79.5 1.1 collective-permute-done.10
  80.8 3.6 %collective-permute-start.13 = (bf16[96,384]{1,0:T(8,128)(2,1)S(1)}, bf16[96,384]{1,0:T(8,128)(2,1)S(1)}, u32[]{:S(2)}, u32[]{:S(2)}) collective-permute-start(bf16[96,384]{1,0:T(8,128)(2,1)S(1)} %collective-permute-done.11), channel_id=1, source_target_pairs={{0,120},{8,0},{16,8},{24,16},{32,24},{40,32},{48,40},{56,48},{64,5... | collective-permute-start | bytes 221192 | tf_op jit(solution)/shard_map/ppermute | solution.py:22
  84.5 0.6 bitcast_dynamic-update-slice_fusion.4
  85.1 0.6 bitcast_dynamic-update-slice_fusion.3
  85.7 1.0 collective-permute-done.12
  86.7 0.6 bitcast_dynamic-update-slice_fusion.2
  87.4 0.6 bitcast_dynamic-update-slice_fusion.1
  88.0 5.0 %collective-permute-done.14 = bf16[96,384]{1,0:T(8,128)(2,1)S(1)} collective-permute-done((bf16[96,384]{1,0:T(8,128)(2,1)S(1)}, bf16[96,384]{1,0:T(8,128)(2,1)S(1)}, u32[]{:S(2)}, u32[]{:S(2)}) %collective-permute-start.14) | collective-permute-done | bytes 73760 | tf_op jit(solution)/shard_map/ppermute | solution.py:22
  93.0 0.6 bitcast_dynamic-update-slice_fusion
  93.7 5.6 %collective-permute-start.15 = (bf16[16,96,384]{2,1,0:T(8,128)(2,1)}, bf16[16,96,384]{2,1,0:T(8,128)(2,1)}, u32[]{:S(2)}, u32[]{:S(2)}) collective-permute-start(bf16[16,96,384]{2,1,0:T(8,128)(2,1)} %bitcast_dynamic-update-slice_fusion), channel_id=1, source_target_pairs={{0,4},{4,0},{1,5},{5,1},{2,6},{6,2},{3,7},{7,3},{8,12},{12,8},{9,1... | collective-permute-start | bytes 3538952 | tf_op jit(solution)/shard_map/ppermute | solution.py:22
  99.7 1.9 add_reduce_fusion
  101.5 1.8 multiply_reduce_fusion
  103.4 3.8 %add_convert_fusion = bf16[1024,3072]{1,0:T(8,128)(2,1)S(1)} fusion(f32[1024,3072]{1,0:T(8,128)S(1)} %get-tuple-element.17, f32[3072]{0:T(1024)S(1)} %get-tuple-element.14, f32[3072]{0:T(1024)S(1)} %get-tuple-element.15, f32[1024]{0:T(1024)S(1)} %add_rsqrt_fusion, f32[1024]{0:T(1024)S(1)} %broadcast_multiply_fusion, f32[3072]{0:T(1024)S(1)} %copy-done.4), kind=kLoop, calls=%fused_computation | loop fusion | flops 18874368 | bytes 18919424 | tf_op jit(solution)/shard_map/convert_element_type | solution.py:182
  107.2 1.5 fusion.10
  108.8 1.5 select_bitcast_fusion.1
  110.5 4.6 %fusion.14.query_ref = f32[1024,384]{1,0:T(8,128)} fusion(bf16[1024,3072]{1,0:T(8,128)(2,1)S(1)} %add_convert_fusion, bf16[3072,384]{1,0:T(8,128)(2,1)S(1)} %bitcast.74), kind=kOutput, calls=%fused_computation.63 | convolution fusion | flops 2415919104 | bytes 10223616 | tf_op jit(solution)/shard_map/dot_general | solution.py:184
  115.1 13.8 %attention.1 = bf16[1024,384]{1,0:T(8,128)(2,1)} custom-call(f32[1024,384]{1,0:T(8,128)} %fusion.14.query_ref, f32[1,128]{1,0:T(1,128)} %bitcast.81, bf16[1280,384]{1,0:T(8,128)(2,1)} %bitcast.76, bf16[1280,384]{1,0:T(8,128)(2,1)} %bitcast.75), custom_call_target="tpu_custom_call" | custom-call | flops 2013265920 | bytes 4325376 | tf_op jit(solution)/shard_map/attention/pallas_call | solution.py:88
  128.9 2.3 %copy.20 = bf16[4,256,384]{1,2,0:T(8,128)(2,1)} copy(bf16[4,256,384]{2,1,0:T(8,128)(2,1)} %bitcast.78) | data formatting | bytes 1572864 | tf_op jit(solution)/shard_map/reshape | solution.py:187
  131.2 6.3 %all-to-all-start.1 = ((bf16[4,256,384]{1,2,0:T(8,128)(2,1)}), bf16[4,256,384]{1,2,0:T(8,128)(2,1)S(1)}, u32[]{:S(2)}, u32[]{:S(2)}) async-start(bf16[4,256,384]{1,2,0:T(8,128)(2,1)} %copy.20), calls=%async_computation.1 | async-start | bytes 1572864 | tf_op jit(solution)/shard_map/all_to_all | solution.py:186
  138.8 10.8 %all-to-all-done.1 = bf16[4,256,384]{1,2,0:T(8,128)(2,1)S(1)} async-done(((bf16[4,256,384]{1,2,0:T(8,128)(2,1)}), bf16[4,256,384]{1,2,0:T(8,128)(2,1)S(1)}, u32[]{:S(2)}, u32[]{:S(2)}) %all-to-all-start.1) | async-done | bytes 786464 | tf_op jit(solution)/shard_map/all_to_all | solution.py:186
  149.6 5.3 %convolution_multiply_fusion = f32[256,3072]{1,0:T(8,128)S(1)} fusion(bf16[256,1536]{0,1:T(8,128)(2,1)S(1)} %bitcast.77, bf16[3072,1536]{1,0:T(8,128)(2,1)} %all-gather.2.cloned.1.call-done, f32[3072]{0:T(1024)S(1)} %get-tuple-element.13), kind=kOutput, calls=%fused_computation.5 | convolution fusion | flops 2416705536 | bytes 13381632 | tf_op jit(solution)/shard_map/dot_general | solution.py:191
  154.9 0.7 fusion.12
  156.6 0.7 fusion.4
  157.5 1.3 collective-permute-start.16
  158.7 0.9 collective-permute-done.16
  159.6 1.3 collective-permute-start.19
  160.9 1.3 collective-permute-start.18
  162.2 1.3 collective-permute-start.17
  163.6 0.8 collective-permute-done.17
  164.4 9.6 %collective-permute-start.22 = (bf16[64,128]{1,0:T(8,128)(2,1)S(1)}, bf16[64,128]{1,0:T(8,128)(2,1)S(1)}, u32[]{:S(2)}, u32[]{:S(2)}) collective-permute-start(bf16[64,128]{1,0:T(8,128)(2,1)S(1)} %add_convert_fusion.2), channel_id=1, source_target_pairs={{0,96},{8,104},{16,112},{24,120},{1,97},{9,105},{17,113},{25,121},... | collective-permute-start | bytes 49160 | tf_op jit(solution)/shard_map/ppermute | solution.py:22
  174.0 5.7 %collective-permute-start.21 = (bf16[64,128]{1,0:T(8,128)(2,1)S(1)}, bf16[64,128]{1,0:T(8,128)(2,1)S(1)}, u32[]{:S(2)}, u32[]{:S(2)}) collective-permute-start(bf16[64,128]{1,0:T(8,128)(2,1)S(1)} %add_convert_fusion.2), channel_id=1, source_target_pairs={{0,64},{8,72},{16,80},{24,88},{32,96},{40,104},{48,112},{56,120},{... | collective-permute-start | bytes 49160 | tf_op jit(solution)/shard_map/ppermute | solution.py:22
  179.7 2.7 %collective-permute-start.20 = (bf16[64,128]{1,0:T(8,128)(2,1)S(1)}, bf16[64,128]{1,0:T(8,128)(2,1)S(1)}, u32[]{:S(2)}, u32[]{:S(2)}) collective-permute-start(bf16[64,128]{1,0:T(8,128)(2,1)S(1)} %add_convert_fusion.2), channel_id=1, source_target_pairs={{0,32},{8,40},{16,48},{24,56},{32,64},{40,72},{48,80},{56,88},{64,... | collective-permute-start | bytes 49160 | tf_op jit(solution)/shard_map/ppermute | solution.py:22
  182.5 0.7 collective-permute-done.20
  183.2 4.1 %all_gather.7 = bf16[128,128]{1,0:T(8,128)(2,1)S(1)} all-gather(bf16[64,128]{1,0:T(8,128)(2,1)S(1)} %add_convert_fusion.1), channel_id=1, replica_groups=mesh['rep'=2,'chip'=16,'core'=2,'patch'=4] {'core'}, dimensions={0}, use_global_device_ids=true | all-gather | bytes 49152 | tf_op jit(solution)/shard_map/all_gather | solution.py:124
  187.4 0.7 copy.23
  (70 shorter events, 4.3 us)
Async XLA Ops:
  6.5 93.1 %copy-start = (bf16[64,3072]{1,0:T(8,128)(2,1)S(1)}, bf16[64,3072]{1,0:T(8,128)(2,1)}, u32[]{:S(2)}) copy-start(bf16[64,3072]{1,0:T(8,128)(2,1)} %param.18) | copy-start | bytes 1179652
  6.6 143.0 %all-gather.2.cloned.1.call-start = ((), (), s32[]{:S(2)}) async-start(), calls=%async_computation.2 | async-start | bytes 9732096 | tf_op jit(solution)/shard_map/all_gather | solution.py:150
  9.0 28.6 %copy-start.1 = (bf16[16,96,384]{2,1,0:T(8,128)(2,1)}, bf16[16,96,384]{2,1,0:T(8,128)(2,1)S(1)}, u32[]{:S(2)}) copy-start(bf16[16,96,384]{2,1,0:T(8,128)(2,1)S(1)} %get-tuple-element.7) | copy-start | bytes 3538948
  9.0 41.5 %collective-permute-start = (bf16[96,384]{1,0:T(8,128)(2,1)}, bf16[96,384]{1,0:T(8,128)(2,1)}, u32[]{:S(2)}, u32[]{:S(2)}) collective-permute-start(bf16[96,384]{1,0:T(8,128)(2,1)} %get-tuple-element.8), channel_id=1, source_target_pairs={{0,8},{8,16},{16,24},{24,32},{32,40},{40,48},{48,56},{56,64},{64,7... | collective-permute-start | bytes 221192 | tf_op jit(solution)/shard_map/ppermute | solution.py:22
  12.3 38.3 %collective-permute-start.1 = (bf16[96,384]{1,0:T(8,128)(2,1)}, bf16[96,384]{1,0:T(8,128)(2,1)}, u32[]{:S(2)}, u32[]{:S(2)}) collective-permute-start(bf16[96,384]{1,0:T(8,128)(2,1)} %get-tuple-element.8), channel_id=1, source_target_pairs={{0,120},{8,0},{16,8},{24,16},{32,24},{40,32},{48,40},{56,48},{64,5... | collective-permute-start | bytes 221192 | tf_op jit(solution)/shard_map/ppermute | solution.py:22
  40.7 5.1 %copy-start.6 = (f32[1000]{0:T(1024)S(1)}, f32[1000]{0:T(1024)}, u32[]{:S(2)}) copy-start(f32[1000]{0:T(1024)} %param.16) | copy-start | bytes 12004
  40.7 58.5 %all-to-all-start = ((bf16[4,688,384]{2,1,0:T(8,128)(2,1)}), bf16[4,688,384]{2,1,0:T(8,128)(2,1)S(1)}, u32[]{:S(2)}, u32[]{:S(2)}) async-start(bf16[4,688,384]{2,1,0:T(8,128)(2,1)} %pad_maximum_fusion.1), calls=%async_computation | async-start | bytes 4227072 | tf_op jit(solution)/shard_map/all_to_all | solution.py:160
  50.4 49.3 %copy-start.4 = (f32[3072]{0:T(1024)S(1)}, f32[3072]{0:T(1024)}, u32[]{:S(2)}) copy-start(f32[3072]{0:T(1024)} %param.19) | copy-start | bytes 36868
  50.5 6.8 %collective-permute-start.2 = (bf16[96,384]{1,0:T(8,128)(2,1)}, bf16[96,384]{1,0:T(8,128)(2,1)S(1)}, u32[]{:S(2)}, u32[]{:S(2)}) collective-permute-start(bf16[96,384]{1,0:T(8,128)(2,1)} %collective-permute-done), channel_id=1, source_target_pairs={{0,8},{8,16},{16,24},{24,32},{32,40},{40,48},{48,56},{56,64},{64,7... | collective-permute-start | bytes 221192 | tf_op jit(solution)/shard_map/ppermute | solution.py:22
  50.6 6.6 %collective-permute-start.3 = (bf16[96,384]{1,0:T(8,128)(2,1)}, bf16[96,384]{1,0:T(8,128)(2,1)S(1)}, u32[]{:S(2)}, u32[]{:S(2)}) collective-permute-start(bf16[96,384]{1,0:T(8,128)(2,1)} %collective-permute-done.1), channel_id=1, source_target_pairs={{0,120},{8,0},{16,8},{24,16},{32,24},{40,32},{48,40},{56,48},{64,5... | collective-permute-start | bytes 221192 | tf_op jit(solution)/shard_map/ppermute | solution.py:22
  57.3 5.6 %collective-permute-start.4 = (bf16[96,384]{1,0:T(8,128)(2,1)S(1)}, bf16[96,384]{1,0:T(8,128)(2,1)S(1)}, u32[]{:S(2)}, u32[]{:S(2)}) collective-permute-start(bf16[96,384]{1,0:T(8,128)(2,1)S(1)} %collective-permute-done.2), channel_id=1, source_target_pairs={{0,8},{8,16},{16,24},{24,32},{32,40},{40,48},{48,56},{56,64},{64,7... | collective-permute-start | bytes 221192 | tf_op jit(solution)/shard_map/ppermute | solution.py:22
  57.3 5.6 %collective-permute-start.5 = (bf16[96,384]{1,0:T(8,128)(2,1)S(1)}, bf16[96,384]{1,0:T(8,128)(2,1)S(1)}, u32[]{:S(2)}, u32[]{:S(2)}) collective-permute-start(bf16[96,384]{1,0:T(8,128)(2,1)S(1)} %collective-permute-done.3), channel_id=1, source_target_pairs={{0,120},{8,0},{16,8},{24,16},{32,24},{40,32},{48,40},{56,48},{64,5... | collective-permute-start | bytes 221192 | tf_op jit(solution)/shard_map/ppermute | solution.py:22
  62.9 5.9 %collective-permute-start.6 = (bf16[96,384]{1,0:T(8,128)(2,1)S(1)}, bf16[96,384]{1,0:T(8,128)(2,1)S(1)}, u32[]{:S(2)}, u32[]{:S(2)}) collective-permute-start(bf16[96,384]{1,0:T(8,128)(2,1)S(1)} %collective-permute-done.4), channel_id=1, source_target_pairs={{0,8},{8,16},{16,24},{24,32},{32,40},{40,48},{48,56},{56,64},{64,7... | collective-permute-start | bytes 221192 | tf_op jit(solution)/shard_map/ppermute | solution.py:22
  62.9 5.9 %collective-permute-start.7 = (bf16[96,384]{1,0:T(8,128)(2,1)S(1)}, bf16[96,384]{1,0:T(8,128)(2,1)S(1)}, u32[]{:S(2)}, u32[]{:S(2)}) collective-permute-start(bf16[96,384]{1,0:T(8,128)(2,1)S(1)} %collective-permute-done.5), channel_id=1, source_target_pairs={{0,120},{8,0},{16,8},{24,16},{32,24},{40,32},{48,40},{56,48},{64,5... | collective-permute-start | bytes 221192 | tf_op jit(solution)/shard_map/ppermute | solution.py:22
  68.8 6.0 %collective-permute-start.8 = (bf16[96,384]{1,0:T(8,128)(2,1)S(1)}, bf16[96,384]{1,0:T(8,128)(2,1)S(1)}, u32[]{:S(2)}, u32[]{:S(2)}) collective-permute-start(bf16[96,384]{1,0:T(8,128)(2,1)S(1)} %collective-permute-done.6), channel_id=1, source_target_pairs={{0,8},{8,16},{16,24},{24,32},{32,40},{40,48},{48,56},{56,64},{64,7... | collective-permute-start | bytes 221192 | tf_op jit(solution)/shard_map/ppermute | solution.py:22
  68.8 6.0 %collective-permute-start.9 = (bf16[96,384]{1,0:T(8,128)(2,1)S(1)}, bf16[96,384]{1,0:T(8,128)(2,1)S(1)}, u32[]{:S(2)}, u32[]{:S(2)}) collective-permute-start(bf16[96,384]{1,0:T(8,128)(2,1)S(1)} %collective-permute-done.7), channel_id=1, source_target_pairs={{0,120},{8,0},{16,8},{24,16},{32,24},{40,32},{48,40},{56,48},{64,5... | collective-permute-start | bytes 221192 | tf_op jit(solution)/shard_map/ppermute | solution.py:22
  74.8 5.8 %collective-permute-start.10 = (bf16[96,384]{1,0:T(8,128)(2,1)S(1)}, bf16[96,384]{1,0:T(8,128)(2,1)S(1)}, u32[]{:S(2)}, u32[]{:S(2)}) collective-permute-start(bf16[96,384]{1,0:T(8,128)(2,1)S(1)} %collective-permute-done.8), channel_id=1, source_target_pairs={{0,8},{8,16},{16,24},{24,32},{32,40},{40,48},{48,56},{56,64},{64,7... | collective-permute-start | bytes 221192 | tf_op jit(solution)/shard_map/ppermute | solution.py:22
  74.8 6.1 %collective-permute-start.11 = (bf16[96,384]{1,0:T(8,128)(2,1)S(1)}, bf16[96,384]{1,0:T(8,128)(2,1)S(1)}, u32[]{:S(2)}, u32[]{:S(2)}) collective-permute-start(bf16[96,384]{1,0:T(8,128)(2,1)S(1)} %collective-permute-done.9), channel_id=1, source_target_pairs={{0,120},{8,0},{16,8},{24,16},{32,24},{40,32},{48,40},{56,48},{64,5... | collective-permute-start | bytes 221192 | tf_op jit(solution)/shard_map/ppermute | solution.py:22
  80.6 6.1 %collective-permute-start.12 = (bf16[96,384]{1,0:T(8,128)(2,1)S(1)}, bf16[96,384]{1,0:T(8,128)(2,1)S(1)}, u32[]{:S(2)}, u32[]{:S(2)}) collective-permute-start(bf16[96,384]{1,0:T(8,128)(2,1)S(1)} %collective-permute-done.10), channel_id=1, source_target_pairs={{0,8},{8,16},{16,24},{24,32},{32,40},{40,48},{48,56},{56,64},{64,7... | collective-permute-start | bytes 221192 | tf_op jit(solution)/shard_map/ppermute | solution.py:22
  80.8 6.6 %collective-permute-start.13 = (bf16[96,384]{1,0:T(8,128)(2,1)S(1)}, bf16[96,384]{1,0:T(8,128)(2,1)S(1)}, u32[]{:S(2)}, u32[]{:S(2)}) collective-permute-start(bf16[96,384]{1,0:T(8,128)(2,1)S(1)} %collective-permute-done.11), channel_id=1, source_target_pairs={{0,120},{8,0},{16,8},{24,16},{32,24},{40,32},{48,40},{56,48},{64,5... | collective-permute-start | bytes 221192 | tf_op jit(solution)/shard_map/ppermute | solution.py:22
  86.7 6.3 %collective-permute-start.14 = (bf16[96,384]{1,0:T(8,128)(2,1)S(1)}, bf16[96,384]{1,0:T(8,128)(2,1)S(1)}, u32[]{:S(2)}, u32[]{:S(2)}) collective-permute-start(bf16[96,384]{1,0:T(8,128)(2,1)S(1)} %collective-permute-done.12), channel_id=1, source_target_pairs={{0,8},{8,16},{16,24},{24,32},{32,40},{40,48},{48,56},{56,64},{64,7... | collective-permute-start | bytes 221192 | tf_op jit(solution)/shard_map/ppermute | solution.py:22
  93.7 15.1 %collective-permute-start.15 = (bf16[16,96,384]{2,1,0:T(8,128)(2,1)}, bf16[16,96,384]{2,1,0:T(8,128)(2,1)}, u32[]{:S(2)}, u32[]{:S(2)}) collective-permute-start(bf16[16,96,384]{2,1,0:T(8,128)(2,1)} %bitcast_dynamic-update-slice_fusion), channel_id=1, source_target_pairs={{0,4},{4,0},{1,5},{5,1},{2,6},{6,2},{3,7},{7,3},{8,12},{12,8},{9,1... | collective-permute-start | bytes 3538952 | tf_op jit(solution)/shard_map/ppermute | solution.py:22
  107.2 1.6 copy-start.2
  131.2 18.4 %all-to-all-start.1 = ((bf16[4,256,384]{1,2,0:T(8,128)(2,1)}), bf16[4,256,384]{1,2,0:T(8,128)(2,1)S(1)}, u32[]{:S(2)}, u32[]{:S(2)}) async-start(bf16[4,256,384]{1,2,0:T(8,128)(2,1)} %copy.20), calls=%async_computation.1 | async-start | bytes 1572864 | tf_op jit(solution)/shard_map/all_to_all | solution.py:186
  155.6 1.0 copy-start.3
  156.6 25.8 %copy-start.5 = (f32[256,64]{0,1:T(8,128)S(1)}, f32[256,64]{0,1:T(8,128)}, u32[]{:S(2)}) copy-start(f32[256,64]{0,1:T(8,128)} %param.14) | copy-start | bytes 196612
  157.5 2.1 %collective-permute-start.16 = (bf16[128,128]{1,0:T(8,128)(2,1)S(1)}, bf16[128,128]{1,0:T(8,128)(2,1)S(1)}, u32[]{:S(2)}, u32[]{:S(2)}) collective-permute-start(bf16[128,128]{1,0:T(8,128)(2,1)S(1)} %convert_element_type.68), channel_id=1, source_target_pairs={{0,4},{4,0},{1,5},{5,1},{2,6},{6,2},{3,7},{7,3},{8,12},{12,8},{9,1... | collective-permute-start | bytes 98312 | tf_op jit(solution)/shard_map/ppermute | solution.py:22
  159.6 3.9 %collective-permute-start.19 = (bf16[64,128]{1,0:T(8,128)(2,1)S(1)}, bf16[64,128]{1,0:T(8,128)(2,1)S(1)}, u32[]{:S(2)}, u32[]{:S(2)}) collective-permute-start(bf16[64,128]{1,0:T(8,128)(2,1)S(1)} %fusion.6), channel_id=1, source_target_pairs={{0,24},{8,32},{16,40},{24,48},{32,56},{40,64},{48,72},{56,80},{64,... | collective-permute-start | bytes 49160 | tf_op jit(solution)/shard_map/ppermute | solution.py:22
  160.9 2.6 %collective-permute-start.18 = (bf16[64,128]{1,0:T(8,128)(2,1)S(1)}, bf16[64,128]{1,0:T(8,128)(2,1)S(1)}, u32[]{:S(2)}, u32[]{:S(2)}) collective-permute-start(bf16[64,128]{1,0:T(8,128)(2,1)S(1)} %fusion.6), channel_id=1, source_target_pairs={{0,16},{8,24},{16,32},{24,40},{32,48},{40,56},{48,64},{56,72},{64,... | collective-permute-start | bytes 49160 | tf_op jit(solution)/shard_map/ppermute | solution.py:22
  162.2 2.2 %collective-permute-start.17 = (bf16[64,128]{1,0:T(8,128)(2,1)S(1)}, bf16[64,128]{1,0:T(8,128)(2,1)S(1)}, u32[]{:S(2)}, u32[]{:S(2)}) collective-permute-start(bf16[64,128]{1,0:T(8,128)(2,1)S(1)} %fusion.6), channel_id=1, source_target_pairs={{0,8},{8,16},{16,24},{24,32},{32,40},{40,48},{48,56},{56,64},{64,7... | collective-permute-start | bytes 49160 | tf_op jit(solution)/shard_map/ppermute | solution.py:22
  164.4 18.0 %collective-permute-start.22 = (bf16[64,128]{1,0:T(8,128)(2,1)S(1)}, bf16[64,128]{1,0:T(8,128)(2,1)S(1)}, u32[]{:S(2)}, u32[]{:S(2)}) collective-permute-start(bf16[64,128]{1,0:T(8,128)(2,1)S(1)} %add_convert_fusion.2), channel_id=1, source_target_pairs={{0,96},{8,104},{16,112},{24,120},{1,97},{9,105},{17,113},{25,121},... | collective-permute-start | bytes 49160 | tf_op jit(solution)/shard_map/ppermute | solution.py:22
  174.0 8.5 %collective-permute-start.21 = (bf16[64,128]{1,0:T(8,128)(2,1)S(1)}, bf16[64,128]{1,0:T(8,128)(2,1)S(1)}, u32[]{:S(2)}, u32[]{:S(2)}) collective-permute-start(bf16[64,128]{1,0:T(8,128)(2,1)S(1)} %add_convert_fusion.2), channel_id=1, source_target_pairs={{0,64},{8,72},{16,80},{24,88},{32,96},{40,104},{48,112},{56,120},{... | collective-permute-start | bytes 49160 | tf_op jit(solution)/shard_map/ppermute | solution.py:22
  179.7 3.5 %collective-permute-start.20 = (bf16[64,128]{1,0:T(8,128)(2,1)S(1)}, bf16[64,128]{1,0:T(8,128)(2,1)S(1)}, u32[]{:S(2)}, u32[]{:S(2)}) collective-permute-start(bf16[64,128]{1,0:T(8,128)(2,1)S(1)} %add_convert_fusion.2), channel_id=1, source_target_pairs={{0,32},{8,40},{16,48},{24,56},{32,64},{40,72},{48,80},{56,88},{64,... | collective-permute-start | bytes 49160 | tf_op jit(solution)/shard_map/ppermute | solution.py:22
Sparse Core Ops, SparseCore 0:
  9.2 100.0 all-gather.1

commit v2 on v1

v2 whole, which is shorter than its diff:
```python
import functools
import math

import jax
import jax.numpy as jnp
from jax import lax
from jax.experimental import pallas as pl
from jax.experimental.pallas import tpu as pltpu
from jax.sharding import Mesh
from jax.sharding import PartitionSpec as P

HEAD = 128
CORES = 2
EXTRA = 16
STEP = ("chip", "core")
REP_STEP = ("rep", "chip", "core")
epsilon = 1e-06


def shift(value, axis, distance, wrap):
    size = lax.axis_size(axis)
    pairs = [(i, (i + distance) % size) for i in range(size) if wrap or 0 <= i + distance < size]
    return lax.ppermute(value, axis, pairs)


def swap_cores(value):
    return lax.ppermute(value, "core", [(0, 1), (1, 0)])


def send_by_core(value, first, second, wrap):
    chips = lax.axis_size("chip")
    pairs = []
    for core, distance in enumerate((first, second)):
        for chip in range(chips):
            target = chip + (distance or 0)
            if distance is not None and (wrap or 0 <= target < chips):
                pairs.append((chip * CORES + core, target % chips * CORES + core))
    return lax.ppermute(value, ("chip", "core"), pairs)


def gather_rows(shard, tasks):
    chips, here, core = lax.axis_size("chip"), lax.axis_index("chip"), lax.axis_index("core")
    other = swap_cores(shard)
    piece = jnp.concatenate([jnp.where(core == 0, shard, other), jnp.where(core == 0, other, shard)])
    rows = piece.shape[0]
    step = jnp.where(core == 0, 1, -1)
    half = chips // 2
    pieces, waiting, results = [(0, piece)], [], {}
    for hop in range(1, half + 1):
        sent = send_by_core(piece, 1, -1, True)
        if hop in tasks:
            task, inputs = tasks[hop]
            if callable(inputs):
                inputs = inputs(results)
            _, inputs = lax.optimization_barrier((piece, inputs))
            results[hop] = task(*inputs)
            sent, results[hop] = lax.optimization_barrier((sent, results[hop]))
        piece = sent
        pieces.append((hop, piece))
        if 2 * hop != chips:
            waiting.append((hop, piece))
        if hop in (half // 2, half - 1):
            swapped = swap_cores(jnp.concatenate([p for _, p in waiting]))
            for i, (at, _) in enumerate(waiting):
                pieces.append((-at, swapped[i * rows : (i + 1) * rows]))
            waiting = []
    held = jnp.zeros((chips, *piece.shape), shard.dtype)
    for at, piece in pieces:
        owner = lax.rem(here - at * step + chips, chips)
        held = lax.dynamic_update_slice_in_dim(held, piece[None], owner, 0)
    return held, results


def time_embed(sigma_now, half_count):
    frequency = jnp.exp(
        -math.log(10000.0) * jnp.arange(half_count).astype(jnp.float32) / half_count
    )
    angles = 1000.0 * sigma_now * frequency
    return jnp.concatenate([jnp.cos(angles), jnp.sin(angles)])


def pack_body(key_ref, value_ref, latent_ref, spread_ref, out_ref):
    rows = key_ref.shape[0]
    channels, tokens = latent_ref.shape
    out_ref[0, :rows] = key_ref[...]
    out_ref[0, rows : 2 * rows] = value_ref[...]
    spread = spread_ref[...]
    coarse = spread.astype(jnp.bfloat16).astype(jnp.float32)
    tail = jnp.concatenate(
        [
            latent_ref[...],
            jnp.ones_like(spread),
            coarse,
            spread - coarse,
            jnp.zeros((EXTRA - 3, tokens), jnp.float32),
        ]
    )
    out_ref[0, 2 * rows :] = jnp.zeros((channels + EXTRA, out_ref.shape[2]), jnp.bfloat16)
    out_ref[0, 2 * rows :, :tokens] = tail.astype(jnp.bfloat16)


def pack(keys, values, latent, spread, parts):
    rows, width = keys.shape
    channels, tokens = latent.shape
    columns = width // parts
    height = 2 * rows + channels + EXTRA
    return pl.pallas_call(
        pack_body,
        grid=(parts,),
        in_specs=[
            pl.BlockSpec((rows, columns), lambda p: (0, p)),
            pl.BlockSpec((rows, columns), lambda p: (0, p)),
            pl.BlockSpec((channels, tokens), lambda p: (0, 0)),
            pl.BlockSpec((1, tokens), lambda p: (0, 0)),
        ],
        out_specs=pl.BlockSpec((1, height, columns), lambda p: (p, 0, 0)),
        out_shape=jax.ShapeDtypeStruct((parts, height, columns), jnp.bfloat16),
        cost_estimate=pl.CostEstimate(
            flops=parts * height * columns,
            bytes_accessed=4 * parts * height * columns,
            transcendentals=0,
        ),
        name="pack",
    )(keys, values, latent, spread)


def attention_body(parts, rows, packed_ref, project_ref, gain_ref, out_ref, even_ref, odd_ref):
    at, last = pl.program_id(0), pl.num_programs(0) - 2
    now, past = jnp.minimum(at, last), jnp.maximum(at - 1, 0)
    tile = even_ref.shape[0]
    head, part = now // parts, lax.rem(now, parts)

    def columns(head):
        return pl.ds(pl.multiple_of(head * HEAD, HEAD), HEAD)

    def run(now_ref, past_ref):
        tokens = packed_ref[part, 2 * rows :, :tile]
        both = lax.dot_general(
            jnp.concatenate([tokens, tokens]),
            project_ref[head],
            (((0,), (0,)), ((), ())),
            preferred_element_type=jnp.float32,
        )
        raw, spread = both[:, :HEAD], both[:, HEAD:]
        square = jnp.mean(raw * raw, axis=-1, keepdims=True) + epsilon * (spread * spread)
        queries = (raw * lax.rsqrt(square) * gain_ref[...]).astype(jnp.bfloat16)
        for p in range(parts):
            now_ref[:, p * rows : (p + 1) * rows] = lax.dot_general(
                queries,
                packed_ref[p, :rows, columns(head)],
                (((1,), (1,)), ((), ())),
                preferred_element_type=jnp.float32,
            )
        peak = jnp.max(past_ref[...], axis=-1, keepdims=True)
        weights = jnp.exp((past_ref[...] - peak) * (1.0 / math.sqrt(HEAD)))
        total = jnp.sum(weights, axis=-1, keepdims=True)
        values = packed_ref[:, rows : 2 * rows, columns(past // parts)].reshape(-1, HEAD)
        blended = jnp.dot(weights.astype(jnp.bfloat16), values, preferred_element_type=jnp.float32)
        out_ref[...] = (blended / total).astype(jnp.bfloat16)

    @pl.when(lax.rem(at, 2) == 0)
    def _():
        run(even_ref, odd_ref)

    @pl.when(lax.rem(at, 2) == 1)
    def _():
        run(odd_ref, even_ref)


def attention(project, query_gain, packed, rows, tile):
    parts, height, width = packed.shape
    tokens = parts * tile
    heads = width // HEAD
    work = tokens * parts * rows * width

    def past(i):
        at = jnp.maximum(i - 1, 0)
        return lax.rem(at, parts), at // parts

    whole = pl.BlockSpec(memory_space=pltpu.VMEM)
    return pl.pallas_call(
        functools.partial(attention_body, parts, rows),
        grid=(heads * parts + 1,),
        in_specs=[whole, whole, whole],
        out_specs=pl.BlockSpec((tile, HEAD), past),
        out_shape=jax.ShapeDtypeStruct((tokens, width), jnp.bfloat16),
        scratch_shapes=[pltpu.VMEM((tile, parts * rows), jnp.float32)] * 2,
        cost_estimate=pl.CostEstimate(
            flops=4 * work,
            bytes_accessed=4 * parts * rows * width + 6 * tokens * width,
            transcendentals=work // HEAD,
        ),
        name="attention",
    )(packed, project, query_gain.reshape(1, HEAD))


def finish_body(
    tile, attended_ref, weight_ref, hidden_ref, gate_ref, final_ref, out_ref, joined_ref, mixed_ref, sum_ref
):
    at = pl.program_id(0)
    parts, tokens, columns = attended_ref.shape

    @pl.when(at == 0)
    def _():
        for p in range(parts):
            joined_ref[:, p * columns : (p + 1) * columns] = attended_ref[p]
        sum_ref[...] = jnp.zeros_like(sum_ref)

    branch = lax.dot_general(
        joined_ref[...], weight_ref[...], (((1,), (1,)), ((), ())), preferred_element_type=jnp.float32
    )
    mixed = hidden_ref[:, pl.ds(pl.multiple_of(at * tile, tile), tile)] + gate_ref[...] * branch
    mixed_ref[at] = mixed
    sum_ref[...] += jnp.sum(mixed, axis=-1, keepdims=True)

    @pl.when(at == pl.num_programs(0) - 1)
    def _():
        count = mixed_ref.shape[0]
        width = count * tile
        mean = sum_ref[...] / width
        squares = functools.reduce(
            lambda a, b: a + b, [jnp.square(mixed_ref[i] - mean) for i in range(count)]
        )
        scale = lax.rsqrt(jnp.sum(squares, axis=-1, keepdims=True) / width + epsilon)
        out_ref[...] = functools.reduce(
            lambda a, b: a + b,
            [
                lax.dot_general(
                    final_ref[:, i * tile : (i + 1) * tile],
                    ((mixed_ref[i] - mean) * scale).astype(jnp.bfloat16),
                    (((1,), (1,)), ((), ())),
                    preferred_element_type=jnp.float32,
                )
                for i in range(count)
            ],
        )


def finish(attended, out_weight, hidden, gate, final_weight):
    parts, tokens, columns = attended.shape
    width, depth = out_weight.shape
    channels = final_weight.shape[1]
    tile = min(512, width)
    return pl.pallas_call(
        functools.partial(finish_body, tile),
        grid=(width // tile,),
        in_specs=[
            pl.BlockSpec(memory_space=pltpu.VMEM),
            pl.BlockSpec((tile, depth), lambda i: (i, 0)),
            pl.BlockSpec(memory_space=pltpu.VMEM),
            pl.BlockSpec((1, tile), lambda i: (0, i)),
            pl.BlockSpec((channels, width), lambda i: (0, 0)),
        ],
        out_specs=pl.BlockSpec((channels, tokens), lambda i: (0, 0)),
        out_shape=jax.ShapeDtypeStruct((channels, tokens), jnp.float32),
        scratch_shapes=[
            pltpu.VMEM((tokens, depth), jnp.bfloat16),
            pltpu.VMEM((width // tile, tokens, tile), jnp.float32),
            pltpu.VMEM((tokens, 1), jnp.float32),
        ],
        cost_estimate=pl.CostEstimate(
            flops=2 * tokens * width * (depth + channels),
            bytes_accessed=2 * width * depth + 4 * tokens * width,
            transcendentals=0,
        ),
        name="finish",
    )(attended, out_weight, hidden, gate.reshape(1, width), final_weight.T)


def prefix_over_steps(drift):
    half = jnp.bfloat16

    def wide(value):
        return value.astype(jnp.float32)

    other = wide(swap_cores(drift.astype(half)))
    within = jnp.where(lax.axis_index("core") == 1, other, jnp.zeros_like(other))
    here = drift + other
    near = wide(shift(here.astype(half), "chip", 1, False))
    near = near + wide(shift((here + near).astype(half), "chip", 2, False))
    window = (here + near).astype(half)
    chips = lax.axis_size("chip")
    far = send_by_core(window, 4, chips - 4, False)
    far = wide(far) + wide(send_by_core(far, 4, None, False))
    return within + near + far + wide(swap_cores(far.astype(half)))


def per_device(
    latent_old,
    noise_start,
    step_index,
    sigma_table,
    mod_weight,
    embed_weight,
    embed_bias,
    query_weight,
    query_gain,
    stale_keys,
    stale_values,
    out_weight,
    final_weight,
):
    parts, part = lax.axis_size("patch"), lax.axis_index("patch")
    width = embed_weight.shape[1]
    columns = query_weight.shape[1] // parts
    latent = latent_old[0].T
    channels, token_count = latent.shape
    key_rows = stale_keys.shape[1]

    all_out_weight = lax.all_gather(out_weight, STEP, axis=0, tiled=True)

    def embed(latent, embed_weight, embed_bias):
        hidden = lax.dot_general(
            latent.astype(jnp.bfloat16),
            embed_weight,
            (((0,), (0,)), ((), ())),
            preferred_element_type=jnp.float32,
        )
        hidden = hidden + embed_bias
        row_mean = jnp.mean(hidden, axis=-1, keepdims=True)
        row_var = jnp.mean(jnp.square(hidden - row_mean), axis=-1)
        return hidden, jnp.sqrt(row_var + epsilon)[None]

    def modulation(step_index, sigma_table, mod_weight):
        slots = jnp.arange(sigma_table.shape[0])
        sigma_now = jnp.sum(jnp.where(slots == step_index[0], sigma_table, 0.0))
        sigma_next = jnp.sum(jnp.where(slots == step_index[0] + 1, sigma_table, 0.0))
        embedded = jax.nn.silu(time_embed(sigma_now, mod_weight.shape[0] // 2)).astype(jnp.bfloat16)
        modulate = jnp.dot(embedded[None, :], mod_weight, preferred_element_type=jnp.float32)[0]
        return modulate, sigma_next - sigma_now

    def split(value):
        coarse = value.astype(jnp.bfloat16)
        return jnp.concatenate([coarse, (value - coarse.astype(jnp.float32)).astype(jnp.bfloat16)])

    def sources(modulate, embed_weight, embed_bias):
        shift_vec, scale_vec = modulate[:width], modulate[width : 2 * width]
        weight = embed_weight.astype(jnp.float32)
        centered = jnp.concatenate(
            [
                weight - jnp.mean(weight, axis=-1, keepdims=True),
                (embed_bias - jnp.mean(embed_bias))[None],
            ]
        )
        rows = [
            centered * (1.0 + scale_vec),
            shift_vec[None],
            shift_vec[None],
            jnp.zeros((EXTRA - 3, width), jnp.float32),
        ]
        return split(jnp.concatenate(rows))

    my_columns = lax.dynamic_slice_in_dim(query_weight, part * columns, columns, 1)
    tasks = {
        1: (embed, (latent, embed_weight, embed_bias)),
        2: (
            functools.partial(pack, parts=parts),
            lambda done: (stale_keys[0], stale_values[0], latent, done[1][1]),
        ),
        4: (modulation, (step_index, sigma_table, mod_weight)),
        6: (sources, lambda done: (done[4][0], embed_weight, embed_bias)),
    }
    gathered, done = gather_rows(my_columns, tasks)
    hidden, (modulate, delta), source = done[1][0], done[4], done[6]
    packed = lax.all_to_all(done[2], "patch", 0, 0, tiled=True)

    project = jnp.dot(source, gathered.reshape(width, columns), preferred_element_type=jnp.float32)
    deep = channels + EXTRA
    project = split(project[:deep] + project[deep:])
    project = jnp.moveaxis(project.reshape(2 * deep, -1, HEAD), 1, 0)
    row = lax.broadcasted_iota(jnp.int32, (1, 2 * deep, HEAD), 1)
    picks = jnp.where((row == channels + 1) | (row == channels + 2), 1.0, 0.0).astype(jnp.bfloat16)
    project = jnp.concatenate([project, jnp.broadcast_to(picks, project.shape)], axis=2)

    attended = attention(project, query_gain, packed, key_rows, token_count)
    attended = lax.all_to_all(
        attended.reshape(parts, token_count, columns), "patch", 0, 0, tiled=True
    )
    velocity = finish(attended, all_out_weight, hidden, modulate[2 * width :], final_weight)
    drift = velocity * delta
    return (noise_start.T + (prefix_over_steps(drift) + drift)).T[None]


def solution(mesh):
    shape = mesh.shape
    torus = Mesh(
        mesh.devices.reshape(shape["rep"], shape["step"] // CORES, CORES, shape["patch"]),
        ("rep", "chip", "core", "patch"),
    )
    placed = (
        P(REP_STEP, "patch", None),
        P(("rep", "patch"), None),
        P(REP_STEP),
        P(),
        P(),
        P(),
        P(),
        P(STEP, None),
        P(),
        P(REP_STEP, "patch", None),
        P(REP_STEP, "patch", None),
        P(STEP, None),
        P(),
    )
    return jax.shard_map(
        per_device,
        mesh=torus,
        in_specs=placed,
        out_specs=P(REP_STEP, "patch", None),
        check_vma=False,
    )
```

time: 196 us -> 186 us (0.949)
  local copies, waits for them, and re-layouts: 25.1 us -> 7.02 us
  Pallas kernels: 13.8 us -> 28.7 us
  matrix products: 16.2 us -> 5.52 us
  blocking collectives: 4.11 us -> 0 us
  waiting for transfers between devices: 27.2 us -> 31.1 us
  starting transfers between devices: 81 us -> 84.2 us
    ppermute x0 -> x15, starting transfers between devices: none -> 70.5 us  [the longest x5 35.7 us: swap_cores(): return lax.ppermute(value, 'core', [(0, 1), (1, 0)])]
    ppermute x23 -> x2, starting transfers between devices: 70.2 us -> 4.53 us  [shift(): return lax.ppermute(value, axis, pairs)]
    ppermute x0 -> x15, waiting for transfers between devices: none -> 19.1 us  [the longest x10 17.3 us: send_by_core(): return lax.ppermute(value, ('chip', 'core'), pairs)]
    pallas_call x1 -> x3, Pallas kernels: 13.8 us -> 28.7 us  [the longest x1 14.5 us: attention(): pl.pallas_call(functools.partial(attention_body, parts, rows), grid=(head...]
    ppermute x23 -> x2, waiting for transfers between devices: 15.6 us -> 2.01 us  [shift(): return lax.ppermute(value, axis, pairs)]
    dot_general x6 -> x3, matrix products: 16.2 us -> 5.52 us  [the longest x1 3.14 us: modulation(): jnp.dot(embedded[None, :], mod_weight, preferred_element_type=jnp.float32)]
    dynamic_update_slice x16 -> x15, local copies, waits for them, and re-layouts: 12.8 us -> 4.07 us  [gather_rows(): held = lax.dynamic_update_slice_in_dim(held, piece[None], owner, 0)]
    another operation x2 -> x0, local copies, waits for them, and re-layouts: 4.6 us -> none  [by_part(): return jnp.moveaxis(rows.reshape(rows.shape[0], parts, columns), 1, 0)]
  transfers between devices with their start and end apart: 26 -> 20, of which waited for: 13 -> 14; matrix products, arithmetic and copies ran while one was open for 22% -> 10% of each run, Pallas kernels for 7% -> 10%
where the time goes in v2:
time: 186 us; the launch traced here: 185 us
  starting transfers between devices  84.2 us (45%)
  waiting for transfers between devices  31.1 us (17%)
  Pallas kernels  28.7 us (15%)
  between operations  17.2 us (9%)
  other arithmetic  11.1 us (6%)
  local copies, waits for them, and re-layouts  7.02 us (4%)
  matrix products  5.52 us (3%)
    ppermute x5, starting transfers between devices, swap_cores(): return lax.ppermute(value, 'core', [(0, 1), (1, 0)])  35.7 us
    ppermute x10, starting transfers between devices, send_by_core(): return lax.ppermute(value, ('chip', 'core'), pairs)  34.8 us
    ppermute x10, waiting for transfers between devices, send_by_core(): return lax.ppermute(value, ('chip', 'core'), pairs)  17.3 us
    pallas_call x1, Pallas kernels, attention(): pl.pallas_call(functools.partial(attention_body, parts, rows), grid=(head...  14.5 us
    pallas_call x1, Pallas kernels, finish(): pl.pallas_call(functools.partial(finish_body, tile), grid=(width // tile,...  10.2 us
    all_to_all x1, waiting for transfers between devices, per_device(): lax.all_to_all(attended.reshape(parts, token_count, columns), 'patch', 0,...  9.23 us
    all_to_all x1, starting transfers between devices, per_device(): packed = lax.all_to_all(done[2], 'patch', 0, 0, tiled=True)  4.6 us
    all_to_all x1, starting transfers between devices, per_device(): lax.all_to_all(attended.reshape(parts, token_count, columns), 'patch', 0,...  4.59 us
  transfers between devices with their start and end apart: 20, of which 14 were waited for; matrix products, arithmetic and copies ran while one was open for 10% of the time, Pallas kernels for 10%

profile of v2, /device:TPU:33, one launch (start us, length us, event | category | flops | bytes accessed | tf_op | source)
XLA Modules:
  0.0 184.8 jit_solution(4380209491921609252)
XLA Ops:
  6.6 0.7 all-gather.2.cloned.1.call-update
  7.3 0.9 constant_dynamic-slice_fusion
  8.2 20.4 %collective-permute-start = (bf16[96,384]{1,0:T(8,128)(2,1)S(1)}, bf16[96,384]{1,0:T(8,128)(2,1)S(1)}, u32[]{:S(2)}, u32[]{:S(2)}) collective-permute-start(bf16[96,384]{1,0:T(8,128)(2,1)S(1)} %constant_dynamic-slice_fusion), channel_id=1, source_target_pairs={{0,4},{4,0},{1,5},{5,1},{2,6},{6,2},{3,7},{7,3},{8,12},{12,8},{9,1... | collective-permute-start | bytes 221192 | tf_op jit(solution)/shard_map/ppermute | solution.py:27
  29.4 0.1 collective-permute-done
  29.5 0.9 broadcast_select_fusion.1
  30.5 3.2 %collective-permute-start.1 = (bf16[192,384]{1,0:T(8,128)(2,1)S(1)}, bf16[192,384]{1,0:T(8,128)(2,1)S(1)}, u32[]{:S(2)}, u32[]{:S(2)}) collective-permute-start(bf16[192,384]{1,0:T(8,128)(2,1)S(1)} %pad_maximum_fusion.4), channel_id=1, source_target_pairs={{0,8},{8,16},{16,24},{24,32},{32,40},{40,48},{48,56},{56,64},{64,7... | collective-permute-start | bytes 442376 | tf_op jit(solution)/shard_map/ppermute | solution.py:38
  33.7 1.7 fusion.24
  35.4 0.5 multiply_reduce_fusion
  35.8 0.9 add_sqrt_fusion
  36.8 0.3 broadcast_in_dim.95
  37.1 1.8 collective-permute-start.2
  38.9 3.9 %pack.1 = bf16[4,720,384]{2,1,0:T(8,128)(2,1)} custom-call(bf16[320,1536]{1,0:T(8,128)(2,1)} %bitcast.82, bf16[320,1536]{1,0:T(8,128)(2,1)} %bitcast.83, f32[64,256]{1,0:T(8,128)} %bitcast.87, f32[1,256]{1,0:T(1,128)} %bitcast.94), custom_call_target="tpu_custom_call" | custom-call | flops 1105920 | bytes 4423680 | tf_op jit(solution)/shard_map/pack/pallas_call | solution.py:107
  42.9 0.4 collective-permute-done.2
  43.2 3.3 %collective-permute-start.3 = (bf16[192,384]{1,0:T(8,128)(2,1)S(1)}, bf16[192,384]{1,0:T(8,128)(2,1)S(1)}, u32[]{:S(2)}, u32[]{:S(2)}) collective-permute-start(bf16[192,384]{1,0:T(8,128)(2,1)S(1)} %collective-permute-done.2), channel_id=1, source_target_pairs={{0,8},{8,16},{16,24},{24,32},{32,40},{40,48},{48,56},{56,64},{64,7... | collective-permute-start | bytes 442376 | tf_op jit(solution)/shard_map/ppermute | solution.py:38
  46.5 4.6 %all-to-all-start = ((bf16[4,720,384]{2,1,0:T(8,128)(2,1)}), bf16[4,720,384]{2,1,0:T(8,128)(2,1)}, u32[]{:S(2)}, u32[]{:S(2)}) async-start(bf16[4,720,384]{2,1,0:T(8,128)(2,1)} %pack.1), calls=%async_computation | async-start | bytes 4423680 | tf_op jit(solution)/shard_map/all_to_all | solution.py:365
  51.2 0.4 collective-permute-done.3
  51.6 0.7 select_reduce_fusion
  53.1 3.6 %collective-permute-start.4 = (bf16[192,384]{1,0:T(8,128)(2,1)S(1)}, bf16[192,384]{1,0:T(8,128)(2,1)S(1)}, u32[]{:S(2)}, u32[]{:S(2)}) collective-permute-start(bf16[192,384]{1,0:T(8,128)(2,1)S(1)} %collective-permute-done.3), channel_id=1, source_target_pairs={{0,8},{8,16},{16,24},{24,32},{32,40},{40,48},{48,56},{56,64},{64,7... | collective-permute-start | bytes 442376 | tf_op jit(solution)/shard_map/ppermute | solution.py:38
  56.7 3.1 %fusion.25 = f32[1,9216]{1,0:T(1,128)S(1)} fusion(bf16[256,1]{0,1:T(2,128)(2,1)S(1)} %reshape.68, bf16[256,9216]{1,0:T(8,128)(2,1)} %param.17), kind=kOutput, calls=%fused_computation.79 | convolution fusion | flops 4718592 | bytes 4755968 | tf_op jit(solution)/shard_map/dot_general | solution.py:329
  61.2 0.4 collective-permute-done.4
  61.6 3.5 %collective-permute-start.5 = (bf16[192,384]{1,0:T(8,128)(2,1)S(1)}, bf16[192,384]{1,0:T(8,128)(2,1)S(1)}, u32[]{:S(2)}, u32[]{:S(2)}) collective-permute-start(bf16[192,384]{1,0:T(8,128)(2,1)S(1)} %collective-permute-done.4), channel_id=1, source_target_pairs={{0,8},{8,16},{16,24},{24,32},{32,40},{40,48},{48,56},{56,64},{64,7... | collective-permute-start | bytes 442376 | tf_op jit(solution)/shard_map/ppermute | solution.py:38
  65.2 0.9 pad_maximum_fusion.1
  66.0 4.2 %collective-permute-done.5 = bf16[192,384]{1,0:T(8,128)(2,1)S(1)} collective-permute-done((bf16[192,384]{1,0:T(8,128)(2,1)S(1)}, bf16[192,384]{1,0:T(8,128)(2,1)S(1)}, u32[]{:S(2)}, u32[]{:S(2)}) %collective-permute-start.5) | collective-permute-done | bytes 147488 | tf_op jit(solution)/shard_map/ppermute | solution.py:38
  70.2 0.6 reduce_sum.59
  71.5 3.6 %collective-permute-start.6 = (bf16[192,384]{1,0:T(8,128)(2,1)S(1)}, bf16[192,384]{1,0:T(8,128)(2,1)S(1)}, u32[]{:S(2)}, u32[]{:S(2)}) collective-permute-start(bf16[192,384]{1,0:T(8,128)(2,1)S(1)} %collective-permute-done.5), channel_id=1, source_target_pairs={{0,8},{8,16},{16,24},{24,32},{32,40},{40,48},{48,56},{56,64},{64,7... | collective-permute-start | bytes 442376 | tf_op jit(solution)/shard_map/ppermute | solution.py:38
  75.1 0.2 convert_reduce_fusion
  75.3 0.1 convert_subtract_fusion
  75.5 0.1 fusion
  75.6 0.2 subtract_convert_fusion
  75.9 4.4 %collective-permute-done.6 = bf16[192,384]{1,0:T(8,128)(2,1)S(1)} collective-permute-done((bf16[192,384]{1,0:T(8,128)(2,1)S(1)}, bf16[192,384]{1,0:T(8,128)(2,1)S(1)}, u32[]{:S(2)}, u32[]{:S(2)}) %collective-permute-start.6) | collective-permute-done | bytes 147488 | tf_op jit(solution)/shard_map/ppermute | solution.py:38
  80.3 3.5 %collective-permute-start.8 = (bf16[192,384]{1,0:T(8,128)(2,1)S(1)}, bf16[192,384]{1,0:T(8,128)(2,1)S(1)}, u32[]{:S(2)}, u32[]{:S(2)}) collective-permute-start(bf16[192,384]{1,0:T(8,128)(2,1)S(1)} %collective-permute-done.6), channel_id=1, source_target_pairs={{0,8},{8,16},{16,24},{24,32},{32,40},{40,48},{48,56},{56,64},{64,7... | collective-permute-start | bytes 442376 | tf_op jit(solution)/shard_map/ppermute | solution.py:38
  83.8 3.8 %collective-permute-done.8 = bf16[192,384]{1,0:T(8,128)(2,1)S(1)} collective-permute-done((bf16[192,384]{1,0:T(8,128)(2,1)S(1)}, bf16[192,384]{1,0:T(8,128)(2,1)S(1)}, u32[]{:S(2)}, u32[]{:S(2)}) %collective-permute-start.8) | collective-permute-done | bytes 147488 | tf_op jit(solution)/shard_map/ppermute | solution.py:38
  87.7 3.4 %collective-permute-start.9 = (bf16[576,384]{1,0:T(8,128)(2,1)S(1)}, bf16[576,384]{1,0:T(8,128)(2,1)S(1)}, u32[]{:S(2)}, u32[]{:S(2)}) collective-permute-start(bf16[576,384]{1,0:T(8,128)(2,1)S(1)} %pad_maximum_fusion.2), channel_id=1, source_target_pairs={{0,4},{4,0},{1,5},{5,1},{2,6},{6,2},{3,7},{7,3},{8,12},{12,8},{9,1... | collective-permute-start | bytes 1327112 | tf_op jit(solution)/shard_map/ppermute | solution.py:27
  91.0 0.7 collective-permute-start.10
  91.8 0.9 fusion.7
  92.7 0.9 fusion.6
  93.7 0.9 fusion.5
  94.6 0.9 fusion.4
  95.8 2.7 %collective-permute-done.10 = bf16[192,384]{1,0:T(8,128)(2,1)S(1)} collective-permute-done((bf16[192,384]{1,0:T(8,128)(2,1)S(1)}, bf16[192,384]{1,0:T(8,128)(2,1)S(1)}, u32[]{:S(2)}, u32[]{:S(2)}) %collective-permute-start.10) | collective-permute-done | bytes 147488 | tf_op jit(solution)/shard_map/ppermute | solution.py:38
  98.5 0.7 fusion.26
  99.3 0.1 broadcast_in_dim.114
  99.4 0.7 pad_maximum_fusion.3.project_ref
  100.1 14.5 %attention.1 = bf16[1024,384]{1,0:T(8,128)(2,1)} custom-call(bf16[4,720,384]{2,1,0:T(8,128)(2,1)} %all-to-all-done.packed_ref, bf16[3,160,256]{2,1,0:T(8,128)(2,1)} %pad_maximum_fusion.3.project_ref, f32[1,128]{1,0:T(1,128)} %bitcast.95), custom_call_target="tpu_custom_call" | custom-call | flops 2013265920 | bytes 4325376 | tf_op jit(solution)/shard_map/attention/pallas_call | solution.py:181
  114.6 4.6 %all-to-all-start.1 = ((bf16[4,256,384]{2,1,0:T(8,128)(2,1)}), bf16[4,256,384]{2,1,0:T(8,128)(2,1)S(1)}, u32[]{:S(2)}, u32[]{:S(2)}) async-start(bf16[4,256,384]{2,1,0:T(8,128)(2,1)} %bitcast.84), calls=%async_computation.1 | async-start | bytes 1572864 | tf_op jit(solution)/shard_map/all_to_all | solution.py:376
  119.2 0.6 slice.47
  119.8 9.2 %all-to-all-done.1.attended_ref = bf16[4,256,384]{2,1,0:T(8,128)(2,1)S(1)} async-done(((bf16[4,256,384]{2,1,0:T(8,128)(2,1)}), bf16[4,256,384]{2,1,0:T(8,128)(2,1)S(1)}, u32[]{:S(2)}, u32[]{:S(2)}) %all-to-all-start.1) | async-done | bytes 786464 | tf_op jit(solution)/shard_map/all_to_all | solution.py:376
  129.1 1.0 copy-done.2
  130.0 10.2 %finish.1 = f32[64,256]{1,0:T(8,128)} custom-call(bf16[4,256,384]{2,1,0:T(8,128)(2,1)} %copy-done.2, bf16[3072,1536]{1,0:T(8,128)(2,1)} %all-gather.2.cloned.1.call-done.weight_ref, f32[256,3072]{1,0:T(8,128)} %copy-done, f32[1,3072]{1,0:T(1,128)} %bitcast.92, bf16[64,3072]{1,0:T(8,128)(2,1)} %bitcast.85), custom_call_target="tpu_custom_call" | custom-call | flops 2516582400 | bytes 12582912 | tf_op jit(solution)/shard_map/finish/pallas_call | solution.py:244
  140.3 0.8 multiply_convert_fusion
  141.1 3.4 %collective-permute-start.11 = (bf16[64,256]{1,0:T(8,128)(2,1)S(1)}, bf16[64,256]{1,0:T(8,128)(2,1)S(1)}, u32[]{:S(2)}, u32[]{:S(2)}) collective-permute-start(bf16[64,256]{1,0:T(8,128)(2,1)S(1)} %multiply_convert_fusion), channel_id=1, source_target_pairs={{0,4},{4,0},{1,5},{5,1},{2,6},{6,2},{3,7},{7,3},{8,12},{12,8},{9,1... | collective-permute-start | bytes 98312 | tf_op jit(solution)/shard_map/ppermute | solution.py:27
  144.5 0.9 collective-permute-done.11
  145.4 0.8 fusion.18
  146.2 1.3 collective-permute-start.12
  147.6 1.0 collective-permute-done.12
  148.6 0.9 fusion.14
  149.4 3.2 %collective-permute-start.13 = (bf16[64,256]{1,0:T(8,128)(2,1)S(1)}, bf16[64,256]{1,0:T(8,128)(2,1)S(1)}, u32[]{:S(2)}, u32[]{:S(2)}) collective-permute-start(bf16[64,256]{1,0:T(8,128)(2,1)S(1)} %fusion.14), channel_id=1, source_target_pairs={{0,16},{8,24},{16,32},{24,40},{32,48},{40,56},{48,64},{56,72},{64,... | collective-permute-start | bytes 98312 | tf_op jit(solution)/shard_map/ppermute | solution.py:23
  152.7 1.0 collective-permute-done.13
  153.7 0.9 add_convert_fusion
  154.5 10.8 %collective-permute-start.14 = (bf16[64,256]{1,0:T(8,128)(2,1)S(1)}, bf16[64,256]{1,0:T(8,128)(2,1)S(1)}, u32[]{:S(2)}, u32[]{:S(2)}) collective-permute-start(bf16[64,256]{1,0:T(8,128)(2,1)S(1)} %add_convert_fusion), channel_id=1, source_target_pairs={{0,32},{8,40},{16,48},{24,56},{32,64},{40,72},{48,80},{56,88},{64,... | collective-permute-start | bytes 98312 | tf_op jit(solution)/shard_map/ppermute | solution.py:38
  165.4 1.0 collective-permute-done.14
  166.4 0.7 collective-permute-start.15
  167.1 8.5 %collective-permute-start.16 = (bf16[64,256]{1,0:T(8,128)(2,1)S(1)}, bf16[64,256]{1,0:T(8,128)(2,1)S(1)}, u32[]{:S(2)}, u32[]{:S(2)}) collective-permute-start(bf16[64,256]{1,0:T(8,128)(2,1)S(1)} %fusion.15), channel_id=1, source_target_pairs={{0,4},{4,0},{1,5},{5,1},{2,6},{6,2},{3,7},{7,3},{8,12},{12,8},{9,1... | collective-permute-start | bytes 98312 | tf_op jit(solution)/shard_map/ppermute | solution.py:27
  175.5 0.9 collective-permute-done.16
  176.4 1.5 fusion.13
  (48 shorter events, 0.8 us)
Async XLA Ops:
  6.5 122.5 %all-gather.2.cloned.1.call-start = ((), (), s32[]{:S(2)}) async-start(), calls=%async_computation.2 | async-start | bytes 9732096 | tf_op jit(solution)/shard_map/all_gather | solution.py:310
  8.2 21.3 %collective-permute-start = (bf16[96,384]{1,0:T(8,128)(2,1)S(1)}, bf16[96,384]{1,0:T(8,128)(2,1)S(1)}, u32[]{:S(2)}, u32[]{:S(2)}) collective-permute-start(bf16[96,384]{1,0:T(8,128)(2,1)S(1)} %constant_dynamic-slice_fusion), channel_id=1, source_target_pairs={{0,4},{4,0},{1,5},{5,1},{2,6},{6,2},{3,7},{7,3},{8,12},{12,8},{9,1... | collective-permute-start | bytes 221192 | tf_op jit(solution)/shard_map/ppermute | solution.py:27
  30.5 6.7 %collective-permute-start.1 = (bf16[192,384]{1,0:T(8,128)(2,1)S(1)}, bf16[192,384]{1,0:T(8,128)(2,1)S(1)}, u32[]{:S(2)}, u32[]{:S(2)}) collective-permute-start(bf16[192,384]{1,0:T(8,128)(2,1)S(1)} %pad_maximum_fusion.4), channel_id=1, source_target_pairs={{0,8},{8,16},{16,24},{24,32},{32,40},{40,48},{48,56},{56,64},{64,7... | collective-permute-start | bytes 442376 | tf_op jit(solution)/shard_map/ppermute | solution.py:38
  35.4 1.7 copy-start
  37.1 6.1 %collective-permute-start.2 = (bf16[192,384]{1,0:T(8,128)(2,1)S(1)}, bf16[192,384]{1,0:T(8,128)(2,1)S(1)}, u32[]{:S(2)}, u32[]{:S(2)}) collective-permute-start(bf16[192,384]{1,0:T(8,128)(2,1)S(1)} %collective-permute-done.1), channel_id=1, source_target_pairs={{0,8},{8,16},{16,24},{24,32},{32,40},{40,48},{48,56},{56,64},{64,7... | collective-permute-start | bytes 442376 | tf_op jit(solution)/shard_map/ppermute | solution.py:38
  42.8 8.8 %copy-start.5 = (f32[1000]{0:T(1024)S(1)}, f32[1000]{0:T(1024)}, u32[]{:S(2)}) copy-start(f32[1000]{0:T(1024)} %param.16) | copy-start | bytes 12004
  43.2 8.4 %collective-permute-start.3 = (bf16[192,384]{1,0:T(8,128)(2,1)S(1)}, bf16[192,384]{1,0:T(8,128)(2,1)S(1)}, u32[]{:S(2)}, u32[]{:S(2)}) collective-permute-start(bf16[192,384]{1,0:T(8,128)(2,1)S(1)} %collective-permute-done.2), channel_id=1, source_target_pairs={{0,8},{8,16},{16,24},{24,32},{32,40},{40,48},{48,56},{56,64},{64,7... | collective-permute-start | bytes 442376 | tf_op jit(solution)/shard_map/ppermute | solution.py:38
  46.5 53.6 %all-to-all-start = ((bf16[4,720,384]{2,1,0:T(8,128)(2,1)}), bf16[4,720,384]{2,1,0:T(8,128)(2,1)}, u32[]{:S(2)}, u32[]{:S(2)}) async-start(bf16[4,720,384]{2,1,0:T(8,128)(2,1)} %pack.1), calls=%async_computation | async-start | bytes 4423680 | tf_op jit(solution)/shard_map/all_to_all | solution.py:365
  53.1 17.1 %copy-start.3 = (f32[3072]{0:T(1024)S(1)}, f32[3072]{0:T(1024)}, u32[]{:S(2)}) copy-start(f32[3072]{0:T(1024)} %param.19) | copy-start | bytes 36868
  53.1 22.0 %copy-start.1 = (bf16[64,3072]{1,0:T(8,128)(2,1)S(1)}, bf16[64,3072]{1,0:T(8,128)(2,1)}, u32[]{:S(2)}) copy-start(bf16[64,3072]{1,0:T(8,128)(2,1)} %param.18) | copy-start | bytes 1179652
  53.1 8.5 %collective-permute-start.4 = (bf16[192,384]{1,0:T(8,128)(2,1)S(1)}, bf16[192,384]{1,0:T(8,128)(2,1)S(1)}, u32[]{:S(2)}, u32[]{:S(2)}) collective-permute-start(bf16[192,384]{1,0:T(8,128)(2,1)S(1)} %collective-permute-done.3), channel_id=1, source_target_pairs={{0,8},{8,16},{16,24},{24,32},{32,40},{40,48},{48,56},{56,64},{64,7... | collective-permute-start | bytes 442376 | tf_op jit(solution)/shard_map/ppermute | solution.py:38
  61.6 8.6 %collective-permute-start.5 = (bf16[192,384]{1,0:T(8,128)(2,1)S(1)}, bf16[192,384]{1,0:T(8,128)(2,1)S(1)}, u32[]{:S(2)}, u32[]{:S(2)}) collective-permute-start(bf16[192,384]{1,0:T(8,128)(2,1)S(1)} %collective-permute-done.4), channel_id=1, source_target_pairs={{0,8},{8,16},{16,24},{24,32},{32,40},{40,48},{48,56},{56,64},{64,7... | collective-permute-start | bytes 442376 | tf_op jit(solution)/shard_map/ppermute | solution.py:38
  66.0 25.7 %collective-permute-start.7 = (bf16[768,384]{1,0:T(8,128)(2,1)}, bf16[768,384]{1,0:T(8,128)(2,1)}, u32[]{:S(2)}, u32[]{:S(2)}) collective-permute-start(bf16[768,384]{1,0:T(8,128)(2,1)} %pad_maximum_fusion.1), channel_id=1, source_target_pairs={{0,4},{4,0},{1,5},{5,1},{2,6},{6,2},{3,7},{7,3},{8,12},{12,8},{9,1... | collective-permute-start | bytes 1769480 | tf_op jit(solution)/shard_map/ppermute | solution.py:27
  71.5 8.8 %collective-permute-start.6 = (bf16[192,384]{1,0:T(8,128)(2,1)S(1)}, bf16[192,384]{1,0:T(8,128)(2,1)S(1)}, u32[]{:S(2)}, u32[]{:S(2)}) collective-permute-start(bf16[192,384]{1,0:T(8,128)(2,1)S(1)} %collective-permute-done.5), channel_id=1, source_target_pairs={{0,8},{8,16},{16,24},{24,32},{32,40},{40,48},{48,56},{56,64},{64,7... | collective-permute-start | bytes 442376 | tf_op jit(solution)/shard_map/ppermute | solution.py:38
  80.3 7.3 %collective-permute-start.8 = (bf16[192,384]{1,0:T(8,128)(2,1)S(1)}, bf16[192,384]{1,0:T(8,128)(2,1)S(1)}, u32[]{:S(2)}, u32[]{:S(2)}) collective-permute-start(bf16[192,384]{1,0:T(8,128)(2,1)S(1)} %collective-permute-done.6), channel_id=1, source_target_pairs={{0,8},{8,16},{16,24},{24,32},{32,40},{40,48},{48,56},{56,64},{64,7... | collective-permute-start | bytes 442376 | tf_op jit(solution)/shard_map/ppermute | solution.py:38
  87.7 8.0 %collective-permute-start.9 = (bf16[576,384]{1,0:T(8,128)(2,1)S(1)}, bf16[576,384]{1,0:T(8,128)(2,1)S(1)}, u32[]{:S(2)}, u32[]{:S(2)}) collective-permute-start(bf16[576,384]{1,0:T(8,128)(2,1)S(1)} %pad_maximum_fusion.2), channel_id=1, source_target_pairs={{0,4},{4,0},{1,5},{5,1},{2,6},{6,2},{3,7},{7,3},{8,12},{12,8},{9,1... | collective-permute-start | bytes 1327112 | tf_op jit(solution)/shard_map/ppermute | solution.py:27
  91.0 7.4 %collective-permute-start.10 = (bf16[192,384]{1,0:T(8,128)(2,1)S(1)}, bf16[192,384]{1,0:T(8,128)(2,1)S(1)}, u32[]{:S(2)}, u32[]{:S(2)}) collective-permute-start(bf16[192,384]{1,0:T(8,128)(2,1)S(1)} %collective-permute-done.8), channel_id=1, source_target_pairs={{0,8},{8,16},{16,24},{24,32},{32,40},{40,48},{48,56},{56,64},{64,7... | collective-permute-start | bytes 442376 | tf_op jit(solution)/shard_map/ppermute | solution.py:38
  114.6 14.4 %all-to-all-start.1 = ((bf16[4,256,384]{2,1,0:T(8,128)(2,1)}), bf16[4,256,384]{2,1,0:T(8,128)(2,1)S(1)}, u32[]{:S(2)}, u32[]{:S(2)}) async-start(bf16[4,256,384]{2,1,0:T(8,128)(2,1)} %bitcast.84), calls=%async_computation.1 | async-start | bytes 1572864 | tf_op jit(solution)/shard_map/all_to_all | solution.py:376
  129.1 1.0 copy-start.2
  130.0 46.4 %copy-start.4 = (f32[256,64]{0,1:T(8,128)S(1)}, f32[256,64]{0,1:T(8,128)}, u32[]{:S(2)}) copy-start(f32[256,64]{0,1:T(8,128)} %param.14) | copy-start | bytes 196612
  141.1 4.3 %collective-permute-start.11 = (bf16[64,256]{1,0:T(8,128)(2,1)S(1)}, bf16[64,256]{1,0:T(8,128)(2,1)S(1)}, u32[]{:S(2)}, u32[]{:S(2)}) collective-permute-start(bf16[64,256]{1,0:T(8,128)(2,1)S(1)} %multiply_convert_fusion), channel_id=1, source_target_pairs={{0,4},{4,0},{1,5},{5,1},{2,6},{6,2},{3,7},{7,3},{8,12},{12,8},{9,1... | collective-permute-start | bytes 98312 | tf_op jit(solution)/shard_map/ppermute | solution.py:27
  146.2 2.3 %collective-permute-start.12 = (bf16[64,256]{1,0:T(8,128)(2,1)S(1)}, bf16[64,256]{1,0:T(8,128)(2,1)S(1)}, u32[]{:S(2)}, u32[]{:S(2)}) collective-permute-start(bf16[64,256]{1,0:T(8,128)(2,1)S(1)} %fusion.18), channel_id=1, source_target_pairs={{0,8},{8,16},{16,24},{24,32},{32,40},{40,48},{48,56},{56,64},{64,7... | collective-permute-start | bytes 98312 | tf_op jit(solution)/shard_map/ppermute | solution.py:23
  149.4 4.2 %collective-permute-start.13 = (bf16[64,256]{1,0:T(8,128)(2,1)S(1)}, bf16[64,256]{1,0:T(8,128)(2,1)S(1)}, u32[]{:S(2)}, u32[]{:S(2)}) collective-permute-start(bf16[64,256]{1,0:T(8,128)(2,1)S(1)} %fusion.14), channel_id=1, source_target_pairs={{0,16},{8,24},{16,32},{24,40},{32,48},{40,56},{48,64},{56,72},{64,... | collective-permute-start | bytes 98312 | tf_op jit(solution)/shard_map/ppermute | solution.py:23
  154.5 11.8 %collective-permute-start.14 = (bf16[64,256]{1,0:T(8,128)(2,1)S(1)}, bf16[64,256]{1,0:T(8,128)(2,1)S(1)}, u32[]{:S(2)}, u32[]{:S(2)}) collective-permute-start(bf16[64,256]{1,0:T(8,128)(2,1)S(1)} %add_convert_fusion), channel_id=1, source_target_pairs={{0,32},{8,40},{16,48},{24,56},{32,64},{40,72},{48,80},{56,88},{64,... | collective-permute-start | bytes 98312 | tf_op jit(solution)/shard_map/ppermute | solution.py:38
  166.4 0.7 collective-permute-start.15
  167.1 9.3 %collective-permute-start.16 = (bf16[64,256]{1,0:T(8,128)(2,1)S(1)}, bf16[64,256]{1,0:T(8,128)(2,1)S(1)}, u32[]{:S(2)}, u32[]{:S(2)}) collective-permute-start(bf16[64,256]{1,0:T(8,128)(2,1)S(1)} %fusion.15), channel_id=1, source_target_pairs={{0,4},{4,0},{1,5},{5,1},{2,6},{6,2},{3,7},{7,3},{8,12},{12,8},{9,1... | collective-permute-start | bytes 98312 | tf_op jit(solution)/shard_map/ppermute | solution.py:27
Sparse Core Ops, SparseCore 0:
  9.2 99.3 all-gather.1

commit v3 on v2

--- a/solution.py
+++ b/solution.py
@@ -12,6 +12,7 @@
 HEAD = 128
 CORES = 2
 EXTRA = 16
+PAIR = 2
 STEP = ("chip", "core")
 REP_STEP = ("rep", "chip", "core")
 epsilon = 1e-06
@@ -38,16 +39,20 @@
     return lax.ppermute(value, ("chip", "core"), pairs)
 
 
-def gather_rows(shard, tasks):
-    chips, here, core = lax.axis_size("chip"), lax.axis_index("chip"), lax.axis_index("core")
-    other = swap_cores(shard)
-    piece = jnp.concatenate([jnp.where(core == 0, shard, other), jnp.where(core == 0, other, shard)])
-    rows = piece.shape[0]
-    step = jnp.where(core == 0, 1, -1)
+def gather_rows(piece, tasks):
+    chips, here = lax.axis_size("chip"), lax.axis_index("chip")
+    step = jnp.where(lax.axis_index("core") == 0, 1, -1)
     half = chips // 2
-    pieces, waiting, results = [(0, piece)], [], {}
+    held = [jnp.zeros((chips, *p.shape), p.dtype) for p in piece]
+
+    def put(held, piece, at):
+        owner = lax.rem(here - at * step + chips, chips)
+        return [lax.dynamic_update_slice_in_dim(h, p[None], owner, 0) for h, p in zip(held, piece)]
+
+    held = put(held, piece, 0)
+    waiting, results = [], {}
     for hop in range(1, half + 1):
-        sent = send_by_core(piece, 1, -1, True)
+        sent = tuple(send_by_core(p, 1, -1, True) for p in piece)
         if hop in tasks:
             task, inputs = tasks[hop]
             if callable(inputs):
@@ -56,18 +61,16 @@
             results[hop] = task(*inputs)
             sent, results[hop] = lax.optimization_barrier((sent, results[hop]))
         piece = sent
-        pieces.append((hop, piece))
+        held = put(held, piece, hop)
         if 2 * hop != chips:
             waiting.append((hop, piece))
         if hop in (half // 2, half - 1):
-            swapped = swap_cores(jnp.concatenate([p for _, p in waiting]))
-            for i, (at, _) in enumerate(waiting):
-                pieces.append((-at, swapped[i * rows : (i + 1) * rows]))
+            for i in range(len(piece)):
+                swapped = swap_cores(jnp.concatenate([p[i] for _, p in waiting]))
+                for j, (at, p) in enumerate(waiting):
+                    rows = p[i].shape[0]
+                    held[i] = put([held[i]], [swapped[j * rows : (j + 1) * rows]], -at)[0]
             waiting = []
-    held = jnp.zeros((chips, *piece.shape), shard.dtype)
-    for at, piece in pieces:
-        owner = lax.rem(here - at * step + chips, chips)
-        held = lax.dynamic_update_slice_in_dim(held, piece[None], owner, 0)
     return held, results
 
 
@@ -156,7 +159,7 @@
         total = jnp.sum(weights, axis=-1, keepdims=True)
         values = packed_ref[:, rows : 2 * rows, columns(past // parts)].reshape(-1, HEAD)
         blended = jnp.dot(weights.astype(jnp.bfloat16), values, preferred_element_type=jnp.float32)
-        out_ref[...] = (blended / total).astype(jnp.bfloat16)
+        out_ref[...] = jnp.broadcast_to((blended / total).astype(jnp.bfloat16), out_ref.shape)
 
     @pl.when(lax.rem(at, 2) == 0)
     def _():
@@ -175,15 +178,16 @@
 
     def past(i):
         at = jnp.maximum(i - 1, 0)
-        return lax.rem(at, parts), at // parts
+        part = lax.rem(at, parts)
+        return part // PAIR, lax.rem(part, PAIR), at // parts
 
     whole = pl.BlockSpec(memory_space=pltpu.VMEM)
     return pl.pallas_call(
         functools.partial(attention_body, parts, rows),
         grid=(heads * parts + 1,),
         in_specs=[whole, whole, whole],
-        out_specs=pl.BlockSpec((tile, HEAD), past),
-        out_shape=jax.ShapeDtypeStruct((tokens, width), jnp.bfloat16),
+        out_specs=pl.BlockSpec((PAIR, tile, HEAD), past),
+        out_shape=jax.ShapeDtypeStruct((parts, PAIR * tile, width), jnp.bfloat16),
         scratch_shapes=[pltpu.VMEM((tile, parts * rows), jnp.float32)] * 2,
         cost_estimate=pl.CostEstimate(
             flops=4 * work,
@@ -195,10 +199,22 @@
 
 
 def finish_body(
-    tile, attended_ref, weight_ref, hidden_ref, gate_ref, final_ref, out_ref, joined_ref, mixed_ref, sum_ref
+    tile,
+    attended_ref,
+    weight_ref,
+    latent_ref,
+    embed_ref,
+    bias_ref,
+    gate_ref,
+    final_ref,
+    out_ref,
+    joined_ref,
+    mixed_ref,
+    sum_ref,
 ):
     at = pl.program_id(0)
     parts, tokens, columns = attended_ref.shape
+    channels = latent_ref.shape[1]
 
     @pl.when(at == 0)
     def _():
@@ -209,62 +225,76 @@
     branch = lax.dot_general(
         joined_ref[...], weight_ref[...], (((1,), (1,)), ((), ())), preferred_element_type=jnp.float32
     )
-    mixed = hidden_ref[:, pl.ds(pl.multiple_of(at * tile, tile), tile)] + gate_ref[...] * branch
+    latent = jnp.concatenate([latent_ref[i] for i in range(PAIR)], axis=1)
+    hidden = lax.dot_general(
+        latent, embed_ref[...], (((0,), (1,)), ((), ())), preferred_element_type=jnp.float32
+    )
+    mixed = hidden + bias_ref[...] + gate_ref[...] * branch
     mixed_ref[at] = mixed
     sum_ref[...] += jnp.sum(mixed, axis=-1, keepdims=True)
 
     @pl.when(at == pl.num_programs(0) - 1)
     def _():
         count = mixed_ref.shape[0]
-        width = count * tile
-        mean = sum_ref[...] / width
-        squares = functools.reduce(
-            lambda a, b: a + b, [jnp.square(mixed_ref[i] - mean) for i in range(count)]
-        )
-        scale = lax.rsqrt(jnp.sum(squares, axis=-1, keepdims=True) / width + epsilon)
-        out_ref[...] = functools.reduce(
-            lambda a, b: a + b,
-            [
-                lax.dot_general(
-                    final_ref[:, i * tile : (i + 1) * tile],
-                    ((mixed_ref[i] - mean) * scale).astype(jnp.bfloat16),
-                    (((1,), (1,)), ((), ())),
-                    preferred_element_type=jnp.float32,
-                )
-                for i in range(count)
-            ],
-        )
-
-
-def finish(attended, out_weight, hidden, gate, final_weight):
+        mean = sum_ref[...] / (count * tile)
+        squares = jnp.zeros_like(mean)
+        product = jnp.zeros((channels, tokens), jnp.float32)
+        for i in range(count):
+            centered = mixed_ref[i] - mean
+            squares += jnp.sum(centered * centered, axis=-1, keepdims=True)
+            product += lax.dot_general(
+                final_ref[i * tile : (i + 1) * tile],
+                centered.astype(jnp.bfloat16),
+                (((0,), (1,)), ((), ())),
+                preferred_element_type=jnp.float32,
+            )
+        lane = lax.broadcasted_iota(jnp.int32, (tokens, HEAD), 1)
+        sums = jnp.where(lane == 0, mean, jnp.where(lane == 1, squares, 0.0)).T[:8]
+        whole = jnp.concatenate([product, sums])
+        for i in range(PAIR):
+            out_ref[i] = whole[:, i * (tokens // PAIR) : (i + 1) * (tokens // PAIR)]
+
+
+def finish(attended, out_weight, latent, embed_rows, embed_bias, gate, final_weight):
     parts, tokens, columns = attended.shape
     width, depth = out_weight.shape
-    channels = final_weight.shape[1]
+    channels = latent.shape[1]
     tile = min(512, width)
+    whole = pl.BlockSpec(memory_space=pltpu.VMEM)
     return pl.pallas_call(
         functools.partial(finish_body, tile),
         grid=(width // tile,),
         in_specs=[
-            pl.BlockSpec(memory_space=pltpu.VMEM),
+            whole,
             pl.BlockSpec((tile, depth), lambda i: (i, 0)),
-            pl.BlockSpec(memory_space=pltpu.VMEM),
+            whole,
+            pl.BlockSpec((tile, channels), lambda i: (i, 0)),
             pl.BlockSpec((1, tile), lambda i: (0, i)),
-            pl.BlockSpec((channels, width), lambda i: (0, 0)),
+            pl.BlockSpec((1, tile), lambda i: (0, i)),
+            whole,
         ],
-        out_specs=pl.BlockSpec((channels, tokens), lambda i: (0, 0)),
-        out_shape=jax.ShapeDtypeStruct((channels, tokens), jnp.float32),
+        out_specs=pl.BlockSpec((PAIR, channels + 8, tokens // PAIR), lambda i: (0, 0, 0)),
+        out_shape=jax.ShapeDtypeStruct((PAIR, channels + 8, tokens // PAIR), jnp.float32),
         scratch_shapes=[
             pltpu.VMEM((tokens, depth), jnp.bfloat16),
             pltpu.VMEM((width // tile, tokens, tile), jnp.float32),
             pltpu.VMEM((tokens, 1), jnp.float32),
         ],
         cost_estimate=pl.CostEstimate(
-            flops=2 * tokens * width * (depth + channels),
-            bytes_accessed=2 * width * depth + 4 * tokens * width,
+            flops=2 * tokens * width * (depth + 2 * channels),
+            bytes_accessed=2 * width * depth,
             transcendentals=0,
         ),
         name="finish",
-    )(attended, out_weight, hidden, gate.reshape(1, width), final_weight.T)
+    )(
+        attended,
+        out_weight,
+        latent,
+        embed_rows,
+        embed_bias.reshape(1, width),
+        gate.reshape(1, width),
+        final_weight,
+    )
 
 
 def prefix_over_steps(drift):
@@ -307,7 +337,13 @@
     channels, token_count = latent.shape
     key_rows = stale_keys.shape[1]
 
-    all_out_weight = lax.all_gather(out_weight, STEP, axis=0, tiled=True)
+    core = lax.axis_index("core")
+    kind = lax.rem(part, PAIR)
+    first_part = part - kind
+
+    def of_kind(rows):
+        rows = rows.reshape(-1, CORES, out_weight.shape[0], *rows.shape[1:])
+        return lax.dynamic_index_in_dim(rows, kind, 1, keepdims=False).reshape(-1, *rows.shape[3:])
 
     def embed(latent, embed_weight, embed_bias):
         hidden = lax.dot_general(
@@ -319,7 +355,7 @@
         hidden = hidden + embed_bias
         row_mean = jnp.mean(hidden, axis=-1, keepdims=True)
         row_var = jnp.mean(jnp.square(hidden - row_mean), axis=-1)
-        return hidden, jnp.sqrt(row_var + epsilon)[None]
+        return jnp.sqrt(row_var + epsilon)[None]
 
     def modulation(step_index, sigma_table, mod_weight):
         slots = jnp.arange(sigma_table.shape[0])
@@ -350,18 +386,30 @@
         ]
         return split(jnp.concatenate(rows))
 
+    def features(modulate, embed_weight, embed_bias, final_weight):
+        return (
+            of_kind(embed_weight.T),
+            of_kind(embed_bias),
+            of_kind(modulate[2 * width :]),
+            of_kind(final_weight),
+        )
+
     my_columns = lax.dynamic_slice_in_dim(query_weight, part * columns, columns, 1)
     tasks = {
         1: (embed, (latent, embed_weight, embed_bias)),
         2: (
             functools.partial(pack, parts=parts),
-            lambda done: (stale_keys[0], stale_values[0], latent, done[1][1]),
+            lambda done: (stale_keys[0], stale_values[0], latent, done[1]),
         ),
         4: (modulation, (step_index, sigma_table, mod_weight)),
         6: (sources, lambda done: (done[4][0], embed_weight, embed_bias)),
+        7: (features, lambda done: (done[4][0], embed_weight, embed_bias, final_weight)),
     }
-    gathered, done = gather_rows(my_columns, tasks)
-    hidden, (modulate, delta), source = done[1][0], done[4], done[6]
+    other = swap_cores(my_columns)
+    both = [jnp.where(core == 0, my_columns, other), jnp.where(core == 0, other, my_columns)]
+    out_rows = jnp.where(core == kind, out_weight, swap_cores(out_weight))
+    (gathered, out_rows), done = gather_rows((jnp.concatenate(both), out_rows), tasks)
+    (modulate, delta), source, parameters = done[4], done[6], done[7]
     packed = lax.all_to_all(done[2], "patch", 0, 0, tiled=True)
 
     project = jnp.dot(source, gathered.reshape(width, columns), preferred_element_type=jnp.float32)
@@ -373,11 +421,20 @@
     project = jnp.concatenate([project, jnp.broadcast_to(picks, project.shape)], axis=2)
 
     attended = attention(project, query_gain, packed, key_rows, token_count)
-    attended = lax.all_to_all(
-        attended.reshape(parts, token_count, columns), "patch", 0, 0, tiled=True
-    )
-    velocity = finish(attended, all_out_weight, hidden, modulate[2 * width :], final_weight)
-    drift = velocity * delta
+    attended = lax.all_to_all(attended, "patch", 0, 0, tiled=True)
+    latents = lax.dynamic_slice_in_dim(packed, first_part, PAIR, 0)
+    latents = latents[:, 2 * key_rows : 2 * key_rows + channels, :token_count]
+    partial = finish(attended, out_rows.reshape(-1, out_rows.shape[2]), latents, *parameters)
+    theirs = lax.dynamic_index_in_dim(partial, 1 - kind, 0, keepdims=False)
+    mine = lax.dynamic_index_in_dim(partial, kind, 0, keepdims=False)
+    theirs = lax.ppermute(theirs, "patch", [(p, p ^ 1) for p in range(parts)])
+    between = 0.5 * (theirs[channels] - mine[channels])
+    squares = mine[channels + 1] + theirs[channels + 1] + width * (between * between)
+    here_sum = jnp.sum(parameters[3].astype(jnp.float32), axis=0)
+    all_sum = jnp.sum(final_weight.astype(jnp.float32), axis=0)
+    lean = (all_sum - 2.0 * here_sum)[:, None] * between
+    scale = delta * lax.rsqrt(squares / width + epsilon)
+    drift = (mine[:channels] + theirs[:channels] + lean) * scale
     return (noise_start.T + (prefix_over_steps(drift) + drift)).T[None]
 
 

time: 186 us -> 225 us (1.21)
  local copies, waits for them, and re-layouts: 7.02 us -> 52 us
  between operations: 17.2 us -> 3.89 us
  other arithmetic: 11.1 us -> 20.4 us
  Pallas kernels: 28.7 us -> 26.3 us
    dynamic_update_slice x15 -> x30, local copies, waits for them, and re-layouts: 4.07 us -> 34 us  [put(): lax.dynamic_update_slice_in_dim(h, p[None], owner, 0)]
    concatenate x3 -> x5, other arithmetic: 0.95 us -> 8 us  [the longest x4 7.98 us: gather_rows(): swapped = swap_cores(jnp.concatenate([p[i] for _, p in waiting]))]
    ppermute x10 -> x18, waiting for transfers between devices: 17.3 us -> 10.4 us  [send_by_core(): return lax.ppermute(value, ('chip', 'core'), pairs)]
    ppermute x10 -> x18, starting transfers between devices: 34.8 us -> 28.5 us  [send_by_core(): return lax.ppermute(value, ('chip', 'core'), pairs)]
    ppermute x2, starting transfers between devices: 4.53 us -> 8.71 us  [shift(): return lax.ppermute(value, axis, pairs)]
    all_to_all x1, waiting for transfers between devices: 9.23 us -> 13.3 us  [per_device(): attended = lax.all_to_all(attended, 'patch', 0, 0, tiled=True)]
    reshape x0 -> x8, local copies, waits for them, and re-layouts: none -> 4.07 us  [the longest x4 2.73 us: of_kind(): rows = rows.reshape(-1, CORES, out_weight.shape[0], *rows.shape[1:])]
    ppermute x5 -> x8, starting transfers between devices: 35.7 us -> 38.9 us  [swap_cores(): return lax.ppermute(value, 'core', [(0, 1), (1, 0)])]
  transfers between devices with their start and end apart: 20 -> 31, of which waited for: 14 -> 10; matrix products, arithmetic and copies ran while one was open for 10% -> 32% of each run, Pallas kernels for 10% -> 8%
where the time goes in v3:
time: 225 us; the launch traced here: 223 us
  starting transfers between devices  85.3 us (38%)
  local copies, waits for them, and re-layouts  52 us (23%)
  waiting for transfers between devices  30.4 us (14%)
  Pallas kernels  26.3 us (12%)
  other arithmetic  20.4 us (9%)
  matrix products  5.03 us (2%)
  between operations  3.89 us (2%)
    ppermute x8, starting transfers between devices, swap_cores(): return lax.ppermute(value, 'core', [(0, 1), (1, 0)])  38.9 us
    dynamic_update_slice x30, local copies, waits for them, and re-layouts, put(): lax.dynamic_update_slice_in_dim(h, p[None], owner, 0)  34 us
    ppermute x18, starting transfers between devices, send_by_core(): return lax.ppermute(value, ('chip', 'core'), pairs)  28.5 us
    pallas_call x1, Pallas kernels, attention(): pl.pallas_call(functools.partial(attention_body, parts, rows), grid=(head...  14.7 us
    all_to_all x1, waiting for transfers between devices, per_device(): attended = lax.all_to_all(attended, 'patch', 0, 0, tiled=True)  13.3 us
    ppermute x18, waiting for transfers between devices, send_by_core(): return lax.ppermute(value, ('chip', 'core'), pairs)  10.4 us
    ppermute x2, starting transfers between devices, shift(): return lax.ppermute(value, axis, pairs)  8.71 us
    concatenate x4, other arithmetic, gather_rows(): swapped = swap_cores(jnp.concatenate([p[i] for _, p in waiting]))  7.98 us
  transfers between devices with their start and end apart: 31, of which 10 were waited for; matrix products, arithmetic and copies ran while one was open for 32% of the time, Pallas kernels for 8%

profile of v3, /device:TPU:33, one launch (start us, length us, event | category | flops | bytes accessed | tf_op | source)
XLA Modules:
  0.0 223.3 jit_solution(1028018383322727065)
XLA Ops:
  0.0 20.4 %collective-permute-start.2 = (bf16[96,1536]{1,0:T(8,128)(2,1)}, bf16[96,1536]{1,0:T(8,128)(2,1)S(1)}, u32[]{:S(2)}, u32[]{:S(2)}) collective-permute-start(bf16[96,1536]{1,0:T(8,128)(2,1)} %param.24), channel_id=1, source_target_pairs={{0,4},{4,0},{1,5},{5,1},{2,6},{6,2},{3,7},{7,3},{8,12},{12,8},{9,1... | collective-permute-start | bytes 884744 | tf_op jit(solution)/shard_map/ppermute | solution.py:28
  22.1 1.8 convert_reduce_fusion.2
  26.0 3.2 %collective-permute-start.1 = (bf16[192,384]{1,0:T(8,128)(2,1)S(1)}, bf16[192,384]{1,0:T(8,128)(2,1)S(1)}, u32[]{:S(2)}, u32[]{:S(2)}) collective-permute-start(bf16[192,384]{1,0:T(8,128)(2,1)S(1)} %pad_maximum_fusion.6), channel_id=1, source_target_pairs={{0,8},{8,16},{16,24},{24,32},{32,40},{40,48},{48,56},{56,64},{64,7... | collective-permute-start | bytes 442376 | tf_op jit(solution)/shard_map/ppermute | solution.py:39
  29.6 2.6 %broadcast_in_dim.169 = bf16[16,96,1536]{2,1,0:T(8,128)(2,1)} broadcast(bf16[]{:T(256)} %constant.123.clone.1), dimensions={} | broadcast | bytes 4718594 | tf_op jit(solution)/shard_map/broadcast_in_dim | solution.py:46
  34.8 3.8 %collective-permute-done.3 = bf16[96,1536]{1,0:T(8,128)(2,1)S(1)} collective-permute-done((bf16[96,1536]{1,0:T(8,128)(2,1)S(1)}, bf16[96,1536]{1,0:T(8,128)(2,1)S(1)}, u32[]{:S(2)}, u32[]{:S(2)}) %collective-permute-start.3) | collective-permute-done | bytes 294944 | tf_op jit(solution)/shard_map/ppermute | solution.py:39
  38.6 1.2 collective-permute-start.5
  40.6 3.9 %pack.1 = bf16[4,720,384]{2,1,0:T(8,128)(2,1)} custom-call(bf16[320,1536]{1,0:T(8,128)(2,1)} %bitcast.160, bf16[320,1536]{1,0:T(8,128)(2,1)} %bitcast.161, f32[64,256]{1,0:T(8,128)} %bitcast.163, f32[1,256]{1,0:T(1,128)} %bitcast.170), custom_call_target="tpu_custom_call" | custom-call | flops 1105920 | bytes 4423680 | tf_op jit(solution)/shard_map/pack/pallas_call | solution.py:110
  44.6 1.6 collective-permute-done.4
  46.2 2.2 collective-permute-start.8
  50.0 4.6 %all-to-all-start = ((bf16[4,720,384]{2,1,0:T(8,128)(2,1)}), bf16[4,720,384]{2,1,0:T(8,128)(2,1)}, u32[]{:S(2)}, u32[]{:S(2)}) async-start(bf16[4,720,384]{2,1,0:T(8,128)(2,1)} %pack.1), calls=%async_computation | async-start | bytes 4423680 | tf_op jit(solution)/shard_map/all_to_all | solution.py:413
  54.6 2.2 collective-permute-start.7
  56.8 1.0 bitcast_dynamic-update-slice_fusion.14
  59.3 1.7 bitcast_dynamic-update-slice_fusion.5
  61.0 3.7 %fusion.45 = f32[1,9216]{1,0:T(1,128)} fusion(bf16[256,1]{0,1:T(2,128)(2,1)S(1)} %reshape.130, bf16[256,9216]{1,0:T(8,128)(2,1)} %param.17), kind=kOutput, calls=%fused_computation.129 | convolution fusion | flops 4718592 | bytes 4755968 | tf_op jit(solution)/shard_map/dot_general | solution.py:365
  66.7 2.1 pad_maximum_fusion
  68.8 1.7 collective-permute-start.19
  70.6 3.0 %collective-permute-start.10 = (bf16[192,384]{1,0:T(8,128)(2,1)}, bf16[192,384]{1,0:T(8,128)(2,1)}, u32[]{:S(2)}, u32[]{:S(2)}) collective-permute-start(bf16[192,384]{1,0:T(8,128)(2,1)} %collective-permute-done.7), channel_id=1, source_target_pairs={{0,8},{8,16},{16,24},{24,32},{32,40},{40,48},{48,56},{56,64},{64,7... | collective-permute-start | bytes 442376 | tf_op jit(solution)/shard_map/ppermute | solution.py:39
  73.5 2.0 pad_maximum_fusion.3
  75.5 1.7 bitcast_dynamic-update-slice_fusion.4
  78.1 1.2 collective-permute-start.11
  82.8 1.0 collective-permute-start.13
  83.8 1.0 pad_maximum_fusion.1
  84.9 4.0 %collective-permute-done.13 = bf16[96,1536]{1,0:T(8,128)(2,1)} collective-permute-done((bf16[96,1536]{1,0:T(8,128)(2,1)S(1)}, bf16[96,1536]{1,0:T(8,128)(2,1)}, u32[]{:S(2)}, u32[]{:S(2)}) %collective-permute-start.13) | collective-permute-done | bytes 294944 | tf_op jit(solution)/shard_map/ppermute | solution.py:39
  88.9 1.8 collective-permute-start.16
  90.8 1.3 reshape.122
  92.1 1.6 constant_dynamic-slice_fusion.3
  93.7 1.1 copy.20
  95.9 1.1 copy.19
  99.8 0.9 fusion.13
  100.8 0.9 fusion.12
  101.7 0.9 fusion.11
  102.7 0.9 bitcast_dynamic-update-slice_fusion.12
  103.6 0.9 bitcast_dynamic-update-slice_fusion.11
  104.6 1.6 collective-permute-start.21
  106.1 2.0 pad_maximum_fusion.2
  108.2 1.2 collective-permute-start.18
  109.4 1.8 pad_maximum_fusion.4
  112.8 1.5 constant_dynamic-slice_fusion.2.latent_ref
  114.3 1.7 fusion.7
  116.0 1.8 fusion.6
  117.7 1.7 fusion.5
  119.4 1.7 fusion.4
  121.9 1.7 bitcast_dynamic-update-slice_fusion.2
  123.5 1.7 bitcast_dynamic-update-slice_fusion.1
  126.2 0.9 fusion.9
  127.1 0.9 fusion.8
  129.7 14.7 %attention.1 = bf16[4,512,384]{2,1,0:T(8,128)(2,1)} custom-call(bf16[4,720,384]{2,1,0:T(8,128)(2,1)} %all-to-all-done.packed_ref, bf16[3,160,256]{2,1,0:T(8,128)(2,1)} %pad_maximum_fusion.5.project_ref, f32[1,128]{1,0:T(1,128)} %bitcast.173), custom_call_target="tpu_custom_call" | custom-call | flops 2013265920 | bytes 4325376 | tf_op jit(solution)/shard_map/attention/pallas_call | solution.py:185
  144.4 4.3 %all-to-all-start.1 = ((bf16[4,512,384]{2,1,0:T(8,128)(2,1)}), bf16[4,512,384]{2,1,0:T(8,128)(2,1)S(1)}, u32[]{:S(2)}, u32[]{:S(2)}) async-start(bf16[4,512,384]{2,1,0:T(8,128)(2,1)} %attention.1), calls=%async_computation.1 | async-start | bytes 3145728 | tf_op jit(solution)/shard_map/all_to_all | solution.py:424
  148.7 1.7 fusion.3
  150.4 1.7 fusion.2
  152.1 1.7 fusion.1
  153.8 1.7 bitcast_dynamic-update-slice_fusion
  155.5 13.3 %all-to-all-done.1.attended_ref = bf16[4,512,384]{2,1,0:T(8,128)(2,1)S(1)} async-done(((bf16[4,512,384]{2,1,0:T(8,128)(2,1)}), bf16[4,512,384]{2,1,0:T(8,128)(2,1)S(1)}, u32[]{:S(2)}, u32[]{:S(2)}) %all-to-all-start.1) | async-done | bytes 1572896 | tf_op jit(solution)/shard_map/all_to_all | solution.py:424
  168.8 1.2 copy-done.1
  170.0 7.7 %finish.1 = f32[2,72,256]{2,1,0:T(8,128)} custom-call(bf16[4,512,384]{2,1,0:T(8,128)(2,1)} %copy-done.1, bf16[1536,1536]{1,0:T(8,128)(2,1)} %bitcast.49.weight_ref, bf16[2,64,256]{2,1,0:T(8,128)(2,1)} %constant_dynamic-slice_fusion.2.latent_ref, bf16[1536,64]{1,0:T(8,128)(2,1)} %bitcast.162, f32[1,1536]{1,0:T(1,128)} %reshape.128.bias_ref, ...), custom_call_target="tpu_custom_call" | custom-call | flops 2617245696 | bytes 4718592 | tf_op jit(solution)/shard_map/finish/pallas_call | solution.py:264
  178.8 2.9 %collective-permute-done.22 = f32[72,256]{1,0:T(8,128)S(1)} collective-permute-done((f32[72,256]{1,0:T(8,128)S(1)}, f32[72,256]{1,0:T(8,128)S(1)}, u32[]{:S(2)}, u32[]{:S(2)}) %collective-permute-start.22) | collective-permute-done | bytes 73760 | tf_op jit(solution)/shard_map/ppermute | solution.py:430
  183.5 2.8 %collective-permute-start.23 = (bf16[64,256]{1,0:T(8,128)(2,1)S(1)}, bf16[64,256]{1,0:T(8,128)(2,1)S(1)}, u32[]{:S(2)}, u32[]{:S(2)}) collective-permute-start(bf16[64,256]{1,0:T(8,128)(2,1)S(1)} %get-tuple-element.79), channel_id=1, source_target_pairs={{0,4},{4,0},{1,5},{5,1},{2,6},{6,2},{3,7},{7,3},{8,12},{12,8},{9,1... | collective-permute-start | bytes 98312 | tf_op jit(solution)/shard_map/ppermute | solution.py:28
  187.2 4.1 %collective-permute-start.24 = (bf16[64,256]{1,0:T(8,128)(2,1)S(1)}, bf16[64,256]{1,0:T(8,128)(2,1)S(1)}, u32[]{:S(2)}, u32[]{:S(2)}) collective-permute-start(bf16[64,256]{1,0:T(8,128)(2,1)S(1)} %fusion.27), channel_id=1, source_target_pairs={{0,8},{8,16},{16,24},{24,32},{32,40},{40,48},{48,56},{56,64},{64,7... | collective-permute-start | bytes 98312 | tf_op jit(solution)/shard_map/ppermute | solution.py:24
  191.3 1.0 collective-permute-done.24
  192.3 4.6 %collective-permute-start.25 = (bf16[64,256]{1,0:T(8,128)(2,1)S(1)}, bf16[64,256]{1,0:T(8,128)(2,1)S(1)}, u32[]{:S(2)}, u32[]{:S(2)}) collective-permute-start(bf16[64,256]{1,0:T(8,128)(2,1)S(1)} %fusion.21), channel_id=1, source_target_pairs={{0,16},{8,24},{16,32},{24,40},{32,48},{40,56},{48,64},{56,72},{64,... | collective-permute-start | bytes 98312 | tf_op jit(solution)/shard_map/ppermute | solution.py:24
  196.9 1.0 collective-permute-done.25
  197.9 8.3 %collective-permute-start.26 = (bf16[64,256]{1,0:T(8,128)(2,1)S(1)}, bf16[64,256]{1,0:T(8,128)(2,1)S(1)}, u32[]{:S(2)}, u32[]{:S(2)}) collective-permute-start(bf16[64,256]{1,0:T(8,128)(2,1)S(1)} %add_convert_fusion), channel_id=1, source_target_pairs={{0,32},{8,40},{16,48},{24,56},{32,64},{40,72},{48,80},{56,88},{64,... | collective-permute-start | bytes 98312 | tf_op jit(solution)/shard_map/ppermute | solution.py:39
  206.2 1.0 collective-permute-done.26
  207.9 13.8 %collective-permute-start.28 = (bf16[64,256]{1,0:T(8,128)(2,1)S(1)}, bf16[64,256]{1,0:T(8,128)(2,1)S(1)}, u32[]{:S(2)}, u32[]{:S(2)}) collective-permute-start(bf16[64,256]{1,0:T(8,128)(2,1)S(1)} %fusion.24), channel_id=1, source_target_pairs={{0,4},{4,0},{1,5},{5,1},{2,6},{6,2},{3,7},{7,3},{8,12},{12,8},{9,1... | collective-permute-start | bytes 98312 | tf_op jit(solution)/shard_map/ppermute | solution.py:28
  (130 shorter events, 28.3 us)
Async XLA Ops:
  0.0 29.6 %collective-permute-start.2 = (bf16[96,1536]{1,0:T(8,128)(2,1)}, bf16[96,1536]{1,0:T(8,128)(2,1)S(1)}, u32[]{:S(2)}, u32[]{:S(2)}) collective-permute-start(bf16[96,1536]{1,0:T(8,128)(2,1)} %param.24), channel_id=1, source_target_pairs={{0,4},{4,0},{1,5},{5,1},{2,6},{6,2},{3,7},{7,3},{8,12},{12,8},{9,1... | collective-permute-start | bytes 884744 | tf_op jit(solution)/shard_map/ppermute | solution.py:28
  21.3 3.8 %collective-permute-start = (bf16[96,384]{1,0:T(8,128)(2,1)S(1)}, bf16[96,384]{1,0:T(8,128)(2,1)S(1)}, u32[]{:S(2)}, u32[]{:S(2)}) collective-permute-start(bf16[96,384]{1,0:T(8,128)(2,1)S(1)} %constant_dynamic-slice_fusion.7), channel_id=1, source_target_pairs={{0,4},{4,0},{1,5},{5,1},{2,6},{6,2},{3,7},{7,3},{8,12},{12,8},{9,1... | collective-permute-start | bytes 221192 | tf_op jit(solution)/shard_map/ppermute | solution.py:28
  26.0 8.8 %collective-permute-start.1 = (bf16[192,384]{1,0:T(8,128)(2,1)S(1)}, bf16[192,384]{1,0:T(8,128)(2,1)S(1)}, u32[]{:S(2)}, u32[]{:S(2)}) collective-permute-start(bf16[192,384]{1,0:T(8,128)(2,1)S(1)} %pad_maximum_fusion.6), channel_id=1, source_target_pairs={{0,8},{8,16},{16,24},{24,32},{32,40},{40,48},{48,56},{56,64},{64,7... | collective-permute-start | bytes 442376 | tf_op jit(solution)/shard_map/ppermute | solution.py:39
  29.6 2.7 %copy-start.8 = (bf16[96,1536]{1,0:T(8,128)(2,1)S(1)}, bf16[96,1536]{1,0:T(8,128)(2,1)}, u32[]{:S(2)}) copy-start(bf16[96,1536]{1,0:T(8,128)(2,1)} %param.24) | copy-start | bytes 884740
  29.6 3.5 %copy-start = (bf16[64,3072]{1,0:T(8,128)(2,1)S(1)}, bf16[64,3072]{1,0:T(8,128)(2,1)}, u32[]{:S(2)}) copy-start(bf16[64,3072]{1,0:T(8,128)(2,1)} %param.18) | copy-start | bytes 1179652
  29.6 3.5 %copy-start.9 = (f32[1,256,64]{1,2,0:T(8,128)S(1)}, f32[1,256,64]{1,2,0:T(8,128)}, u32[]{:S(2)}) copy-start(f32[1,256,64]{1,2,0:T(8,128)} %param.13) | copy-start | bytes 196612
  29.6 3.5 %copy-start.10 = (f32[3072]{0:T(1024)S(1)}, f32[3072]{0:T(1024)}, u32[]{:S(2)}) copy-start(f32[3072]{0:T(1024)} %param.19) | copy-start | bytes 36868
  33.0 5.6 %collective-permute-start.3 = (bf16[96,1536]{1,0:T(8,128)(2,1)S(1)}, bf16[96,1536]{1,0:T(8,128)(2,1)S(1)}, u32[]{:S(2)}, u32[]{:S(2)}) collective-permute-start(bf16[96,1536]{1,0:T(8,128)(2,1)S(1)} %get-tuple-element.84), channel_id=1, source_target_pairs={{0,8},{8,16},{16,24},{24,32},{32,40},{40,48},{48,56},{56,64},{64,7... | collective-permute-start | bytes 884744 | tf_op jit(solution)/shard_map/ppermute | solution.py:39
  38.6 7.6 %collective-permute-start.5 = (bf16[96,1536]{1,0:T(8,128)(2,1)S(1)}, bf16[96,1536]{1,0:T(8,128)(2,1)S(1)}, u32[]{:S(2)}, u32[]{:S(2)}) collective-permute-start(bf16[96,1536]{1,0:T(8,128)(2,1)S(1)} %collective-permute-done.3), channel_id=1, source_target_pairs={{0,8},{8,16},{16,24},{24,32},{32,40},{40,48},{48,56},{56,64},{64,7... | collective-permute-start | bytes 884744 | tf_op jit(solution)/shard_map/ppermute | solution.py:39
  39.9 6.3 %collective-permute-start.4 = (bf16[192,384]{1,0:T(8,128)(2,1)S(1)}, bf16[192,384]{1,0:T(8,128)(2,1)}, u32[]{:S(2)}, u32[]{:S(2)}) collective-permute-start(bf16[192,384]{1,0:T(8,128)(2,1)S(1)} %collective-permute-done.1), channel_id=1, source_target_pairs={{0,8},{8,16},{16,24},{24,32},{32,40},{40,48},{48,56},{56,64},{64,7... | collective-permute-start | bytes 442376 | tf_op jit(solution)/shard_map/ppermute | solution.py:39
  46.2 11.6 %collective-permute-start.8 = (bf16[96,1536]{1,0:T(8,128)(2,1)S(1)}, bf16[96,1536]{1,0:T(8,128)(2,1)}, u32[]{:S(2)}, u32[]{:S(2)}) collective-permute-start(bf16[96,1536]{1,0:T(8,128)(2,1)S(1)} %collective-permute-done.5), channel_id=1, source_target_pairs={{0,8},{8,16},{16,24},{24,32},{32,40},{40,48},{48,56},{56,64},{64,7... | collective-permute-start | bytes 884744 | tf_op jit(solution)/shard_map/ppermute | solution.py:39
  48.3 6.3 %collective-permute-start.6 = (bf16[192,384]{1,0:T(8,128)(2,1)}, bf16[192,384]{1,0:T(8,128)(2,1)}, u32[]{:S(2)}, u32[]{:S(2)}) collective-permute-start(bf16[192,384]{1,0:T(8,128)(2,1)} %collective-permute-done.4), channel_id=1, source_target_pairs={{0,8},{8,16},{16,24},{24,32},{32,40},{40,48},{48,56},{56,64},{64,7... | collective-permute-start | bytes 442376 | tf_op jit(solution)/shard_map/ppermute | solution.py:39
  50.0 7.8 %copy-start.13 = (f32[1000]{0:T(1024)S(1)}, f32[1000]{0:T(1024)}, u32[]{:S(2)}) copy-start(f32[1000]{0:T(1024)} %param.16) | copy-start | bytes 12004
  50.0 62.7 %all-to-all-start = ((bf16[4,720,384]{2,1,0:T(8,128)(2,1)}), bf16[4,720,384]{2,1,0:T(8,128)(2,1)}, u32[]{:S(2)}, u32[]{:S(2)}) async-start(bf16[4,720,384]{2,1,0:T(8,128)(2,1)} %pack.1), calls=%async_computation | async-start | bytes 4423680 | tf_op jit(solution)/shard_map/all_to_all | solution.py:413
  54.6 11.3 %collective-permute-start.7 = (bf16[192,384]{1,0:T(8,128)(2,1)}, bf16[192,384]{1,0:T(8,128)(2,1)}, u32[]{:S(2)}, u32[]{:S(2)}) collective-permute-start(bf16[192,384]{1,0:T(8,128)(2,1)} %collective-permute-done.6), channel_id=1, source_target_pairs={{0,8},{8,16},{16,24},{24,32},{32,40},{40,48},{48,56},{56,64},{64,7... | collective-permute-start | bytes 442376 | tf_op jit(solution)/shard_map/ppermute | solution.py:39
  59.2 6.8 %collective-permute-start.9 = (bf16[96,1536]{1,0:T(8,128)(2,1)}, bf16[96,1536]{1,0:T(8,128)(2,1)}, u32[]{:S(2)}, u32[]{:S(2)}) collective-permute-start(bf16[96,1536]{1,0:T(8,128)(2,1)} %collective-permute-done.8), channel_id=1, source_target_pairs={{0,8},{8,16},{16,24},{24,32},{32,40},{40,48},{48,56},{56,64},{64,7... | collective-permute-start | bytes 884744 | tf_op jit(solution)/shard_map/ppermute | solution.py:39
  66.0 13.4 %collective-permute-start.12 = (bf16[96,1536]{1,0:T(8,128)(2,1)}, bf16[96,1536]{1,0:T(8,128)(2,1)S(1)}, u32[]{:S(2)}, u32[]{:S(2)}) collective-permute-start(bf16[96,1536]{1,0:T(8,128)(2,1)} %collective-permute-done.9), channel_id=1, source_target_pairs={{0,8},{8,16},{16,24},{24,32},{32,40},{40,48},{48,56},{56,64},{64,7... | collective-permute-start | bytes 884744 | tf_op jit(solution)/shard_map/ppermute | solution.py:39
  68.8 11.4 %copy-start.11 = (f32[3072]{0:T(1024)S(1)}, f32[3072]{0:T(1024)}, u32[]{:S(2)}) copy-start(f32[3072]{0:T(1024)} %param.19) | copy-start | bytes 36868
  68.8 45.4 %collective-permute-start.19 = (bf16[384,1536]{1,0:T(8,128)(2,1)}, bf16[384,1536]{1,0:T(8,128)(2,1)}, u32[]{:S(2)}, u32[]{:S(2)}) collective-permute-start(bf16[384,1536]{1,0:T(8,128)(2,1)} %pad_maximum_fusion), channel_id=1, source_target_pairs={{0,4},{4,0},{1,5},{5,1},{2,6},{6,2},{3,7},{7,3},{8,12},{12,8},{9,1... | collective-permute-start | bytes 3538952 | tf_op jit(solution)/shard_map/ppermute | solution.py:28
  70.6 7.6 %collective-permute-start.10 = (bf16[192,384]{1,0:T(8,128)(2,1)}, bf16[192,384]{1,0:T(8,128)(2,1)}, u32[]{:S(2)}, u32[]{:S(2)}) collective-permute-start(bf16[192,384]{1,0:T(8,128)(2,1)} %collective-permute-done.7), channel_id=1, source_target_pairs={{0,8},{8,16},{16,24},{24,32},{32,40},{40,48},{48,56},{56,64},{64,7... | collective-permute-start | bytes 442376 | tf_op jit(solution)/shard_map/ppermute | solution.py:39
  75.5 7.0 %copy-start.14 = (f32[80]{0:T(128)S(1)}, f32[80]{0:T(128)}, u32[]{:S(2)}) copy-start(f32[80]{0:T(128)} %pad.23.clone) | copy-start | bytes 964
  75.5 23.4 %collective-permute-start.14 = (bf16[768,384]{1,0:T(8,128)(2,1)}, bf16[768,384]{1,0:T(8,128)(2,1)}, u32[]{:S(2)}, u32[]{:S(2)}) collective-permute-start(bf16[768,384]{1,0:T(8,128)(2,1)} %pad_maximum_fusion.3), channel_id=1, source_target_pairs={{0,4},{4,0},{1,5},{5,1},{2,6},{6,2},{3,7},{7,3},{8,12},{12,8},{9,1... | collective-permute-start | bytes 1769480 | tf_op jit(solution)/shard_map/ppermute | solution.py:28
  78.1 6.7 %collective-permute-start.11 = (bf16[192,384]{1,0:T(8,128)(2,1)}, bf16[192,384]{1,0:T(8,128)(2,1)}, u32[]{:S(2)}, u32[]{:S(2)}) collective-permute-start(bf16[192,384]{1,0:T(8,128)(2,1)} %collective-permute-done.10), channel_id=1, source_target_pairs={{0,8},{8,16},{16,24},{24,32},{32,40},{40,48},{48,56},{56,64},{64,7... | collective-permute-start | bytes 442376 | tf_op jit(solution)/shard_map/ppermute | solution.py:39
  79.3 0.7 copy-start.4
  81.6 1.2 copy-start.5
  82.5 8.3 %copy-start.2 = (bf16[3072,64]{0,1:T(8,128)(2,1)S(1)}, bf16[3072,64]{0,1:T(8,128)(2,1)}, u32[]{:S(2)}) copy-start(bf16[3072,64]{0,1:T(8,128)(2,1)} %param.25) | copy-start | bytes 1179652
  82.8 6.1 %collective-permute-start.13 = (bf16[96,1536]{1,0:T(8,128)(2,1)S(1)}, bf16[96,1536]{1,0:T(8,128)(2,1)}, u32[]{:S(2)}, u32[]{:S(2)}) collective-permute-start(bf16[96,1536]{1,0:T(8,128)(2,1)S(1)} %copy-done.5), channel_id=1, source_target_pairs={{0,8},{8,16},{16,24},{24,32},{32,40},{40,48},{48,56},{56,64},{64,7... | collective-permute-start | bytes 884744 | tf_op jit(solution)/shard_map/ppermute | solution.py:39
  88.9 15.7 %collective-permute-start.16 = (bf16[96,1536]{1,0:T(8,128)(2,1)}, bf16[96,1536]{1,0:T(8,128)(2,1)}, u32[]{:S(2)}, u32[]{:S(2)}) collective-permute-start(bf16[96,1536]{1,0:T(8,128)(2,1)} %collective-permute-done.13), channel_id=1, source_target_pairs={{0,8},{8,16},{16,24},{24,32},{32,40},{40,48},{48,56},{56,64},{64,7... | collective-permute-start | bytes 884744 | tf_op jit(solution)/shard_map/ppermute | solution.py:39
  90.7 13.8 %collective-permute-start.15 = (bf16[192,384]{1,0:T(8,128)(2,1)}, bf16[192,384]{1,0:T(8,128)(2,1)S(1)}, u32[]{:S(2)}, u32[]{:S(2)}) collective-permute-start(bf16[192,384]{1,0:T(8,128)(2,1)} %collective-permute-done.11), channel_id=1, source_target_pairs={{0,8},{8,16},{16,24},{24,32},{32,40},{40,48},{48,56},{56,64},{64,7... | collective-permute-start | bytes 442376 | tf_op jit(solution)/shard_map/ppermute | solution.py:39
  95.9 10.3 %copy-start.6 = (bf16[96,1536]{1,0:T(8,128)(2,1)S(1)}, bf16[96,1536]{1,0:T(8,128)(2,1)}, u32[]{:S(2)}) copy-start(bf16[96,1536]{1,0:T(8,128)(2,1)} %copy-done.4) | copy-start | bytes 884740
  97.0 15.5 %copy-start.3 = (bf16[16,1,96,64]{3,2,0,1:T(8,128)(2,1)S(1)}, bf16[16,1,96,64]{3,2,0,1:T(8,128)(2,1)}, u32[]{:S(2)}) copy-start(bf16[16,1,96,64]{3,2,0,1:T(8,128)(2,1)} %copy.20) | copy-start | bytes 589828
  104.6 49.2 %collective-permute-start.21 = (bf16[96,1536]{1,0:T(8,128)(2,1)}, bf16[96,1536]{1,0:T(8,128)(2,1)}, u32[]{:S(2)}, u32[]{:S(2)}) collective-permute-start(bf16[96,1536]{1,0:T(8,128)(2,1)} %collective-permute-done.16), channel_id=1, source_target_pairs={{0,8},{8,16},{16,24},{24,32},{32,40},{40,48},{48,56},{56,64},{64,7... | collective-permute-start | bytes 884744 | tf_op jit(solution)/shard_map/ppermute | solution.py:39
  108.2 40.5 %collective-permute-start.20 = (bf16[288,1536]{1,0:T(8,128)(2,1)}, bf16[288,1536]{1,0:T(8,128)(2,1)}, u32[]{:S(2)}, u32[]{:S(2)}) collective-permute-start(bf16[288,1536]{1,0:T(8,128)(2,1)} %pad_maximum_fusion.2), channel_id=1, source_target_pairs={{0,4},{4,0},{1,5},{5,1},{2,6},{6,2},{3,7},{7,3},{8,12},{12,8},{9,1... | collective-permute-start | bytes 2654216 | tf_op jit(solution)/shard_map/ppermute | solution.py:28
  108.2 19.9 %collective-permute-start.18 = (bf16[192,384]{1,0:T(8,128)(2,1)S(1)}, bf16[192,384]{1,0:T(8,128)(2,1)S(1)}, u32[]{:S(2)}, u32[]{:S(2)}) collective-permute-start(bf16[192,384]{1,0:T(8,128)(2,1)S(1)} %collective-permute-done.15), channel_id=1, source_target_pairs={{0,8},{8,16},{16,24},{24,32},{32,40},{40,48},{48,56},{56,64},{64,7... | collective-permute-start | bytes 442376 | tf_op jit(solution)/shard_map/ppermute | solution.py:39
  111.2 14.0 %collective-permute-start.17 = (bf16[576,384]{1,0:T(8,128)(2,1)}, bf16[576,384]{1,0:T(8,128)(2,1)}, u32[]{:S(2)}, u32[]{:S(2)}) collective-permute-start(bf16[576,384]{1,0:T(8,128)(2,1)} %pad_maximum_fusion.4), channel_id=1, source_target_pairs={{0,4},{4,0},{1,5},{5,1},{2,6},{6,2},{3,7},{7,3},{8,12},{12,8},{9,1... | collective-permute-start | bytes 1327112 | tf_op jit(solution)/shard_map/ppermute | solution.py:28
  116.0 12.1 %copy-start.7 = (bf16[160,3072]{1,0:T(8,128)(2,1)S(1)}, bf16[160,3072]{1,0:T(8,128)(2,1)}, u32[]{:S(2)}) copy-start(bf16[160,3072]{1,0:T(8,128)(2,1)} %pad_maximum_fusion.1) | copy-start | bytes 2949124
  128.1 0.8 copy-start.16
  144.4 24.4 %all-to-all-start.1 = ((bf16[4,512,384]{2,1,0:T(8,128)(2,1)}), bf16[4,512,384]{2,1,0:T(8,128)(2,1)S(1)}, u32[]{:S(2)}, u32[]{:S(2)}) async-start(bf16[4,512,384]{2,1,0:T(8,128)(2,1)} %attention.1), calls=%async_computation.1 | async-start | bytes 3145728 | tf_op jit(solution)/shard_map/all_to_all | solution.py:424
  168.8 1.2 copy-start.1
  170.0 8.8 %copy-start.15 = (f32[64]{0:T(128)S(1)}, f32[64]{0:T(128)}, u32[]{:S(2)}) copy-start(f32[64]{0:T(128)} %convert_reduce_fusion.2) | copy-start | bytes 772
  170.0 52.6 %copy-start.12 = (f32[256,64]{0,1:T(8,128)S(1)}, f32[256,64]{0,1:T(8,128)}, u32[]{:S(2)}) copy-start(f32[256,64]{0,1:T(8,128)} %param.14) | copy-start | bytes 196612
  178.5 3.2 %collective-permute-start.22 = (f32[72,256]{1,0:T(8,128)S(1)}, f32[72,256]{1,0:T(8,128)S(1)}, u32[]{:S(2)}, u32[]{:S(2)}) collective-permute-start(f32[72,256]{1,0:T(8,128)S(1)} %dynamic-slice_bitcast_fusion), channel_id=1, source_target_pairs={{0,1},{1,0},{2,3},{3,2},{4,5},{5,4},{6,7},{7,6},{8,9},{9,8},{10,11... | collective-permute-start | bytes 221192 | tf_op jit(solution)/shard_map/ppermute | solution.py:430
  183.5 3.7 %collective-permute-start.23 = (bf16[64,256]{1,0:T(8,128)(2,1)S(1)}, bf16[64,256]{1,0:T(8,128)(2,1)S(1)}, u32[]{:S(2)}, u32[]{:S(2)}) collective-permute-start(bf16[64,256]{1,0:T(8,128)(2,1)S(1)} %get-tuple-element.79), channel_id=1, source_target_pairs={{0,4},{4,0},{1,5},{5,1},{2,6},{6,2},{3,7},{7,3},{8,12},{12,8},{9,1... | collective-permute-start | bytes 98312 | tf_op jit(solution)/shard_map/ppermute | solution.py:28
  187.2 5.2 %collective-permute-start.24 = (bf16[64,256]{1,0:T(8,128)(2,1)S(1)}, bf16[64,256]{1,0:T(8,128)(2,1)S(1)}, u32[]{:S(2)}, u32[]{:S(2)}) collective-permute-start(bf16[64,256]{1,0:T(8,128)(2,1)S(1)} %fusion.27), channel_id=1, source_target_pairs={{0,8},{8,16},{16,24},{24,32},{32,40},{40,48},{48,56},{56,64},{64,7... | collective-permute-start | bytes 98312 | tf_op jit(solution)/shard_map/ppermute | solution.py:24
  192.3 5.6 %collective-permute-start.25 = (bf16[64,256]{1,0:T(8,128)(2,1)S(1)}, bf16[64,256]{1,0:T(8,128)(2,1)S(1)}, u32[]{:S(2)}, u32[]{:S(2)}) collective-permute-start(bf16[64,256]{1,0:T(8,128)(2,1)S(1)} %fusion.21), channel_id=1, source_target_pairs={{0,16},{8,24},{16,32},{24,40},{32,48},{40,56},{48,64},{56,72},{64,... | collective-permute-start | bytes 98312 | tf_op jit(solution)/shard_map/ppermute | solution.py:24
  197.9 9.3 %collective-permute-start.26 = (bf16[64,256]{1,0:T(8,128)(2,1)S(1)}, bf16[64,256]{1,0:T(8,128)(2,1)S(1)}, u32[]{:S(2)}, u32[]{:S(2)}) collective-permute-start(bf16[64,256]{1,0:T(8,128)(2,1)S(1)} %add_convert_fusion), channel_id=1, source_target_pairs={{0,32},{8,40},{16,48},{24,56},{32,64},{40,72},{48,80},{56,88},{64,... | collective-permute-start | bytes 98312 | tf_op jit(solution)/shard_map/ppermute | solution.py:39
  207.2 0.7 collective-permute-start.27
  207.9 14.7 %collective-permute-start.28 = (bf16[64,256]{1,0:T(8,128)(2,1)S(1)}, bf16[64,256]{1,0:T(8,128)(2,1)S(1)}, u32[]{:S(2)}, u32[]{:S(2)}) collective-permute-start(bf16[64,256]{1,0:T(8,128)(2,1)S(1)} %fusion.24), channel_id=1, source_target_pairs={{0,4},{4,0},{1,5},{5,1},{2,6},{6,2},{3,7},{7,3},{8,12},{12,8},{9,1... | collective-permute-start | bytes 98312 | tf_op jit(solution)/shard_map/ppermute | solution.py:28

commit v4 on v2

--- a/solution.py
+++ b/solution.py
@@ -12,6 +12,7 @@
 HEAD = 128
 CORES = 2
 EXTRA = 16
+GATHER_AFTER = 2
 STEP = ("chip", "core")
 REP_STEP = ("rep", "chip", "core")
 epsilon = 1e-06
@@ -38,37 +39,55 @@
     return lax.ppermute(value, ("chip", "core"), pairs)
 
 
-def gather_rows(shard, tasks):
-    chips, here, core = lax.axis_size("chip"), lax.axis_index("chip"), lax.axis_index("core")
-    other = swap_cores(shard)
-    piece = jnp.concatenate([jnp.where(core == 0, shard, other), jnp.where(core == 0, other, shard)])
-    rows = piece.shape[0]
-    step = jnp.where(core == 0, 1, -1)
-    half = chips // 2
-    pieces, waiting, results = [(0, piece)], [], {}
-    for hop in range(1, half + 1):
+def project_body(chips, order_ref, source_ref, *refs):
+    pieces, out_ref = refs[:-1], refs[-1]
+    total = jnp.zeros((source_ref.shape[1], out_ref.shape[2]), jnp.float32)
+    for k, piece in enumerate(pieces):
+        product = jnp.dot(
+            source_ref[order_ref[k]], piece[...], preferred_element_type=jnp.float32
+        )
+        total += jnp.where(order_ref[len(pieces) + k] == 1, product, 0.0)
+    deep = out_ref.shape[1]
+    for i in range(2):
+        out_ref[i] = total[2 * i * deep : (2 * i + 1) * deep] + total[(2 * i + 1) * deep : (2 * i + 2) * deep]
+
+
+def project_rows(source, pieces, owners, used):
+    chips, height, rows = source.shape
+    columns = pieces[0].shape[1]
+    order = jnp.stack(owners + [u.astype(jnp.int32) for u in used])
+    whole = pl.BlockSpec(memory_space=pltpu.VMEM)
+    return pl.pallas_call(
+        functools.partial(project_body, chips),
+        in_specs=[pl.BlockSpec(memory_space=pltpu.SMEM), whole] + [whole] * len(pieces),
+        out_specs=whole,
+        out_shape=jax.ShapeDtypeStruct((2, height // 4, columns), jnp.float32),
+        cost_estimate=pl.CostEstimate(
+            flops=2 * len(pieces) * height * rows * columns,
+            bytes_accessed=len(pieces) * rows * (2 * columns + 2 * height),
+            transcendentals=0,
+        ),
+        name="project",
+    )(order, source, *pieces)
+
+
+def pass_round(piece, tasks):
+    chips, here = lax.axis_size("chip"), lax.axis_index("chip")
+    step = jnp.where(lax.axis_index("core") == 0, 1, -1)
+    pieces, results = [piece], {}
+    owners = [lax.rem(here - hop * step + chips, chips) for hop in range(chips // 2 + 1)]
+    for hop in range(1, chips // 2 + 1):
         sent = send_by_core(piece, 1, -1, True)
         if hop in tasks:
             task, inputs = tasks[hop]
             if callable(inputs):
-                inputs = inputs(results)
+                inputs = inputs(results, pieces, owners)
             _, inputs = lax.optimization_barrier((piece, inputs))
             results[hop] = task(*inputs)
             sent, results[hop] = lax.optimization_barrier((sent, results[hop]))
         piece = sent
-        pieces.append((hop, piece))
-        if 2 * hop != chips:
-            waiting.append((hop, piece))
-        if hop in (half // 2, half - 1):
-            swapped = swap_cores(jnp.concatenate([p for _, p in waiting]))
-            for i, (at, _) in enumerate(waiting):
-                pieces.append((-at, swapped[i * rows : (i + 1) * rows]))
-            waiting = []
-    held = jnp.zeros((chips, *piece.shape), shard.dtype)
-    for at, piece in pieces:
-        owner = lax.rem(here - at * step + chips, chips)
-        held = lax.dynamic_update_slice_in_dim(held, piece[None], owner, 0)
-    return held, results
+        pieces.append(piece)
+    return pieces, owners, results
 
 
 def time_embed(sigma_now, half_count):
@@ -144,13 +163,10 @@
         raw, spread = both[:, :HEAD], both[:, HEAD:]
         square = jnp.mean(raw * raw, axis=-1, keepdims=True) + epsilon * (spread * spread)
         queries = (raw * lax.rsqrt(square) * gain_ref[...]).astype(jnp.bfloat16)
-        for p in range(parts):
-            now_ref[:, p * rows : (p + 1) * rows] = lax.dot_general(
-                queries,
-                packed_ref[p, :rows, columns(head)],
-                (((1,), (1,)), ((), ())),
-                preferred_element_type=jnp.float32,
-            )
+        keys = packed_ref[:, :rows, columns(head)].reshape(-1, HEAD)
+        now_ref[...] = lax.dot_general(
+            queries, keys, (((1,), (1,)), ((), ())), preferred_element_type=jnp.float32
+        )
         peak = jnp.max(past_ref[...], axis=-1, keepdims=True)
         weights = jnp.exp((past_ref[...] - peak) * (1.0 / math.sqrt(HEAD)))
         total = jnp.sum(weights, axis=-1, keepdims=True)
@@ -195,10 +211,10 @@
 
 
 def finish_body(
-    tile, attended_ref, weight_ref, hidden_ref, gate_ref, final_ref, out_ref, joined_ref, mixed_ref, sum_ref
+    tile, attended_ref, weight_ref, hidden_ref, gate_ref, final_ref, delta_ref, out_ref, joined_ref, mixed_ref, sum_ref
 ):
     at = pl.program_id(0)
-    parts, tokens, columns = attended_ref.shape
+    parts, _, columns = attended_ref.shape
 
     @pl.when(at == 0)
     def _():
@@ -207,56 +223,54 @@
         sum_ref[...] = jnp.zeros_like(sum_ref)
 
     branch = lax.dot_general(
-        joined_ref[...], weight_ref[...], (((1,), (1,)), ((), ())), preferred_element_type=jnp.float32
-    )
-    mixed = hidden_ref[:, pl.ds(pl.multiple_of(at * tile, tile), tile)] + gate_ref[...] * branch
+        weight_ref[...], joined_ref[...], (((1,), (1,)), ((), ())), preferred_element_type=jnp.float32
+    )
+    mixed = hidden_ref[pl.ds(pl.multiple_of(at * tile, tile), tile)] + gate_ref[...] * branch
     mixed_ref[at] = mixed
-    sum_ref[...] += jnp.sum(mixed, axis=-1, keepdims=True)
+    sum_ref[...] += jnp.sum(mixed, axis=0, keepdims=True)
 
     @pl.when(at == pl.num_programs(0) - 1)
     def _():
         count = mixed_ref.shape[0]
         width = count * tile
         mean = sum_ref[...] / width
-        squares = functools.reduce(
-            lambda a, b: a + b, [jnp.square(mixed_ref[i] - mean) for i in range(count)]
-        )
-        scale = lax.rsqrt(jnp.sum(squares, axis=-1, keepdims=True) / width + epsilon)
-        out_ref[...] = functools.reduce(
-            lambda a, b: a + b,
-            [
-                lax.dot_general(
-                    final_ref[:, i * tile : (i + 1) * tile],
-                    ((mixed_ref[i] - mean) * scale).astype(jnp.bfloat16),
-                    (((1,), (1,)), ((), ())),
-                    preferred_element_type=jnp.float32,
-                )
-                for i in range(count)
-            ],
-        )
-
-
-def finish(attended, out_weight, hidden, gate, final_weight):
+        squares = jnp.zeros_like(mean)
+        for i in range(count):
+            squares += jnp.sum(jnp.square(mixed_ref[i] - mean), axis=0, keepdims=True)
+        scale = lax.rsqrt(squares / width + epsilon)
+        velocity = jnp.zeros(out_ref.shape, jnp.float32)
+        for i in range(count):
+            velocity += jnp.dot(
+                final_ref[:, i * tile : (i + 1) * tile],
+                ((mixed_ref[i] - mean) * scale).astype(jnp.bfloat16),
+                preferred_element_type=jnp.float32,
+            )
+        out_ref[...] = velocity * delta_ref[0]
+
+
+def finish(attended, out_weight, hidden, gate, final_weight, delta):
     parts, tokens, columns = attended.shape
     width, depth = out_weight.shape
     channels = final_weight.shape[1]
     tile = min(512, width)
+    whole = pl.BlockSpec(memory_space=pltpu.VMEM)
     return pl.pallas_call(
         functools.partial(finish_body, tile),
         grid=(width // tile,),
         in_specs=[
-            pl.BlockSpec(memory_space=pltpu.VMEM),
+            whole,
             pl.BlockSpec((tile, depth), lambda i: (i, 0)),
-            pl.BlockSpec(memory_space=pltpu.VMEM),
-            pl.BlockSpec((1, tile), lambda i: (0, i)),
-            pl.BlockSpec((channels, width), lambda i: (0, 0)),
+            whole,
+            pl.BlockSpec((tile, 1), lambda i: (i, 0)),
+            whole,
+            pl.BlockSpec(memory_space=pltpu.SMEM),
         ],
-        out_specs=pl.BlockSpec((channels, tokens), lambda i: (0, 0)),
+        out_specs=whole,
         out_shape=jax.ShapeDtypeStruct((channels, tokens), jnp.float32),
         scratch_shapes=[
             pltpu.VMEM((tokens, depth), jnp.bfloat16),
-            pltpu.VMEM((width // tile, tokens, tile), jnp.float32),
-            pltpu.VMEM((tokens, 1), jnp.float32),
+            pltpu.VMEM((width // tile, tile, tokens), jnp.float32),
+            pltpu.VMEM((1, tokens), jnp.float32),
         ],
         cost_estimate=pl.CostEstimate(
             flops=2 * tokens * width * (depth + channels),
@@ -264,7 +278,7 @@
             transcendentals=0,
         ),
         name="finish",
-    )(attended, out_weight, hidden, gate.reshape(1, width), final_weight.T)
+    )(attended, out_weight, hidden, gate.reshape(width, 1), final_weight.T, delta.reshape(1))
 
 
 def prefix_over_steps(drift):
@@ -307,66 +321,86 @@
     channels, token_count = latent.shape
     key_rows = stale_keys.shape[1]
 
-    all_out_weight = lax.all_gather(out_weight, STEP, axis=0, tiled=True)
+    core = lax.axis_index("core")
 
     def embed(latent, embed_weight, embed_bias):
         hidden = lax.dot_general(
+            embed_weight,
             latent.astype(jnp.bfloat16),
-            embed_weight,
             (((0,), (0,)), ((), ())),
             preferred_element_type=jnp.float32,
         )
-        hidden = hidden + embed_bias
-        row_mean = jnp.mean(hidden, axis=-1, keepdims=True)
-        row_var = jnp.mean(jnp.square(hidden - row_mean), axis=-1)
-        return hidden, jnp.sqrt(row_var + epsilon)[None]
-
-    def modulation(step_index, sigma_table, mod_weight):
+        hidden = hidden + embed_bias[:, None]
+        mean = jnp.mean(hidden, axis=0, keepdims=True)
+        variance = jnp.mean(jnp.square(hidden - mean), axis=0, keepdims=True)
+        return hidden, jnp.sqrt(variance + epsilon)
+
+    def levels(step_index, sigma_table):
         slots = jnp.arange(sigma_table.shape[0])
         sigma_now = jnp.sum(jnp.where(slots == step_index[0], sigma_table, 0.0))
         sigma_next = jnp.sum(jnp.where(slots == step_index[0] + 1, sigma_table, 0.0))
-        embedded = jax.nn.silu(time_embed(sigma_now, mod_weight.shape[0] // 2)).astype(jnp.bfloat16)
-        modulate = jnp.dot(embedded[None, :], mod_weight, preferred_element_type=jnp.float32)[0]
-        return modulate, sigma_next - sigma_now
-
-    def split(value):
-        coarse = value.astype(jnp.bfloat16)
-        return jnp.concatenate([coarse, (value - coarse.astype(jnp.float32)).astype(jnp.bfloat16)])
+        return sigma_now, sigma_next - sigma_now
+
+    def modulation(sigma_now, sigma_other, mod_weight):
+        embedded = [time_embed(s, mod_weight.shape[0] // 2) for s in (sigma_now, sigma_other)]
+        embedded = jax.nn.silu(jnp.stack(embedded)).astype(jnp.bfloat16)
+        return jnp.dot(embedded, mod_weight, preferred_element_type=jnp.float32)
 
     def sources(modulate, embed_weight, embed_bias):
-        shift_vec, scale_vec = modulate[:width], modulate[width : 2 * width]
         weight = embed_weight.astype(jnp.float32)
         centered = jnp.concatenate(
             [
                 weight - jnp.mean(weight, axis=-1, keepdims=True),
                 (embed_bias - jnp.mean(embed_bias))[None],
+                jnp.zeros((EXTRA - 1, width), jnp.float32),
             ]
         )
-        rows = [
-            centered * (1.0 + scale_vec),
-            shift_vec[None],
-            shift_vec[None],
-            jnp.zeros((EXTRA - 3, width), jnp.float32),
-        ]
-        return split(jnp.concatenate(rows))
+        row = lax.broadcasted_iota(jnp.int32, (centered.shape[0], 1), 0)
+        shifted = (row == channels + 1) | (row == channels + 2)
+        rows = []
+        for i in range(CORES):
+            shift_vec, scale_vec = modulate[i, :width], modulate[i, width : 2 * width]
+            value = jnp.where(shifted, shift_vec, centered * (1.0 + scale_vec))
+            coarse = value.astype(jnp.bfloat16)
+            rows += [coarse, (value - coarse.astype(jnp.float32)).astype(jnp.bfloat16)]
+        rows = jnp.concatenate(rows)
+        return jnp.moveaxis(rows.reshape(rows.shape[0], lax.axis_size("chip"), -1), 1, 0)
+
+    def split(value):
+        coarse = value.astype(jnp.bfloat16)
+        return jnp.concatenate([coarse, (value - coarse.astype(jnp.float32)).astype(jnp.bfloat16)])
+
+    def first_pieces(done, pieces, owners):
+        ready = pieces[: last_hop - 1]
+        return done[6], ready, owners[: len(ready)], [core == 0] + [core >= 0] * (len(ready) - 1)
 
     my_columns = lax.dynamic_slice_in_dim(query_weight, part * columns, columns, 1)
+    sigma_now, delta = levels(step_index, sigma_table)
+    sigma_other = swap_cores(jnp.full((8, HEAD), sigma_now))[0, 0]
+    other = swap_cores(my_columns)
+    piece = [jnp.where(core == 0, my_columns, other), jnp.where(core == 0, other, my_columns)]
+    last_hop = lax.axis_size("chip") // 2
     tasks = {
         1: (embed, (latent, embed_weight, embed_bias)),
         2: (
             functools.partial(pack, parts=parts),
-            lambda done: (stale_keys[0], stale_values[0], latent, done[1][1]),
+            lambda done, *_: (stale_keys[0], stale_values[0], latent, done[1][1]),
         ),
-        4: (modulation, (step_index, sigma_table, mod_weight)),
-        6: (sources, lambda done: (done[4][0], embed_weight, embed_bias)),
+        4: (modulation, (sigma_now, sigma_other, mod_weight)),
+        6: (sources, lambda done, *_: (done[4], embed_weight, embed_bias)),
+        last_hop: (project_rows, first_pieces),
     }
-    gathered, done = gather_rows(my_columns, tasks)
-    hidden, (modulate, delta), source = done[1][0], done[4], done[6]
+    pieces, owners, done = pass_round(jnp.concatenate(piece), tasks)
+    hidden, modulate, source = done[1][0], done[4][0], done[6]
     packed = lax.all_to_all(done[2], "patch", 0, 0, tiled=True)
-
-    project = jnp.dot(source, gathered.reshape(width, columns), preferred_element_type=jnp.float32)
+    _, late = lax.optimization_barrier((pieces[GATHER_AFTER], out_weight))
+    all_out_weight = lax.all_gather(late, STEP, axis=0, tiled=True)
+
     deep = channels + EXTRA
-    project = split(project[:deep] + project[deep:])
+    shares = done[last_hop] + project_rows(
+        source, pieces[-2:], owners[-2:], [core >= 0, core == 1]
+    )
+    project = split(shares[0] + swap_cores(shares[1]))
     project = jnp.moveaxis(project.reshape(2 * deep, -1, HEAD), 1, 0)
     row = lax.broadcasted_iota(jnp.int32, (1, 2 * deep, HEAD), 1)
     picks = jnp.where((row == channels + 1) | (row == channels + 2), 1.0, 0.0).astype(jnp.bfloat16)
@@ -376,8 +410,7 @@
     attended = lax.all_to_all(
         attended.reshape(parts, token_count, columns), "patch", 0, 0, tiled=True
     )
-    velocity = finish(attended, all_out_weight, hidden, modulate[2 * width :], final_weight)
-    drift = velocity * delta
+    drift = finish(attended, all_out_weight, hidden, modulate[2 * width :], final_weight, delta)
     return (noise_start.T + (prefix_over_steps(drift) + drift)).T[None]
 
 

time: 186 us -> 188 us (1.011)
  Pallas kernels: 28.7 us -> 34.6 us
  waiting for transfers between devices: 31.1 us -> 25.5 us
  other arithmetic: 11.1 us -> 14.2 us
    ppermute x10, waiting for transfers between devices: 17.3 us -> 9.29 us  [send_by_core(): return lax.ppermute(value, ('chip', 'core'), pairs)]
    pallas_call x0 -> x2, Pallas kernels: none -> 6.49 us  [project_rows(): pl.pallas_call(functools.partial(project_body, chips), in_specs=[pl.Block...]
    dynamic_update_slice x15 -> x0, local copies, waits for them, and re-layouts: 4.07 us -> none  [gather_rows(): held = lax.dynamic_update_slice_in_dim(held, piece[None], owner, 0)]
    ppermute x10, starting transfers between devices: 34.8 us -> 31.3 us  [send_by_core(): return lax.ppermute(value, ('chip', 'core'), pairs)]
    ppermute x5, starting transfers between devices: 35.7 us -> 38.5 us  [swap_cores(): return lax.ppermute(value, 'core', [(0, 1), (1, 0)])]
    ppermute x5, waiting for transfers between devices: 1.87 us -> 3.78 us  [swap_cores(): return lax.ppermute(value, 'core', [(0, 1), (1, 0)])]
    dot_general x3 -> x2, matrix products: 5.52 us -> 4.91 us  [the longest x1 3.06 us: modulation(): return jnp.dot(embedded, mod_weight, preferred_element_type=jnp.float32)]
  transfers between devices with their start and end apart: 20 -> 20, of which waited for: 14 -> 12; matrix products, arithmetic and copies ran while one was open for 10% -> 10% of each run, Pallas kernels for 10% -> 13%
where the time goes in v4:
time: 188 us; the launch traced here: 187 us
  starting transfers between devices  82.9 us (44%)
  Pallas kernels  34.6 us (18%)
  waiting for transfers between devices  25.5 us (14%)
  between operations  17.5 us (9%)
  other arithmetic  14.2 us (8%)
  local copies, waits for them, and re-layouts  7.59 us (4%)
  matrix products  4.91 us (3%)
    ppermute x5, starting transfers between devices, swap_cores(): return lax.ppermute(value, 'core', [(0, 1), (1, 0)])  38.5 us
    ppermute x10, starting transfers between devices, send_by_core(): return lax.ppermute(value, ('chip', 'core'), pairs)  31.3 us
    pallas_call x1, Pallas kernels, attention(): pl.pallas_call(functools.partial(attention_body, parts, rows), grid=(head...  14.2 us
    all_to_all x1, waiting for transfers between devices, per_device(): lax.all_to_all(attended.reshape(parts, token_count, columns), 'patch', 0,...  10.4 us
    pallas_call x1, Pallas kernels, finish(): pl.pallas_call(functools.partial(finish_body, tile), grid=(width // tile,...  9.92 us
    ppermute x10, waiting for transfers between devices, send_by_core(): return lax.ppermute(value, ('chip', 'core'), pairs)  9.29 us
    pallas_call x2, Pallas kernels, project_rows(): pl.pallas_call(functools.partial(project_body, chips), in_specs=[pl.Block...  6.49 us
    all_to_all x1, starting transfers between devices, per_device(): packed = lax.all_to_all(done[2], 'patch', 0, 0, tiled=True)  4.79 us
  transfers between devices with their start and end apart: 20, of which 12 were waited for; matrix products, arithmetic and copies ran while one was open for 10% of the time, Pallas kernels for 13%

profile of v4, /device:TPU:33, one launch (start us, length us, event | category | flops | bytes accessed | tf_op | source)
XLA Modules:
  0.0 187.2 jit_solution(9670199975615724891)
XLA Ops:
  6.6 0.9 constant_dynamic-slice_fusion
  7.4 20.4 %collective-permute-start = (bf16[96,384]{1,0:T(8,128)(2,1)S(1)}, bf16[96,384]{1,0:T(8,128)(2,1)S(1)}, u32[]{:S(2)}, u32[]{:S(2)}) collective-permute-start(bf16[96,384]{1,0:T(8,128)(2,1)S(1)} %constant_dynamic-slice_fusion), channel_id=1, source_target_pairs={{0,4},{4,0},{1,5},{5,1},{2,6},{6,2},{3,7},{7,3},{8,12},{12,8},{9,1... | collective-permute-start | bytes 221192 | tf_op jit(solution)/shard_map/ppermute | solution.py:28
  27.9 0.9 collective-permute-done
  28.8 0.9 broadcast_select_fusion.1
  29.7 3.2 %collective-permute-start.1 = (bf16[192,384]{1,0:T(8,128)(2,1)S(1)}, bf16[192,384]{1,0:T(8,128)(2,1)S(1)}, u32[]{:S(2)}, u32[]{:S(2)}) collective-permute-start(bf16[192,384]{1,0:T(8,128)(2,1)S(1)} %pad_maximum_fusion.1.refs_0_), channel_id=1, source_target_pairs={{0,8},{8,16},{16,24},{24,32},{32,40},{40,48},{48,56},{56,64},{64,7... | collective-permute-start | bytes 442376 | tf_op jit(solution)/shard_map/ppermute | solution.py:39
  32.9 1.8 fusion.28
  34.8 0.4 multiply_reduce_fusion
  35.3 0.9 add_sqrt_fusion
  36.2 2.0 %collective-permute-start.2 = (bf16[192,384]{1,0:T(8,128)(2,1)S(1)}, bf16[192,384]{1,0:T(8,128)(2,1)S(1)}, u32[]{:S(2)}, u32[]{:S(2)}) collective-permute-start(bf16[192,384]{1,0:T(8,128)(2,1)S(1)} %collective-permute-done.1.refs_1_), channel_id=1, source_target_pairs={{0,8},{8,16},{16,24},{24,32},{32,40},{40,48},{48,56},{56,64},{64,7... | collective-permute-start | bytes 442376 | tf_op jit(solution)/shard_map/ppermute | solution.py:39
  38.2 4.0 %pack.1 = bf16[4,720,384]{2,1,0:T(8,128)(2,1)} custom-call(bf16[320,1536]{1,0:T(8,128)(2,1)} %bitcast.64, bf16[320,1536]{1,0:T(8,128)(2,1)} %bitcast.65, f32[64,256]{1,0:T(8,128)} %bitcast.69, f32[1,256]{1,0:T(1,128)} %bitcast.70), custom_call_target="tpu_custom_call" | custom-call | flops 1105920 | bytes 4423680 | tf_op jit(solution)/shard_map/pack/pallas_call | solution.py:126
  42.2 1.3 collective-permute-start.3
  44.2 0.7 select_reduce_fusion
  44.9 0.6 broadcast_in_dim.62
  45.5 0.1 collective-permute-start.5
  45.6 1.1 collective-permute-done.5
  46.8 0.5 slice.27
  48.6 2.4 %collective-permute-start.4 = (bf16[192,384]{1,0:T(8,128)(2,1)S(1)}, bf16[192,384]{1,0:T(8,128)(2,1)S(1)}, u32[]{:S(2)}, u32[]{:S(2)}) collective-permute-start(bf16[192,384]{1,0:T(8,128)(2,1)S(1)} %collective-permute-done.3.refs_3_), channel_id=1, source_target_pairs={{0,8},{8,16},{16,24},{24,32},{32,40},{40,48},{48,56},{56,64},{64,7... | collective-permute-start | bytes 442376 | tf_op jit(solution)/shard_map/ppermute | solution.py:39
  51.2 3.1 %fusion.15 = f32[2,9216]{1,0:T(2,128)S(1)} fusion(bf16[256,9216]{1,0:T(8,128)(2,1)} %param.17, f32[1,256]{1,0:T(1,128)S(1)} %bitcast.72, f32[1,256]{1,0:T(1,128)S(1)} %bitcast.71), kind=kOutput, calls=%fused_computation.54 | convolution fusion | flops 9440256 | bytes 4794368 | tf_op jit(solution)/shard_map/dot_general | solution.py:347
  54.2 1.1 collective-permute-done.4.refs_4_
  55.3 3.5 %collective-permute-start.6 = (bf16[192,384]{1,0:T(8,128)(2,1)S(1)}, bf16[192,384]{1,0:T(8,128)(2,1)S(1)}, u32[]{:S(2)}, u32[]{:S(2)}) collective-permute-start(bf16[192,384]{1,0:T(8,128)(2,1)S(1)} %collective-permute-done.4.refs_4_), channel_id=1, source_target_pairs={{0,8},{8,16},{16,24},{24,32},{32,40},{40,48},{48,56},{56,64},{64,7... | collective-permute-start | bytes 442376 | tf_op jit(solution)/shard_map/ppermute | solution.py:39
  58.9 4.8 %all-to-all-start = ((bf16[4,720,384]{2,1,0:T(8,128)(2,1)}), bf16[4,720,384]{2,1,0:T(8,128)(2,1)}, u32[]{:S(2)}, u32[]{:S(2)}) async-start(bf16[4,720,384]{2,1,0:T(8,128)(2,1)} %pack.1), calls=%async_computation | async-start | bytes 4423680 | tf_op jit(solution)/shard_map/all_to_all | solution.py:395
  63.8 0.2 convert_reduce_fusion
  64.1 0.5 concatenate.33
  64.6 0.6 copy.14
  65.2 0.1 slice_reduce_fusion.1
  65.6 0.6 reduce_sum.58
  67.0 0.4 fusion
  67.5 3.6 %collective-permute-start.7 = (bf16[192,384]{1,0:T(8,128)(2,1)S(1)}, bf16[192,384]{1,0:T(8,128)(2,1)S(1)}, u32[]{:S(2)}, u32[]{:S(2)}) collective-permute-start(bf16[192,384]{1,0:T(8,128)(2,1)S(1)} %collective-permute-done.6.refs_5_), channel_id=1, source_target_pairs={{0,8},{8,16},{16,24},{24,32},{32,40},{40,48},{48,56},{56,64},{64,7... | collective-permute-start | bytes 442376 | tf_op jit(solution)/shard_map/ppermute | solution.py:39
  71.1 0.6 subtract_convert_fusion.1
  71.7 1.7 maximum_bitcast_fusion.source_ref
  73.4 2.9 %collective-permute-done.7.refs_6_ = bf16[192,384]{1,0:T(8,128)(2,1)S(1)} collective-permute-done((bf16[192,384]{1,0:T(8,128)(2,1)S(1)}, bf16[192,384]{1,0:T(8,128)(2,1)S(1)}, u32[]{:S(2)}, u32[]{:S(2)}) %collective-permute-start.7) | collective-permute-done | bytes 147488 | tf_op jit(solution)/shard_map/ppermute | solution.py:39
  76.3 3.5 %collective-permute-start.8 = (bf16[192,384]{1,0:T(8,128)(2,1)S(1)}, bf16[192,384]{1,0:T(8,128)(2,1)S(1)}, u32[]{:S(2)}, u32[]{:S(2)}) collective-permute-start(bf16[192,384]{1,0:T(8,128)(2,1)S(1)} %collective-permute-done.7.refs_6_), channel_id=1, source_target_pairs={{0,8},{8,16},{16,24},{24,32},{32,40},{40,48},{48,56},{56,64},{64,7... | collective-permute-start | bytes 442376 | tf_op jit(solution)/shard_map/ppermute | solution.py:39
  79.8 4.1 %collective-permute-done.8.refs_0_ = bf16[192,384]{1,0:T(8,128)(2,1)S(1)} collective-permute-done((bf16[192,384]{1,0:T(8,128)(2,1)S(1)}, bf16[192,384]{1,0:T(8,128)(2,1)S(1)}, u32[]{:S(2)}, u32[]{:S(2)}) %collective-permute-start.8) | collective-permute-done | bytes 147488 | tf_op jit(solution)/shard_map/ppermute | solution.py:39
  83.9 3.5 %collective-permute-start.9 = (bf16[192,384]{1,0:T(8,128)(2,1)S(1)}, bf16[192,384]{1,0:T(8,128)(2,1)S(1)}, u32[]{:S(2)}, u32[]{:S(2)}) collective-permute-start(bf16[192,384]{1,0:T(8,128)(2,1)S(1)} %collective-permute-done.8.refs_0_), channel_id=1, source_target_pairs={{0,8},{8,16},{16,24},{24,32},{32,40},{40,48},{48,56},{56,64},{64,7... | collective-permute-start | bytes 442376 | tf_op jit(solution)/shard_map/ppermute | solution.py:39
  87.4 0.6 pad_add_fusion.order_ref
  88.0 0.6 stack.120.order_ref
  88.7 3.6 %project.2 = f32[2,80,384]{2,1,0:T(8,128)} custom-call(s32[14]{0:T(128)} %stack.120.order_ref, bf16[16,320,192]{2,1,0:T(8,128)(2,1)} %maximum_bitcast_fusion.source_ref, bf16[192,384]{1,0:T(8,128)(2,1)} %copy-done.4, bf16[192,384]{1,0:T(8,128)(2,1)} %copy-done.5, bf16[192,384]{1,0:T(8,128)(2,1)} %copy-done.6, bf16[192,384]{1,0:T(8,128)(2,1)} %copy-done.7, ...), custom_call_target="tpu_custom_call" | custom-call | flops 330301440 | bytes 1892352 | tf_op jit(solution)/shard_map/project/pallas_call | solution.py:60
  92.3 0.6 copy-done.12
  92.9 2.9 %project.3 = f32[2,80,384]{2,1,0:T(8,128)} custom-call(s32[4]{0:T(128)} %pad_add_fusion.order_ref, bf16[16,320,192]{2,1,0:T(8,128)(2,1)} %maximum_bitcast_fusion.source_ref, bf16[192,384]{1,0:T(8,128)(2,1)} %copy-done.11, bf16[192,384]{1,0:T(8,128)(2,1)} %copy-done.12), custom_call_target="tpu_custom_call" | custom-call | flops 94371840 | bytes 540672 | tf_op jit(solution)/shard_map/project/pallas_call | solution.py:60
  95.8 1.0 add.121
  96.8 6.3 %collective-permute-start.10 = (f32[80,384]{1,0:T(8,128)S(1)}, f32[80,384]{1,0:T(8,128)S(1)}, u32[]{:S(2)}, u32[]{:S(2)}) collective-permute-start(f32[80,384]{1,0:T(8,128)S(1)} %slice_bitcast_fusion), channel_id=1, source_target_pairs={{0,4},{4,0},{1,5},{5,1},{2,6},{6,2},{3,7},{7,3},{8,12},{12,8},{9,1... | collective-permute-start | bytes 368648 | tf_op jit(solution)/shard_map/ppermute | solution.py:28
  104.4 0.8 pad_maximum_fusion.project_ref
  105.2 14.2 %attention.1 = bf16[1024,384]{1,0:T(8,128)(2,1)} custom-call(bf16[4,720,384]{2,1,0:T(8,128)(2,1)} %all-to-all-done.packed_ref, bf16[3,160,256]{2,1,0:T(8,128)(2,1)} %pad_maximum_fusion.project_ref, f32[1,128]{1,0:T(1,128)} %bitcast.73), custom_call_target="tpu_custom_call" | custom-call | flops 2013265920 | bytes 4325376 | tf_op jit(solution)/shard_map/attention/pallas_call | solution.py:197
  119.4 3.6 %all-to-all-start.1 = ((bf16[4,256,384]{2,1,0:T(8,128)(2,1)}), bf16[4,256,384]{2,1,0:T(8,128)(2,1)S(1)}, u32[]{:S(2)}, u32[]{:S(2)}) async-start(bf16[4,256,384]{2,1,0:T(8,128)(2,1)} %bitcast.66), calls=%async_computation.1 | async-start | bytes 1572864 | tf_op jit(solution)/shard_map/all_to_all | solution.py:410
  123.0 1.7 copy.16.gate_ref
  124.7 10.4 %all-to-all-done.1.attended_ref = bf16[4,256,384]{2,1,0:T(8,128)(2,1)S(1)} async-done(((bf16[4,256,384]{2,1,0:T(8,128)(2,1)}), bf16[4,256,384]{2,1,0:T(8,128)(2,1)S(1)}, u32[]{:S(2)}, u32[]{:S(2)}) %all-to-all-start.1) | async-done | bytes 786464 | tf_op jit(solution)/shard_map/all_to_all | solution.py:410
  135.1 0.9 copy-done.2
  136.0 9.9 %finish.1 = f32[64,256]{1,0:T(8,128)} custom-call(bf16[4,256,384]{2,1,0:T(8,128)(2,1)} %copy-done.2, bf16[3072,1536]{1,0:T(8,128)(2,1)} %all-gather.2.cloned.1.call-done.weight_ref, f32[3072,256]{1,0:T(8,128)} %copy-done, f32[3072,1]{1,0:T(8,128)} %copy.16.gate_ref, bf16[64,3072]{1,0:T(8,128)(2,1)} %bitcast.67, f32[1]{0:T(128)} %bitcast.37.delta_ref), custom_call_target="tpu_custom_call" | custom-call | flops 2516582400 | bytes 12582912 | tf_op jit(solution)/shard_map/finish/pallas_call | solution.py:257
  145.9 0.8 convert_element_type.112
  146.8 1.0 collective-permute-start.11
  147.8 0.9 collective-permute-done.11
  148.7 0.8 fusion.13
  149.5 1.3 collective-permute-start.12
  150.8 1.0 collective-permute-done.12
  151.8 0.9 fusion.9
  152.7 3.4 %collective-permute-start.13 = (bf16[64,256]{1,0:T(8,128)(2,1)S(1)}, bf16[64,256]{1,0:T(8,128)(2,1)S(1)}, u32[]{:S(2)}, u32[]{:S(2)}) collective-permute-start(bf16[64,256]{1,0:T(8,128)(2,1)S(1)} %fusion.9), channel_id=1, source_target_pairs={{0,16},{8,24},{16,32},{24,40},{32,48},{40,56},{48,64},{56,72},{64,... | collective-permute-start | bytes 98312 | tf_op jit(solution)/shard_map/ppermute | solution.py:24
  156.1 1.0 collective-permute-done.13
  157.1 0.9 add_convert_fusion
  158.0 7.5 %collective-permute-start.14 = (bf16[64,256]{1,0:T(8,128)(2,1)S(1)}, bf16[64,256]{1,0:T(8,128)(2,1)S(1)}, u32[]{:S(2)}, u32[]{:S(2)}) collective-permute-start(bf16[64,256]{1,0:T(8,128)(2,1)S(1)} %add_convert_fusion), channel_id=1, source_target_pairs={{0,32},{8,40},{16,48},{24,56},{32,64},{40,72},{48,80},{56,88},{64,... | collective-permute-start | bytes 98312 | tf_op jit(solution)/shard_map/ppermute | solution.py:39
  165.5 1.1 collective-permute-done.14
  166.6 0.7 collective-permute-start.15
  167.3 10.7 %collective-permute-start.16 = (bf16[64,256]{1,0:T(8,128)(2,1)S(1)}, bf16[64,256]{1,0:T(8,128)(2,1)S(1)}, u32[]{:S(2)}, u32[]{:S(2)}) collective-permute-start(bf16[64,256]{1,0:T(8,128)(2,1)S(1)} %fusion.10), channel_id=1, source_target_pairs={{0,4},{4,0},{1,5},{5,1},{2,6},{6,2},{3,7},{7,3},{8,12},{12,8},{9,1... | collective-permute-start | bytes 98312 | tf_op jit(solution)/shard_map/ppermute | solution.py:28
  178.0 0.9 collective-permute-done.16
  178.8 1.5 fusion.8
  (65 shorter events, 1.1 us)
Async XLA Ops:
  6.5 128.6 %all-gather.2.cloned.1.call-start = ((), (), s32[]{:S(2)}) async-start(), calls=%async_computation.2 | async-start | bytes 9732096 | tf_op jit(solution)/shard_map/all_gather | solution.py:397
  7.4 21.3 %collective-permute-start = (bf16[96,384]{1,0:T(8,128)(2,1)S(1)}, bf16[96,384]{1,0:T(8,128)(2,1)S(1)}, u32[]{:S(2)}, u32[]{:S(2)}) collective-permute-start(bf16[96,384]{1,0:T(8,128)(2,1)S(1)} %constant_dynamic-slice_fusion), channel_id=1, source_target_pairs={{0,4},{4,0},{1,5},{5,1},{2,6},{6,2},{3,7},{7,3},{8,12},{12,8},{9,1... | collective-permute-start | bytes 221192 | tf_op jit(solution)/shard_map/ppermute | solution.py:28
  29.7 5.5 %copy-start.4 = (bf16[192,384]{1,0:T(8,128)(2,1)}, bf16[192,384]{1,0:T(8,128)(2,1)S(1)}, u32[]{:S(2)}) copy-start(bf16[192,384]{1,0:T(8,128)(2,1)S(1)} %pad_maximum_fusion.1.refs_0_) | copy-start | bytes 442372
  29.7 6.5 %collective-permute-start.1 = (bf16[192,384]{1,0:T(8,128)(2,1)S(1)}, bf16[192,384]{1,0:T(8,128)(2,1)S(1)}, u32[]{:S(2)}, u32[]{:S(2)}) collective-permute-start(bf16[192,384]{1,0:T(8,128)(2,1)S(1)} %pad_maximum_fusion.1.refs_0_), channel_id=1, source_target_pairs={{0,8},{8,16},{16,24},{24,32},{32,40},{40,48},{48,56},{56,64},{64,7... | collective-permute-start | bytes 442376 | tf_op jit(solution)/shard_map/ppermute | solution.py:39
  34.8 7.3 %copy-start = (f32[3072,256]{1,0:T(8,128)}, f32[3072,256]{1,0:T(8,128)S(1)}, u32[]{:S(2)}) copy-start(f32[3072,256]{1,0:T(8,128)S(1)} %get-tuple-element.98.hidden_ref) | copy-start | bytes 9437188
  36.2 6.0 %copy-start.5 = (bf16[192,384]{1,0:T(8,128)(2,1)}, bf16[192,384]{1,0:T(8,128)(2,1)S(1)}, u32[]{:S(2)}) copy-start(bf16[192,384]{1,0:T(8,128)(2,1)S(1)} %collective-permute-done.1.refs_1_) | copy-start | bytes 442372
  36.2 5.9 %collective-permute-start.2 = (bf16[192,384]{1,0:T(8,128)(2,1)S(1)}, bf16[192,384]{1,0:T(8,128)(2,1)S(1)}, u32[]{:S(2)}, u32[]{:S(2)}) collective-permute-start(bf16[192,384]{1,0:T(8,128)(2,1)S(1)} %collective-permute-done.1.refs_1_), channel_id=1, source_target_pairs={{0,8},{8,16},{16,24},{24,32},{32,40},{40,48},{48,56},{56,64},{64,7... | collective-permute-start | bytes 442376 | tf_op jit(solution)/shard_map/ppermute | solution.py:39
  38.2 6.0 %copy-start.15 = (f32[1000]{0:T(1024)S(1)}, f32[1000]{0:T(1024)}, u32[]{:S(2)}) copy-start(f32[1000]{0:T(1024)} %param.16) | copy-start | bytes 12004
  42.1 12.1 %copy-start.6 = (bf16[192,384]{1,0:T(8,128)(2,1)}, bf16[192,384]{1,0:T(8,128)(2,1)S(1)}, u32[]{:S(2)}) copy-start(bf16[192,384]{1,0:T(8,128)(2,1)S(1)} %collective-permute-done.2.refs_2_) | copy-start | bytes 442372
  42.2 5.1 %collective-permute-start.3 = (bf16[192,384]{1,0:T(8,128)(2,1)S(1)}, bf16[192,384]{1,0:T(8,128)(2,1)S(1)}, u32[]{:S(2)}, u32[]{:S(2)}) collective-permute-start(bf16[192,384]{1,0:T(8,128)(2,1)S(1)} %collective-permute-done.2.refs_2_), channel_id=1, source_target_pairs={{0,8},{8,16},{16,24},{24,32},{32,40},{40,48},{48,56},{56,64},{64,7... | collective-permute-start | bytes 442376 | tf_op jit(solution)/shard_map/ppermute | solution.py:39
  45.5 1.3 collective-permute-start.5
  47.3 6.9 %copy-start.7 = (bf16[192,384]{1,0:T(8,128)(2,1)}, bf16[192,384]{1,0:T(8,128)(2,1)S(1)}, u32[]{:S(2)}) copy-start(bf16[192,384]{1,0:T(8,128)(2,1)S(1)} %collective-permute-done.3.refs_3_) | copy-start | bytes 442372
  48.6 6.7 %collective-permute-start.4 = (bf16[192,384]{1,0:T(8,128)(2,1)S(1)}, bf16[192,384]{1,0:T(8,128)(2,1)S(1)}, u32[]{:S(2)}, u32[]{:S(2)}) collective-permute-start(bf16[192,384]{1,0:T(8,128)(2,1)S(1)} %collective-permute-done.3.refs_3_), channel_id=1, source_target_pairs={{0,8},{8,16},{16,24},{24,32},{32,40},{40,48},{48,56},{56,64},{64,7... | collective-permute-start | bytes 442376 | tf_op jit(solution)/shard_map/ppermute | solution.py:39
  55.3 3.6 %copy-start.8 = (bf16[192,384]{1,0:T(8,128)(2,1)}, bf16[192,384]{1,0:T(8,128)(2,1)S(1)}, u32[]{:S(2)}) copy-start(bf16[192,384]{1,0:T(8,128)(2,1)S(1)} %collective-permute-done.4.refs_4_) | copy-start | bytes 442372
  55.3 8.5 %collective-permute-start.6 = (bf16[192,384]{1,0:T(8,128)(2,1)S(1)}, bf16[192,384]{1,0:T(8,128)(2,1)S(1)}, u32[]{:S(2)}, u32[]{:S(2)}) collective-permute-start(bf16[192,384]{1,0:T(8,128)(2,1)S(1)} %collective-permute-done.4.refs_4_), channel_id=1, source_target_pairs={{0,8},{8,16},{16,24},{24,32},{32,40},{40,48},{48,56},{56,64},{64,7... | collective-permute-start | bytes 442376 | tf_op jit(solution)/shard_map/ppermute | solution.py:39
  58.9 4.9 %copy-start.1 = (bf16[64,3072]{1,0:T(8,128)(2,1)S(1)}, bf16[64,3072]{1,0:T(8,128)(2,1)}, u32[]{:S(2)}) copy-start(bf16[64,3072]{1,0:T(8,128)(2,1)} %param.18) | copy-start | bytes 1179652
  58.9 46.3 %all-to-all-start = ((bf16[4,720,384]{2,1,0:T(8,128)(2,1)}), bf16[4,720,384]{2,1,0:T(8,128)(2,1)}, u32[]{:S(2)}, u32[]{:S(2)}) async-start(bf16[4,720,384]{2,1,0:T(8,128)(2,1)} %pack.1), calls=%async_computation | async-start | bytes 4423680 | tf_op jit(solution)/shard_map/all_to_all | solution.py:395
  63.8 3.6 %copy-start.9 = (bf16[192,384]{1,0:T(8,128)(2,1)}, bf16[192,384]{1,0:T(8,128)(2,1)S(1)}, u32[]{:S(2)}) copy-start(bf16[192,384]{1,0:T(8,128)(2,1)S(1)} %collective-permute-done.6.refs_5_) | copy-start | bytes 442372
  64.1 1.5 copy-start.13
  67.5 8.9 %collective-permute-start.7 = (bf16[192,384]{1,0:T(8,128)(2,1)S(1)}, bf16[192,384]{1,0:T(8,128)(2,1)S(1)}, u32[]{:S(2)}, u32[]{:S(2)}) collective-permute-start(bf16[192,384]{1,0:T(8,128)(2,1)S(1)} %collective-permute-done.6.refs_5_), channel_id=1, source_target_pairs={{0,8},{8,16},{16,24},{24,32},{32,40},{40,48},{48,56},{56,64},{64,7... | collective-permute-start | bytes 442376 | tf_op jit(solution)/shard_map/ppermute | solution.py:39
  76.3 12.3 %copy-start.10 = (bf16[192,384]{1,0:T(8,128)(2,1)}, bf16[192,384]{1,0:T(8,128)(2,1)S(1)}, u32[]{:S(2)}) copy-start(bf16[192,384]{1,0:T(8,128)(2,1)S(1)} %collective-permute-done.7.refs_6_) | copy-start | bytes 442372
  76.3 7.6 %collective-permute-start.8 = (bf16[192,384]{1,0:T(8,128)(2,1)S(1)}, bf16[192,384]{1,0:T(8,128)(2,1)S(1)}, u32[]{:S(2)}, u32[]{:S(2)}) collective-permute-start(bf16[192,384]{1,0:T(8,128)(2,1)S(1)} %collective-permute-done.7.refs_6_), channel_id=1, source_target_pairs={{0,8},{8,16},{16,24},{24,32},{32,40},{40,48},{48,56},{56,64},{64,7... | collective-permute-start | bytes 442376 | tf_op jit(solution)/shard_map/ppermute | solution.py:39
  83.9 8.3 %copy-start.11 = (bf16[192,384]{1,0:T(8,128)(2,1)}, bf16[192,384]{1,0:T(8,128)(2,1)S(1)}, u32[]{:S(2)}) copy-start(bf16[192,384]{1,0:T(8,128)(2,1)S(1)} %collective-permute-done.8.refs_0_) | copy-start | bytes 442372
  83.9 8.3 %collective-permute-start.9 = (bf16[192,384]{1,0:T(8,128)(2,1)S(1)}, bf16[192,384]{1,0:T(8,128)(2,1)S(1)}, u32[]{:S(2)}, u32[]{:S(2)}) collective-permute-start(bf16[192,384]{1,0:T(8,128)(2,1)S(1)} %collective-permute-done.8.refs_0_), channel_id=1, source_target_pairs={{0,8},{8,16},{16,24},{24,32},{32,40},{40,48},{48,56},{56,64},{64,7... | collective-permute-start | bytes 442376 | tf_op jit(solution)/shard_map/ppermute | solution.py:39
  92.2 3.6 %copy-start.3 = (f32[2,80,384]{2,1,0:T(8,128)S(1)}, f32[2,80,384]{2,1,0:T(8,128)}, u32[]{:S(2)}) copy-start(f32[2,80,384]{2,1,0:T(8,128)} %project.2) | copy-start | bytes 737284
  92.3 0.7 copy-start.12
  96.8 7.4 %collective-permute-start.10 = (f32[80,384]{1,0:T(8,128)S(1)}, f32[80,384]{1,0:T(8,128)S(1)}, u32[]{:S(2)}, u32[]{:S(2)}) collective-permute-start(f32[80,384]{1,0:T(8,128)S(1)} %slice_bitcast_fusion), channel_id=1, source_target_pairs={{0,4},{4,0},{1,5},{5,1},{2,6},{6,2},{3,7},{7,3},{8,12},{12,8},{9,1... | collective-permute-start | bytes 368648 | tf_op jit(solution)/shard_map/ppermute | solution.py:28
  119.4 15.7 %all-to-all-start.1 = ((bf16[4,256,384]{2,1,0:T(8,128)(2,1)}), bf16[4,256,384]{2,1,0:T(8,128)(2,1)S(1)}, u32[]{:S(2)}, u32[]{:S(2)}) async-start(bf16[4,256,384]{2,1,0:T(8,128)(2,1)} %bitcast.66), calls=%async_computation.1 | async-start | bytes 1572864 | tf_op jit(solution)/shard_map/all_to_all | solution.py:410
  135.1 0.9 copy-start.2
  136.0 42.8 %copy-start.14 = (f32[256,64]{0,1:T(8,128)S(1)}, f32[256,64]{0,1:T(8,128)}, u32[]{:S(2)}) copy-start(f32[256,64]{0,1:T(8,128)} %param.14) | copy-start | bytes 196612
  146.8 1.9 %collective-permute-start.11 = (bf16[64,256]{1,0:T(8,128)(2,1)S(1)}, bf16[64,256]{1,0:T(8,128)(2,1)S(1)}, u32[]{:S(2)}, u32[]{:S(2)}) collective-permute-start(bf16[64,256]{1,0:T(8,128)(2,1)S(1)} %convert_element_type.112), channel_id=1, source_target_pairs={{0,4},{4,0},{1,5},{5,1},{2,6},{6,2},{3,7},{7,3},{8,12},{12,8},{9,1... | collective-permute-start | bytes 98312 | tf_op jit(solution)/shard_map/ppermute | solution.py:28
  149.5 2.3 %collective-permute-start.12 = (bf16[64,256]{1,0:T(8,128)(2,1)S(1)}, bf16[64,256]{1,0:T(8,128)(2,1)S(1)}, u32[]{:S(2)}, u32[]{:S(2)}) collective-permute-start(bf16[64,256]{1,0:T(8,128)(2,1)S(1)} %fusion.13), channel_id=1, source_target_pairs={{0,8},{8,16},{16,24},{24,32},{32,40},{40,48},{48,56},{56,64},{64,7... | collective-permute-start | bytes 98312 | tf_op jit(solution)/shard_map/ppermute | solution.py:24
  152.7 4.4 %collective-permute-start.13 = (bf16[64,256]{1,0:T(8,128)(2,1)S(1)}, bf16[64,256]{1,0:T(8,128)(2,1)S(1)}, u32[]{:S(2)}, u32[]{:S(2)}) collective-permute-start(bf16[64,256]{1,0:T(8,128)(2,1)S(1)} %fusion.9), channel_id=1, source_target_pairs={{0,16},{8,24},{16,32},{24,40},{32,48},{40,56},{48,64},{56,72},{64,... | collective-permute-start | bytes 98312 | tf_op jit(solution)/shard_map/ppermute | solution.py:24
  158.0 8.6 %collective-permute-start.14 = (bf16[64,256]{1,0:T(8,128)(2,1)S(1)}, bf16[64,256]{1,0:T(8,128)(2,1)S(1)}, u32[]{:S(2)}, u32[]{:S(2)}) collective-permute-start(bf16[64,256]{1,0:T(8,128)(2,1)S(1)} %add_convert_fusion), channel_id=1, source_target_pairs={{0,32},{8,40},{16,48},{24,56},{32,64},{40,72},{48,80},{56,88},{64,... | collective-permute-start | bytes 98312 | tf_op jit(solution)/shard_map/ppermute | solution.py:39
  166.6 0.7 collective-permute-start.15
  167.3 11.6 %collective-permute-start.16 = (bf16[64,256]{1,0:T(8,128)(2,1)S(1)}, bf16[64,256]{1,0:T(8,128)(2,1)S(1)}, u32[]{:S(2)}, u32[]{:S(2)}) collective-permute-start(bf16[64,256]{1,0:T(8,128)(2,1)S(1)} %fusion.10), channel_id=1, source_target_pairs={{0,4},{4,0},{1,5},{5,1},{2,6},{6,2},{3,7},{7,3},{8,12},{12,8},{9,1... | collective-permute-start | bytes 98312 | tf_op jit(solution)/shard_map/ppermute | solution.py:28
Sparse Core Ops, SparseCore 0:
  42.3 76.8 all-gather.1

commit v5 on v2

--- a/solution.py
+++ b/solution.py
@@ -124,47 +124,32 @@
     )(keys, values, latent, spread)
 
 
-def attention_body(parts, rows, packed_ref, project_ref, gain_ref, out_ref, even_ref, odd_ref):
-    at, last = pl.program_id(0), pl.num_programs(0) - 2
-    now, past = jnp.minimum(at, last), jnp.maximum(at - 1, 0)
-    tile = even_ref.shape[0]
-    head, part = now // parts, lax.rem(now, parts)
-
-    def columns(head):
-        return pl.ds(pl.multiple_of(head * HEAD, HEAD), HEAD)
-
-    def run(now_ref, past_ref):
+def attention_body(parts, rows, tile, packed_ref, project_ref, gain_ref, out_ref):
+    columns = pl.ds(pl.multiple_of(pl.program_id(0) * HEAD, HEAD), HEAD)
+    keys = packed_ref[:, :rows, columns].reshape(-1, HEAD)
+    values = packed_ref[:, rows : 2 * rows, columns].reshape(-1, HEAD)
+    queries = []
+    for part in range(parts):
         tokens = packed_ref[part, 2 * rows :, :tile]
         both = lax.dot_general(
             jnp.concatenate([tokens, tokens]),
-            project_ref[head],
+            project_ref[0],
             (((0,), (0,)), ((), ())),
             preferred_element_type=jnp.float32,
         )
         raw, spread = both[:, :HEAD], both[:, HEAD:]
         square = jnp.mean(raw * raw, axis=-1, keepdims=True) + epsilon * (spread * spread)
-        queries = (raw * lax.rsqrt(square) * gain_ref[...]).astype(jnp.bfloat16)
-        for p in range(parts):
-            now_ref[:, p * rows : (p + 1) * rows] = lax.dot_general(
-                queries,
-                packed_ref[p, :rows, columns(head)],
-                (((1,), (1,)), ((), ())),
-                preferred_element_type=jnp.float32,
-            )
-        peak = jnp.max(past_ref[...], axis=-1, keepdims=True)
-        weights = jnp.exp((past_ref[...] - peak) * (1.0 / math.sqrt(HEAD)))
+        queries.append((raw * lax.rsqrt(square) * gain_ref[...]).astype(jnp.bfloat16))
+    scores = [
+        lax.dot_general(q, keys, (((1,), (1,)), ((), ())), preferred_element_type=jnp.float32)
+        for q in queries
+    ]
+    for part in range(parts):
+        peak = jnp.max(scores[part], axis=-1, keepdims=True)
+        weights = jnp.exp((scores[part] - peak) * (1.0 / math.sqrt(HEAD)))
         total = jnp.sum(weights, axis=-1, keepdims=True)
-        values = packed_ref[:, rows : 2 * rows, columns(past // parts)].reshape(-1, HEAD)
         blended = jnp.dot(weights.astype(jnp.bfloat16), values, preferred_element_type=jnp.float32)
-        out_ref[...] = (blended / total).astype(jnp.bfloat16)
-
-    @pl.when(lax.rem(at, 2) == 0)
-    def _():
-        run(even_ref, odd_ref)
-
-    @pl.when(lax.rem(at, 2) == 1)
-    def _():
-        run(odd_ref, even_ref)
+        out_ref[part] = (blended / total).astype(jnp.bfloat16)
 
 
 def attention(project, query_gain, packed, rows, tile):
@@ -172,19 +157,13 @@
     tokens = parts * tile
     heads = width // HEAD
     work = tokens * parts * rows * width
-
-    def past(i):
-        at = jnp.maximum(i - 1, 0)
-        return lax.rem(at, parts), at // parts
-
     whole = pl.BlockSpec(memory_space=pltpu.VMEM)
     return pl.pallas_call(
-        functools.partial(attention_body, parts, rows),
-        grid=(heads * parts + 1,),
-        in_specs=[whole, whole, whole],
-        out_specs=pl.BlockSpec((tile, HEAD), past),
-        out_shape=jax.ShapeDtypeStruct((tokens, width), jnp.bfloat16),
-        scratch_shapes=[pltpu.VMEM((tile, parts * rows), jnp.float32)] * 2,
+        functools.partial(attention_body, parts, rows, tile),
+        grid=(heads,),
+        in_specs=[whole, pl.BlockSpec((1, *project.shape[1:]), lambda h: (h, 0, 0)), whole],
+        out_specs=pl.BlockSpec((parts, tile, HEAD), lambda h: (0, 0, h)),
+        out_shape=jax.ShapeDtypeStruct((parts, tile, width), jnp.bfloat16),
         cost_estimate=pl.CostEstimate(
             flops=4 * work,
             bytes_accessed=4 * parts * rows * width + 6 * tokens * width,
@@ -192,79 +171,6 @@
         ),
         name="attention",
     )(packed, project, query_gain.reshape(1, HEAD))
-
-
-def finish_body(
-    tile, attended_ref, weight_ref, hidden_ref, gate_ref, final_ref, out_ref, joined_ref, mixed_ref, sum_ref
-):
-    at = pl.program_id(0)
-    parts, tokens, columns = attended_ref.shape
-
-    @pl.when(at == 0)
-    def _():
-        for p in range(parts):
-            joined_ref[:, p * columns : (p + 1) * columns] = attended_ref[p]
-        sum_ref[...] = jnp.zeros_like(sum_ref)
-
-    branch = lax.dot_general(
-        joined_ref[...], weight_ref[...], (((1,), (1,)), ((), ())), preferred_element_type=jnp.float32
-    )
-    mixed = hidden_ref[:, pl.ds(pl.multiple_of(at * tile, tile), tile)] + gate_ref[...] * branch
-    mixed_ref[at] = mixed
-    sum_ref[...] += jnp.sum(mixed, axis=-1, keepdims=True)
-
-    @pl.when(at == pl.num_programs(0) - 1)
-    def _():
-        count = mixed_ref.shape[0]
-        width = count * tile
-        mean = sum_ref[...] / width
-        squares = functools.reduce(
-            lambda a, b: a + b, [jnp.square(mixed_ref[i] - mean) for i in range(count)]
-        )
-        scale = lax.rsqrt(jnp.sum(squares, axis=-1, keepdims=True) / width + epsilon)
-        out_ref[...] = functools.reduce(
-            lambda a, b: a + b,
-            [
-                lax.dot_general(
-                    final_ref[:, i * tile : (i + 1) * tile],
-                    ((mixed_ref[i] - mean) * scale).astype(jnp.bfloat16),
-                    (((1,), (1,)), ((), ())),
-                    preferred_element_type=jnp.float32,
-                )
-                for i in range(count)
-            ],
-        )
-
-
-def finish(attended, out_weight, hidden, gate, final_weight):
-    parts, tokens, columns = attended.shape
-    width, depth = out_weight.shape
-    channels = final_weight.shape[1]
-    tile = min(512, width)
-    return pl.pallas_call(
-        functools.partial(finish_body, tile),
-        grid=(width // tile,),
-        in_specs=[
-            pl.BlockSpec(memory_space=pltpu.VMEM),
-            pl.BlockSpec((tile, depth), lambda i: (i, 0)),
-            pl.BlockSpec(memory_space=pltpu.VMEM),
-            pl.BlockSpec((1, tile), lambda i: (0, i)),
-            pl.BlockSpec((channels, width), lambda i: (0, 0)),
-        ],
-        out_specs=pl.BlockSpec((channels, tokens), lambda i: (0, 0)),
-        out_shape=jax.ShapeDtypeStruct((channels, tokens), jnp.float32),
-        scratch_shapes=[
-            pltpu.VMEM((tokens, depth), jnp.bfloat16),
-            pltpu.VMEM((width // tile, tokens, tile), jnp.float32),
-            pltpu.VMEM((tokens, 1), jnp.float32),
-        ],
-        cost_estimate=pl.CostEstimate(
-            flops=2 * tokens * width * (depth + channels),
-            bytes_accessed=2 * width * depth + 4 * tokens * width,
-            transcendentals=0,
-        ),
-        name="finish",
-    )(attended, out_weight, hidden, gate.reshape(1, width), final_weight.T)
 
 
 def prefix_over_steps(drift):
@@ -373,10 +279,18 @@
     project = jnp.concatenate([project, jnp.broadcast_to(picks, project.shape)], axis=2)
 
     attended = attention(project, query_gain, packed, key_rows, token_count)
-    attended = lax.all_to_all(
-        attended.reshape(parts, token_count, columns), "patch", 0, 0, tiled=True
-    )
-    velocity = finish(attended, all_out_weight, hidden, modulate[2 * width :], final_weight)
+    attended = lax.all_to_all(attended, "patch", 0, 0, tiled=True)
+    attended = jnp.moveaxis(attended, 0, 1).reshape(token_count, -1)
+    branch = lax.dot_general(
+        attended, all_out_weight, (((1,), (1,)), ((), ())), preferred_element_type=jnp.float32
+    )
+    mixed = hidden + modulate[2 * width :] * branch
+    centered = mixed - jnp.mean(mixed, axis=-1, keepdims=True)
+    variance = jnp.mean(jnp.square(centered), axis=-1, keepdims=True)
+    normed = (centered * lax.rsqrt(variance + epsilon)).astype(jnp.bfloat16)
+    velocity = lax.dot_general(
+        final_weight, normed, (((0,), (1,)), ((), ())), preferred_element_type=jnp.float32
+    )
     drift = velocity * delta
     return (noise_start.T + (prefix_over_steps(drift) + drift)).T[None]
 

time: 186 us -> 186 us (level)
  local copies, waits for them, and re-layouts: 7.02 us -> 24.1 us
  Pallas kernels: 28.7 us -> 13.8 us
  matrix products: 5.52 us -> 14 us
  starting transfers between devices: 84.2 us -> 76.6 us
  waiting for transfers between devices: 31.1 us -> 25.8 us
  other arithmetic: 11.1 us -> 13.8 us
    pallas_call x2 -> x1, Pallas kernels: 24.8 us -> 9.9 us  [attention(): pl.pallas_call(functools.partial(attention_body, parts, rows, tile), grid...]
    dynamic_update_slice x15, local copies, waits for them, and re-layouts: 4.07 us -> 18.3 us  [gather_rows(): held = lax.dynamic_update_slice_in_dim(held, piece[None], owner, 0)]
    ppermute x10, starting transfers between devices: 34.8 us -> 26.1 us  [send_by_core(): return lax.ppermute(value, ('chip', 'core'), pairs)]
    ppermute x10, waiting for transfers between devices: 17.3 us -> 10.2 us  [send_by_core(): return lax.ppermute(value, ('chip', 'core'), pairs)]
    dot_general x0 -> x2, matrix products: none -> 6.16 us  [the longest x1 5.47 us: per_device(): lax.dot_general(attended, all_out_weight, (((1,), (1,)), ((), ())), prefe...]
    transpose x0 -> x1, local copies, waits for them, and re-layouts: none -> 2.29 us  [per_device(): attended = jnp.moveaxis(attended, 0, 1).reshape(token_count, -1)]
    concatenate x2, other arithmetic: 0.93 us -> 2.96 us  [gather_rows(): swapped = swap_cores(jnp.concatenate([p for _, p in waiting]))]
    all_to_all x1, waiting for transfers between devices: 9.23 us -> 11.1 us  [per_device(): attended = lax.all_to_all(attended, 'patch', 0, 0, tiled=True)]
  transfers between devices with their start and end apart: 20 -> 20, of which waited for: 14 -> 11; matrix products, arithmetic and copies ran while one was open for 10% -> 24% of each run, Pallas kernels for 10% -> 7%
where the time goes in v5:
time: 186 us; the launch traced here: 185 us
  starting transfers between devices  76.6 us (41%)
  waiting for transfers between devices  25.8 us (14%)
  local copies, waits for them, and re-layouts  24.1 us (13%)
  between operations  16.8 us (9%)
  matrix products  14 us (8%)
  other arithmetic  13.8 us (7%)
  Pallas kernels  13.8 us (7%)
    ppermute x5, starting transfers between devices, swap_cores(): return lax.ppermute(value, 'core', [(0, 1), (1, 0)])  35 us
    ppermute x10, starting transfers between devices, send_by_core(): return lax.ppermute(value, ('chip', 'core'), pairs)  26.1 us
    dynamic_update_slice x15, local copies, waits for them, and re-layouts, gather_rows(): held = lax.dynamic_update_slice_in_dim(held, piece[None], owner, 0)  18.3 us
    all_to_all x1, waiting for transfers between devices, per_device(): attended = lax.all_to_all(attended, 'patch', 0, 0, tiled=True)  11.1 us
    ppermute x10, waiting for transfers between devices, send_by_core(): return lax.ppermute(value, ('chip', 'core'), pairs)  10.2 us
    pallas_call x1, Pallas kernels, attention(): pl.pallas_call(functools.partial(attention_body, parts, rows, tile), grid...  9.9 us
    ppermute x2, starting transfers between devices, shift(): return lax.ppermute(value, axis, pairs)  5.87 us
    dot_general x1, matrix products, per_device(): lax.dot_general(attended, all_out_weight, (((1,), (1,)), ((), ())), prefe...  5.47 us
  transfers between devices with their start and end apart: 20, of which 11 were waited for; matrix products, arithmetic and copies ran while one was open for 24% of the time, Pallas kernels for 7%

profile of v5, /device:TPU:33, one launch (start us, length us, event | category | flops | bytes accessed | tf_op | source)
XLA Modules:
  0.0 184.9 jit_solution(2953290017318849286)
XLA Ops:
  6.6 0.7 all-gather.2.cloned.1.call-update
  7.3 0.9 constant_dynamic-slice_fusion
  8.2 20.4 %collective-permute-start = (bf16[96,384]{1,0:T(8,128)(2,1)S(1)}, bf16[96,384]{1,0:T(8,128)(2,1)S(1)}, u32[]{:S(2)}, u32[]{:S(2)}) collective-permute-start(bf16[96,384]{1,0:T(8,128)(2,1)S(1)} %constant_dynamic-slice_fusion), channel_id=1, source_target_pairs={{0,4},{4,0},{1,5},{5,1},{2,6},{6,2},{3,7},{7,3},{8,12},{12,8},{9,1... | collective-permute-start | bytes 221192 | tf_op jit(solution)/shard_map/ppermute | solution.py:27
  29.9 0.9 broadcast_select_fusion.1
  30.9 3.2 %collective-permute-start.1 = (bf16[192,384]{1,0:T(8,128)(2,1)S(1)}, bf16[192,384]{1,0:T(8,128)(2,1)}, u32[]{:S(2)}, u32[]{:S(2)}) collective-permute-start(bf16[192,384]{1,0:T(8,128)(2,1)S(1)} %pad_maximum_fusion.4), channel_id=1, source_target_pairs={{0,8},{8,16},{16,24},{24,32},{32,40},{40,48},{48,56},{56,64},{64,7... | collective-permute-start | bytes 442376 | tf_op jit(solution)/shard_map/ppermute | solution.py:38
  34.1 1.7 fusion.28
  36.8 1.7 broadcast_in_dim.98
  38.5 0.7 bitcast_dynamic-update-slice_fusion.8
  39.4 3.9 %pack.1 = bf16[4,720,384]{2,1,0:T(8,128)(2,1)} custom-call(bf16[320,1536]{1,0:T(8,128)(2,1)} %bitcast.93, bf16[320,1536]{1,0:T(8,128)(2,1)} %bitcast.94, f32[64,256]{1,0:T(8,128)} %bitcast.97, f32[1,256]{1,0:T(1,128)} %bitcast.103), custom_call_target="tpu_custom_call" | custom-call | flops 1105920 | bytes 4423680 | tf_op jit(solution)/shard_map/pack/pallas_call | solution.py:107
  43.3 1.6 bitcast_dynamic-update-slice_fusion.7
  44.9 1.9 %collective-permute-done.2 = bf16[192,384]{1,0:T(8,128)(2,1)} collective-permute-done((bf16[192,384]{1,0:T(8,128)(2,1)}, bf16[192,384]{1,0:T(8,128)(2,1)}, u32[]{:S(2)}, u32[]{:S(2)}) %collective-permute-start.2) | collective-permute-done | bytes 147488 | tf_op jit(solution)/shard_map/ppermute | solution.py:38
  46.9 4.5 %all-to-all-start = ((bf16[4,720,384]{2,1,0:T(8,128)(2,1)}), bf16[4,720,384]{2,1,0:T(8,128)(2,1)}, u32[]{:S(2)}, u32[]{:S(2)}) async-start(bf16[4,720,384]{2,1,0:T(8,128)(2,1)} %pack.1), calls=%async_computation | async-start | bytes 4423680 | tf_op jit(solution)/shard_map/all_to_all | solution.py:271
  51.4 1.6 bitcast_dynamic-update-slice_fusion.6
  53.0 0.7 select_reduce_fusion
  54.3 2.8 %collective-permute-start.4 = (bf16[192,384]{1,0:T(8,128)(2,1)}, bf16[192,384]{1,0:T(8,128)(2,1)}, u32[]{:S(2)}, u32[]{:S(2)}) collective-permute-start(bf16[192,384]{1,0:T(8,128)(2,1)} %collective-permute-done.3), channel_id=1, source_target_pairs={{0,8},{8,16},{16,24},{24,32},{32,40},{40,48},{48,56},{56,64},{64,7... | collective-permute-start | bytes 442376 | tf_op jit(solution)/shard_map/ppermute | solution.py:38
  57.1 3.8 %fusion.29 = f32[1,9216]{1,0:T(1,128)} fusion(bf16[256,1]{0,1:T(2,128)(2,1)S(1)} %reshape.77, bf16[256,9216]{1,0:T(8,128)(2,1)} %param.17), kind=kOutput, calls=%fused_computation.88 | convolution fusion | flops 4718592 | bytes 4755968 | tf_op jit(solution)/shard_map/dot_general | solution.py:235
  62.3 3.4 %collective-permute-start.5 = (bf16[192,384]{1,0:T(8,128)(2,1)}, bf16[192,384]{1,0:T(8,128)(2,1)}, u32[]{:S(2)}, u32[]{:S(2)}) collective-permute-start(bf16[192,384]{1,0:T(8,128)(2,1)} %collective-permute-done.4), channel_id=1, source_target_pairs={{0,8},{8,16},{16,24},{24,32},{32,40},{40,48},{48,56},{56,64},{64,7... | collective-permute-start | bytes 442376 | tf_op jit(solution)/shard_map/ppermute | solution.py:38
  65.8 1.6 bitcast_dynamic-update-slice_fusion.5
  67.4 2.0 %pad_maximum_fusion.1 = bf16[768,384]{1,0:T(8,128)(2,1)} fusion(bf16[192,384]{1,0:T(8,128)(2,1)} %collective-permute-done.4, bf16[192,384]{1,0:T(8,128)(2,1)} %collective-permute-done.3, bf16[192,384]{1,0:T(8,128)(2,1)} %collective-permute-done.2, bf16[192,384]{1,0:T(8,128)(2,1)} %collective-permute-done.1), kind=kLoop, calls=%fused_computation.15 | loop fusion | flops 2359296 | bytes 1179648 | tf_op jit(solution)/shard_map/concatenate | solution.py:63
  69.4 1.6 collective-permute-done.5
  71.0 0.7 reduce_sum.77
  72.3 3.5 %collective-permute-start.6 = (bf16[192,384]{1,0:T(8,128)(2,1)}, bf16[192,384]{1,0:T(8,128)(2,1)S(1)}, u32[]{:S(2)}, u32[]{:S(2)}) collective-permute-start(bf16[192,384]{1,0:T(8,128)(2,1)} %collective-permute-done.5), channel_id=1, source_target_pairs={{0,8},{8,16},{16,24},{24,32},{32,40},{40,48},{48,56},{56,64},{64,7... | collective-permute-start | bytes 442376 | tf_op jit(solution)/shard_map/ppermute | solution.py:38
  75.8 1.2 convert_reduce_fusion
  77.0 0.7 slice_add_fusion.1
  77.8 1.1 convert_subtract_fusion
  79.3 2.0 %collective-permute-done.6 = bf16[192,384]{1,0:T(8,128)(2,1)S(1)} collective-permute-done((bf16[192,384]{1,0:T(8,128)(2,1)}, bf16[192,384]{1,0:T(8,128)(2,1)S(1)}, u32[]{:S(2)}, u32[]{:S(2)}) %collective-permute-start.6) | collective-permute-done | bytes 147488 | tf_op jit(solution)/shard_map/ppermute | solution.py:38
  81.3 3.4 %collective-permute-start.8 = (bf16[192,384]{1,0:T(8,128)(2,1)S(1)}, bf16[192,384]{1,0:T(8,128)(2,1)S(1)}, u32[]{:S(2)}, u32[]{:S(2)}) collective-permute-start(bf16[192,384]{1,0:T(8,128)(2,1)S(1)} %collective-permute-done.6), channel_id=1, source_target_pairs={{0,8},{8,16},{16,24},{24,32},{32,40},{40,48},{48,56},{56,64},{64,7... | collective-permute-start | bytes 442376 | tf_op jit(solution)/shard_map/ppermute | solution.py:38
  84.8 1.6 bitcast_dynamic-update-slice_fusion.4
  86.3 3.4 %collective-permute-done.8 = bf16[192,384]{1,0:T(8,128)(2,1)S(1)} collective-permute-done((bf16[192,384]{1,0:T(8,128)(2,1)S(1)}, bf16[192,384]{1,0:T(8,128)(2,1)S(1)}, u32[]{:S(2)}, u32[]{:S(2)}) %collective-permute-start.8) | collective-permute-done | bytes 147488 | tf_op jit(solution)/shard_map/ppermute | solution.py:38
  89.8 1.0 pad_maximum_fusion.2
  90.7 4.3 %collective-permute-start.9 = (bf16[576,384]{1,0:T(8,128)(2,1)S(1)}, bf16[576,384]{1,0:T(8,128)(2,1)S(1)}, u32[]{:S(2)}, u32[]{:S(2)}) collective-permute-start(bf16[576,384]{1,0:T(8,128)(2,1)S(1)} %pad_maximum_fusion.2), channel_id=1, source_target_pairs={{0,4},{4,0},{1,5},{5,1},{2,6},{6,2},{3,7},{7,3},{8,12},{12,8},{9,1... | collective-permute-start | bytes 1327112 | tf_op jit(solution)/shard_map/ppermute | solution.py:27
  95.1 1.6 fusion.10
  96.7 1.6 fusion.9
  98.2 1.6 fusion.8
  99.8 1.6 fusion.7
  101.4 1.6 bitcast_dynamic-update-slice_fusion.3
  103.0 0.7 bitcast_dynamic-update-slice_fusion.2
  103.7 0.7 bitcast_dynamic-update-slice_fusion.1
  104.3 0.7 fusion.6
  105.0 0.7 fusion.5
  105.7 0.7 fusion.4
  106.4 0.7 bitcast_dynamic-update-slice_fusion
  107.1 2.4 %fusion.30 = f32[160,384]{1,0:T(8,128)S(1)} fusion(bf16[160,3072]{1,0:T(8,128)(2,1)S(1)} %pad_maximum_fusion, bf16[3072,384]{1,0:T(8,128)(2,1)} %bitcast.27), kind=kOutput, calls=%fused_computation.89 | convolution fusion | flops 377487360 | bytes 3588096 | tf_op jit(solution)/shard_map/dot_general | solution.py:273
  109.6 0.8 pad_maximum_fusion.3.project_ref
  110.4 9.9 %attention.1 = bf16[4,256,384]{2,1,0:T(8,128)(2,1)} custom-call(bf16[4,720,384]{2,1,0:T(8,128)(2,1)} %all-to-all-done.packed_ref, bf16[3,160,256]{2,1,0:T(8,128)(2,1)} %pad_maximum_fusion.3.project_ref, f32[1,128]{1,0:T(1,128)} %bitcast.104), custom_call_target="tpu_custom_call" | custom-call | flops 2013265920 | bytes 4325376 | tf_op jit(solution)/shard_map/attention/pallas_call | solution.py:161
  120.3 5.1 %all-to-all-start.1 = ((bf16[4,256,384]{2,1,0:T(8,128)(2,1)}), bf16[4,256,384]{2,1,0:T(8,128)(2,1)}, u32[]{:S(2)}, u32[]{:S(2)}) async-start(bf16[4,256,384]{2,1,0:T(8,128)(2,1)} %attention.1), calls=%async_computation.1 | async-start | bytes 1572864 | tf_op jit(solution)/shard_map/all_to_all | solution.py:282
  125.4 0.7 slice.36
  126.1 11.1 %all-to-all-done.1 = bf16[4,256,384]{2,1,0:T(8,128)(2,1)} async-done(((bf16[4,256,384]{2,1,0:T(8,128)(2,1)}), bf16[4,256,384]{2,1,0:T(8,128)(2,1)}, u32[]{:S(2)}, u32[]{:S(2)}) %all-to-all-start.1) | async-done | bytes 786464 | tf_op jit(solution)/shard_map/all_to_all | solution.py:282
  137.2 2.3 %copy.15 = bf16[256,4,384]{0,2,1:T(8,128)(2,1)} copy(bf16[256,4,384]{2,0,1:T(8,128)(2,1)} %bitcast.30) | data formatting | bytes 1572864 | tf_op jit(solution)/shard_map/transpose | solution.py:283
  139.5 5.5 %fusion.31 = f32[256,3072]{1,0:T(8,128)S(1)} fusion(bf16[256,1536]{0,1:T(8,128)(2,1)} %bitcast.95, bf16[3072,1536]{1,0:T(8,128)(2,1)} %all-gather.2.cloned.1.call-done), kind=kOutput, calls=%fused_computation.90 | convolution fusion | flops 2415919104 | bytes 13369344 | tf_op jit(solution)/shard_map/dot_general | solution.py:284
  145.0 0.8 fusion.26
  146.3 0.7 bitcast_convert_fusion
  147.0 1.7 collective-permute-start.11
  148.6 0.9 collective-permute-done.11
  149.5 2.2 %collective-permute-start.12 = (bf16[64,256]{1,0:T(8,128)(2,1)S(1)}, bf16[64,256]{1,0:T(8,128)(2,1)S(1)}, u32[]{:S(2)}, u32[]{:S(2)}) collective-permute-start(bf16[64,256]{1,0:T(8,128)(2,1)S(1)} %fusion.21), channel_id=1, source_target_pairs={{0,8},{8,16},{16,24},{24,32},{32,40},{40,48},{48,56},{56,64},{64,7... | collective-permute-start | bytes 98312 | tf_op jit(solution)/shard_map/ppermute | solution.py:23
  151.7 1.0 collective-permute-done.12
  152.7 3.7 %collective-permute-start.13 = (bf16[64,256]{1,0:T(8,128)(2,1)S(1)}, bf16[64,256]{1,0:T(8,128)(2,1)S(1)}, u32[]{:S(2)}, u32[]{:S(2)}) collective-permute-start(bf16[64,256]{1,0:T(8,128)(2,1)S(1)} %fusion.17), channel_id=1, source_target_pairs={{0,16},{8,24},{16,32},{24,40},{32,48},{40,56},{48,64},{56,72},{64,... | collective-permute-start | bytes 98312 | tf_op jit(solution)/shard_map/ppermute | solution.py:23
  156.4 1.0 collective-permute-done.13
  157.5 8.8 %collective-permute-start.14 = (bf16[64,256]{1,0:T(8,128)(2,1)S(1)}, bf16[64,256]{1,0:T(8,128)(2,1)S(1)}, u32[]{:S(2)}, u32[]{:S(2)}) collective-permute-start(bf16[64,256]{1,0:T(8,128)(2,1)S(1)} %add_convert_fusion), channel_id=1, source_target_pairs={{0,32},{8,40},{16,48},{24,56},{32,64},{40,72},{48,80},{56,88},{64,... | collective-permute-start | bytes 98312 | tf_op jit(solution)/shard_map/ppermute | solution.py:38
  166.3 1.0 collective-permute-done.14
  167.3 0.7 collective-permute-start.15
  168.0 8.5 %collective-permute-start.16 = (bf16[64,256]{1,0:T(8,128)(2,1)S(1)}, bf16[64,256]{1,0:T(8,128)(2,1)S(1)}, u32[]{:S(2)}, u32[]{:S(2)}) collective-permute-start(bf16[64,256]{1,0:T(8,128)(2,1)S(1)} %fusion.18), channel_id=1, source_target_pairs={{0,4},{4,0},{1,5},{5,1},{2,6},{6,2},{3,7},{7,3},{8,12},{12,8},{9,1... | collective-permute-start | bytes 98312 | tf_op jit(solution)/shard_map/ppermute | solution.py:27
  176.5 0.9 collective-permute-done.16
  177.4 0.7 fusion.16
  (51 shorter events, 3.3 us)
Async XLA Ops:
  6.5 139.7 %copy-start = (bf16[3072,64]{0,1:T(8,128)(2,1)S(1)}, bf16[3072,64]{0,1:T(8,128)(2,1)}, u32[]{:S(2)}) copy-start(bf16[3072,64]{0,1:T(8,128)(2,1)} %param.25) | copy-start | bytes 1179652
  6.6 132.9 %all-gather.2.cloned.1.call-start = ((), (), s32[]{:S(2)}) async-start(), calls=%async_computation.2 | async-start | bytes 9732096 | tf_op jit(solution)/shard_map/all_gather | solution.py:216
  8.2 21.7 %collective-permute-start = (bf16[96,384]{1,0:T(8,128)(2,1)S(1)}, bf16[96,384]{1,0:T(8,128)(2,1)S(1)}, u32[]{:S(2)}, u32[]{:S(2)}) collective-permute-start(bf16[96,384]{1,0:T(8,128)(2,1)S(1)} %constant_dynamic-slice_fusion), channel_id=1, source_target_pairs={{0,4},{4,0},{1,5},{5,1},{2,6},{6,2},{3,7},{7,3},{8,12},{12,8},{9,1... | collective-permute-start | bytes 221192 | tf_op jit(solution)/shard_map/ppermute | solution.py:27
  30.9 8.3 %collective-permute-start.1 = (bf16[192,384]{1,0:T(8,128)(2,1)S(1)}, bf16[192,384]{1,0:T(8,128)(2,1)}, u32[]{:S(2)}, u32[]{:S(2)}) collective-permute-start(bf16[192,384]{1,0:T(8,128)(2,1)S(1)} %pad_maximum_fusion.4), channel_id=1, source_target_pairs={{0,8},{8,16},{16,24},{24,32},{32,40},{40,48},{48,56},{56,64},{64,7... | collective-permute-start | bytes 442376 | tf_op jit(solution)/shard_map/ppermute | solution.py:38
  39.2 7.7 %collective-permute-start.2 = (bf16[192,384]{1,0:T(8,128)(2,1)}, bf16[192,384]{1,0:T(8,128)(2,1)}, u32[]{:S(2)}, u32[]{:S(2)}) collective-permute-start(bf16[192,384]{1,0:T(8,128)(2,1)} %collective-permute-done.1), channel_id=1, source_target_pairs={{0,8},{8,16},{16,24},{24,32},{32,40},{40,48},{48,56},{56,64},{64,7... | collective-permute-start | bytes 442376 | tf_op jit(solution)/shard_map/ppermute | solution.py:38
  44.9 8.1 %copy-start.3 = (f32[1000]{0:T(1024)S(1)}, f32[1000]{0:T(1024)}, u32[]{:S(2)}) copy-start(f32[1000]{0:T(1024)} %param.16) | copy-start | bytes 12004
  46.9 6.1 %collective-permute-start.3 = (bf16[192,384]{1,0:T(8,128)(2,1)}, bf16[192,384]{1,0:T(8,128)(2,1)}, u32[]{:S(2)}, u32[]{:S(2)}) collective-permute-start(bf16[192,384]{1,0:T(8,128)(2,1)} %collective-permute-done.2), channel_id=1, source_target_pairs={{0,8},{8,16},{16,24},{24,32},{32,40},{40,48},{48,56},{56,64},{64,7... | collective-permute-start | bytes 442376 | tf_op jit(solution)/shard_map/ppermute | solution.py:38
  46.9 63.5 %all-to-all-start = ((bf16[4,720,384]{2,1,0:T(8,128)(2,1)}), bf16[4,720,384]{2,1,0:T(8,128)(2,1)}, u32[]{:S(2)}, u32[]{:S(2)}) async-start(bf16[4,720,384]{2,1,0:T(8,128)(2,1)} %pack.1), calls=%async_computation | async-start | bytes 4423680 | tf_op jit(solution)/shard_map/all_to_all | solution.py:271
  54.3 16.7 %copy-start.1 = (f32[3072]{0:T(1024)S(1)}, f32[3072]{0:T(1024)}, u32[]{:S(2)}) copy-start(f32[3072]{0:T(1024)} %param.19) | copy-start | bytes 36868
  54.3 8.0 %collective-permute-start.4 = (bf16[192,384]{1,0:T(8,128)(2,1)}, bf16[192,384]{1,0:T(8,128)(2,1)}, u32[]{:S(2)}, u32[]{:S(2)}) collective-permute-start(bf16[192,384]{1,0:T(8,128)(2,1)} %collective-permute-done.3), channel_id=1, source_target_pairs={{0,8},{8,16},{16,24},{24,32},{32,40},{40,48},{48,56},{56,64},{64,7... | collective-permute-start | bytes 442376 | tf_op jit(solution)/shard_map/ppermute | solution.py:38
  62.3 8.7 %collective-permute-start.5 = (bf16[192,384]{1,0:T(8,128)(2,1)}, bf16[192,384]{1,0:T(8,128)(2,1)}, u32[]{:S(2)}, u32[]{:S(2)}) collective-permute-start(bf16[192,384]{1,0:T(8,128)(2,1)} %collective-permute-done.4), channel_id=1, source_target_pairs={{0,8},{8,16},{16,24},{24,32},{32,40},{40,48},{48,56},{56,64},{64,7... | collective-permute-start | bytes 442376 | tf_op jit(solution)/shard_map/ppermute | solution.py:38
  69.4 25.7 %collective-permute-start.7 = (bf16[768,384]{1,0:T(8,128)(2,1)}, bf16[768,384]{1,0:T(8,128)(2,1)}, u32[]{:S(2)}, u32[]{:S(2)}) collective-permute-start(bf16[768,384]{1,0:T(8,128)(2,1)} %pad_maximum_fusion.1), channel_id=1, source_target_pairs={{0,4},{4,0},{1,5},{5,1},{2,6},{6,2},{3,7},{7,3},{8,12},{12,8},{9,1... | collective-permute-start | bytes 1769480 | tf_op jit(solution)/shard_map/ppermute | solution.py:27
  72.3 9.0 %collective-permute-start.6 = (bf16[192,384]{1,0:T(8,128)(2,1)}, bf16[192,384]{1,0:T(8,128)(2,1)S(1)}, u32[]{:S(2)}, u32[]{:S(2)}) collective-permute-start(bf16[192,384]{1,0:T(8,128)(2,1)} %collective-permute-done.5), channel_id=1, source_target_pairs={{0,8},{8,16},{16,24},{24,32},{32,40},{40,48},{48,56},{56,64},{64,7... | collective-permute-start | bytes 442376 | tf_op jit(solution)/shard_map/ppermute | solution.py:38
  81.3 8.4 %collective-permute-start.8 = (bf16[192,384]{1,0:T(8,128)(2,1)S(1)}, bf16[192,384]{1,0:T(8,128)(2,1)S(1)}, u32[]{:S(2)}, u32[]{:S(2)}) collective-permute-start(bf16[192,384]{1,0:T(8,128)(2,1)S(1)} %collective-permute-done.6), channel_id=1, source_target_pairs={{0,8},{8,16},{16,24},{24,32},{32,40},{40,48},{48,56},{56,64},{64,7... | collective-permute-start | bytes 442376 | tf_op jit(solution)/shard_map/ppermute | solution.py:38
  90.7 13.6 %collective-permute-start.9 = (bf16[576,384]{1,0:T(8,128)(2,1)S(1)}, bf16[576,384]{1,0:T(8,128)(2,1)S(1)}, u32[]{:S(2)}, u32[]{:S(2)}) collective-permute-start(bf16[576,384]{1,0:T(8,128)(2,1)S(1)} %pad_maximum_fusion.2), channel_id=1, source_target_pairs={{0,4},{4,0},{1,5},{5,1},{2,6},{6,2},{3,7},{7,3},{8,12},{12,8},{9,1... | collective-permute-start | bytes 1327112 | tf_op jit(solution)/shard_map/ppermute | solution.py:27
  95.1 11.3 %collective-permute-start.10 = (bf16[192,384]{1,0:T(8,128)(2,1)S(1)}, bf16[192,384]{1,0:T(8,128)(2,1)S(1)}, u32[]{:S(2)}, u32[]{:S(2)}) collective-permute-start(bf16[192,384]{1,0:T(8,128)(2,1)S(1)} %collective-permute-done.8), channel_id=1, source_target_pairs={{0,8},{8,16},{16,24},{24,32},{32,40},{40,48},{48,56},{56,64},{64,7... | collective-permute-start | bytes 442376 | tf_op jit(solution)/shard_map/ppermute | solution.py:38
  107.1 2.4 %copy-start.4 = (bf16[160]{0:T(256)(128)(2,1)S(1)}, bf16[160]{0:T(256)(128)(2,1)}, u32[]{:S(2)}) copy-start(bf16[160]{0:T(256)(128)(2,1)} %fusion.22) | copy-start | bytes 964
  120.3 16.9 %all-to-all-start.1 = ((bf16[4,256,384]{2,1,0:T(8,128)(2,1)}), bf16[4,256,384]{2,1,0:T(8,128)(2,1)}, u32[]{:S(2)}, u32[]{:S(2)}) async-start(bf16[4,256,384]{2,1,0:T(8,128)(2,1)} %attention.1), calls=%async_computation.1 | async-start | bytes 1572864 | tf_op jit(solution)/shard_map/all_to_all | solution.py:282
  146.2 31.2 %copy-start.2 = (f32[256,64]{0,1:T(8,128)S(1)}, f32[256,64]{0,1:T(8,128)}, u32[]{:S(2)}) copy-start(f32[256,64]{0,1:T(8,128)} %param.14) | copy-start | bytes 196612
  147.0 2.5 %collective-permute-start.11 = (bf16[64,256]{1,0:T(8,128)(2,1)S(1)}, bf16[64,256]{1,0:T(8,128)(2,1)S(1)}, u32[]{:S(2)}, u32[]{:S(2)}) collective-permute-start(bf16[64,256]{1,0:T(8,128)(2,1)S(1)} %get-tuple-element.63), channel_id=1, source_target_pairs={{0,4},{4,0},{1,5},{5,1},{2,6},{6,2},{3,7},{7,3},{8,12},{12,8},{9,1... | collective-permute-start | bytes 98312 | tf_op jit(solution)/shard_map/ppermute | solution.py:27
  149.5 3.2 %collective-permute-start.12 = (bf16[64,256]{1,0:T(8,128)(2,1)S(1)}, bf16[64,256]{1,0:T(8,128)(2,1)S(1)}, u32[]{:S(2)}, u32[]{:S(2)}) collective-permute-start(bf16[64,256]{1,0:T(8,128)(2,1)S(1)} %fusion.21), channel_id=1, source_target_pairs={{0,8},{8,16},{16,24},{24,32},{32,40},{40,48},{48,56},{56,64},{64,7... | collective-permute-start | bytes 98312 | tf_op jit(solution)/shard_map/ppermute | solution.py:23
  152.7 4.7 %collective-permute-start.13 = (bf16[64,256]{1,0:T(8,128)(2,1)S(1)}, bf16[64,256]{1,0:T(8,128)(2,1)S(1)}, u32[]{:S(2)}, u32[]{:S(2)}) collective-permute-start(bf16[64,256]{1,0:T(8,128)(2,1)S(1)} %fusion.17), channel_id=1, source_target_pairs={{0,16},{8,24},{16,32},{24,40},{32,48},{40,56},{48,64},{56,72},{64,... | collective-permute-start | bytes 98312 | tf_op jit(solution)/shard_map/ppermute | solution.py:23
  157.5 9.8 %collective-permute-start.14 = (bf16[64,256]{1,0:T(8,128)(2,1)S(1)}, bf16[64,256]{1,0:T(8,128)(2,1)S(1)}, u32[]{:S(2)}, u32[]{:S(2)}) collective-permute-start(bf16[64,256]{1,0:T(8,128)(2,1)S(1)} %add_convert_fusion), channel_id=1, source_target_pairs={{0,32},{8,40},{16,48},{24,56},{32,64},{40,72},{48,80},{56,88},{64,... | collective-permute-start | bytes 98312 | tf_op jit(solution)/shard_map/ppermute | solution.py:38
  167.3 0.7 collective-permute-start.15
  168.0 9.4 %collective-permute-start.16 = (bf16[64,256]{1,0:T(8,128)(2,1)S(1)}, bf16[64,256]{1,0:T(8,128)(2,1)S(1)}, u32[]{:S(2)}, u32[]{:S(2)}) collective-permute-start(bf16[64,256]{1,0:T(8,128)(2,1)S(1)} %fusion.18), channel_id=1, source_target_pairs={{0,4},{4,0},{1,5},{5,1},{2,6},{6,2},{3,7},{7,3},{8,12},{12,8},{9,1... | collective-permute-start | bytes 98312 | tf_op jit(solution)/shard_map/ppermute | solution.py:27
Sparse Core Ops, SparseCore 0:
  9.2 99.2 all-gather.1

commit v6 on v5

--- a/solution.py
+++ b/solution.py
@@ -38,14 +38,9 @@
     return lax.ppermute(value, ("chip", "core"), pairs)
 
 
-def gather_rows(shard, tasks):
-    chips, here, core = lax.axis_size("chip"), lax.axis_index("chip"), lax.axis_index("core")
-    other = swap_cores(shard)
-    piece = jnp.concatenate([jnp.where(core == 0, shard, other), jnp.where(core == 0, other, shard)])
-    rows = piece.shape[0]
-    step = jnp.where(core == 0, 1, -1)
-    half = chips // 2
-    pieces, waiting, results = [(0, piece)], [], {}
+def pass_round(piece, tasks):
+    half = lax.axis_size("chip") // 2
+    own, swapped, waiting, results = [piece], [], [], {}
     for hop in range(1, half + 1):
         sent = send_by_core(piece, 1, -1, True)
         if hop in tasks:
@@ -56,19 +51,65 @@
             results[hop] = task(*inputs)
             sent, results[hop] = lax.optimization_barrier((sent, results[hop]))
         piece = sent
-        pieces.append((hop, piece))
-        if 2 * hop != chips:
-            waiting.append((hop, piece))
+        own.append(piece)
+        waiting.append(piece)
         if hop in (half // 2, half - 1):
-            swapped = swap_cores(jnp.concatenate([p for _, p in waiting]))
-            for i, (at, _) in enumerate(waiting):
-                pieces.append((-at, swapped[i * rows : (i + 1) * rows]))
+            swapped.append(swap_cores(jnp.concatenate(waiting)))
             waiting = []
-    held = jnp.zeros((chips, *piece.shape), shard.dtype)
-    for at, piece in pieces:
-        owner = lax.rem(here - at * step + chips, chips)
-        held = lax.dynamic_update_slice_in_dim(held, piece[None], owner, 0)
-    return held, results
+    return own, swapped, results
+
+
+def project_body(counts, place_ref, source_ref, *refs):
+    own, swapped, out_ref, joined_ref = refs[:-4], refs[-4:-2], refs[-2], refs[-1]
+    rows = own[0].shape[0]
+
+    def put(value, slot):
+        joined_ref[pl.ds(pl.multiple_of(place_ref[slot] * rows, rows), rows)] = value
+
+    for hop, piece in enumerate(own):
+        put(piece[...], hop)
+    slot = len(own)
+    for count, batch in zip(counts, swapped):
+        for i in range(count):
+            put(batch[i * rows : (i + 1) * rows], slot)
+            slot += 1
+    total = jnp.dot(source_ref[...], joined_ref[...], preferred_element_type=jnp.float32)
+    deep = total.shape[0] // 2
+    total = total[:deep] + total[deep:]
+    coarse = total.astype(jnp.bfloat16)
+    fine = (total - coarse.astype(jnp.float32)).astype(jnp.bfloat16)
+    row = lax.broadcasted_iota(jnp.int32, (deep, HEAD), 0)
+    spread = (row == deep - EXTRA + 1) | (row == deep - EXTRA + 2)
+    picks = jnp.where(spread, 1.0, 0.0).astype(jnp.bfloat16)
+    for head in range(out_ref.shape[0]):
+        columns = slice(head * HEAD, (head + 1) * HEAD)
+        out_ref[head, :deep, :HEAD] = coarse[:, columns]
+        out_ref[head, deep:, :HEAD] = fine[:, columns]
+        out_ref[head, :deep, HEAD:] = picks
+        out_ref[head, deep:, HEAD:] = jnp.zeros_like(picks)
+
+
+def project_latents(source, own, swapped):
+    chips, here = lax.axis_size("chip"), lax.axis_index("chip")
+    step = jnp.where(lax.axis_index("core") == 0, 1, -1)
+    rows, columns = own[0].shape
+    counts = [batch.shape[0] // rows for batch in swapped]
+    hops = list(range(len(own))) + [-hop for hop in range(1, sum(counts) + 1)]
+    places = lax.rem(here - jnp.array(hops, jnp.int32) * step + chips, chips)
+    whole = pl.BlockSpec(memory_space=pltpu.VMEM)
+    return pl.pallas_call(
+        functools.partial(project_body, counts),
+        in_specs=[pl.BlockSpec(memory_space=pltpu.SMEM)] + [whole] * (1 + len(own) + len(swapped)),
+        out_specs=whole,
+        out_shape=jax.ShapeDtypeStruct((columns // HEAD, source.shape[0], 2 * HEAD), jnp.bfloat16),
+        scratch_shapes=[pltpu.VMEM((chips * rows, columns), jnp.bfloat16)],
+        cost_estimate=pl.CostEstimate(
+            flops=2 * source.size * columns,
+            bytes_accessed=2 * source.size + 4 * chips * rows * columns,
+            transcendentals=0,
+        ),
+        name="project",
+    )(places, source, *own, *swapped)
 
 
 def time_embed(sigma_now, half_count):
@@ -213,6 +254,8 @@
     channels, token_count = latent.shape
     key_rows = stale_keys.shape[1]
 
+    core = lax.axis_index("core")
+
     all_out_weight = lax.all_gather(out_weight, STEP, axis=0, tiled=True)
 
     def embed(latent, embed_weight, embed_bias):
@@ -266,18 +309,13 @@
         4: (modulation, (step_index, sigma_table, mod_weight)),
         6: (sources, lambda done: (done[4][0], embed_weight, embed_bias)),
     }
-    gathered, done = gather_rows(my_columns, tasks)
+    other = swap_cores(my_columns)
+    piece = [jnp.where(core == 0, my_columns, other), jnp.where(core == 0, other, my_columns)]
+    own, swapped, done = pass_round(jnp.concatenate(piece), tasks)
     hidden, (modulate, delta), source = done[1][0], done[4], done[6]
     packed = lax.all_to_all(done[2], "patch", 0, 0, tiled=True)
 
-    project = jnp.dot(source, gathered.reshape(width, columns), preferred_element_type=jnp.float32)
-    deep = channels + EXTRA
-    project = split(project[:deep] + project[deep:])
-    project = jnp.moveaxis(project.reshape(2 * deep, -1, HEAD), 1, 0)
-    row = lax.broadcasted_iota(jnp.int32, (1, 2 * deep, HEAD), 1)
-    picks = jnp.where((row == channels + 1) | (row == channels + 2), 1.0, 0.0).astype(jnp.bfloat16)
-    project = jnp.concatenate([project, jnp.broadcast_to(picks, project.shape)], axis=2)
-
+    project = project_latents(source, own, swapped)
     attended = attention(project, query_gain, packed, key_rows, token_count)
     attended = lax.all_to_all(attended, "patch", 0, 0, tiled=True)
     attended = jnp.moveaxis(attended, 0, 1).reshape(token_count, -1)

time: 186 us -> 182 us (0.978)
  local copies, waits for them, and re-layouts: 24.1 us -> 4.04 us
  starting transfers between devices: 76.6 us -> 85.4 us
  waiting for transfers between devices: 25.8 us -> 31.1 us
  Pallas kernels: 13.8 us -> 17.5 us
  matrix products: 14 us -> 11.6 us
    dynamic_update_slice x15 -> x0, local copies, waits for them, and re-layouts: 18.3 us -> none  [gather_rows(): held = lax.dynamic_update_slice_in_dim(held, piece[None], owner, 0)]
    ppermute x10, starting transfers between devices: 26.1 us -> 33.4 us  [send_by_core(): return lax.ppermute(value, ('chip', 'core'), pairs)]
    ppermute x10, waiting for transfers between devices: 10.2 us -> 16.4 us  [send_by_core(): return lax.ppermute(value, ('chip', 'core'), pairs)]
    pallas_call x0 -> x1, Pallas kernels: none -> 3.61 us  [project_latents(): pl.pallas_call(functools.partial(project_body, counts), in_specs=[pl.Bloc...]
    ppermute x5, starting transfers between devices: 35 us -> 37.8 us  [swap_cores(): return lax.ppermute(value, 'core', [(0, 1), (1, 0)])]
    dot_general x1 -> x0, matrix products: 2.37 us -> none  [per_device(): jnp.dot(source, gathered.reshape(width, columns), preferred_element_type=...]
    concatenate x4 -> x3, other arithmetic: 3.74 us -> 3.81 us  [the longest x2 3.79 us: pass_round(): swapped.append(swap_cores(jnp.concatenate(waiting)))]
  transfers between devices with their start and end apart: 20 -> 20, of which waited for: 11 -> 14; matrix products, arithmetic and copies ran while one was open for 24% -> 12% of each run, Pallas kernels for 7% -> 10%
where the time goes in v6:
time: 182 us; the launch traced here: 181 us
  starting transfers between devices  85.4 us (47%)
  waiting for transfers between devices  31.1 us (17%)
  Pallas kernels  17.5 us (10%)
  between operations  16.8 us (9%)
  other arithmetic  14.1 us (8%)
  matrix products  11.6 us (6%)
  local copies, waits for them, and re-layouts  4.04 us (2%)
    ppermute x5, starting transfers between devices, swap_cores(): return lax.ppermute(value, 'core', [(0, 1), (1, 0)])  37.8 us
    ppermute x10, starting transfers between devices, send_by_core(): return lax.ppermute(value, ('chip', 'core'), pairs)  33.4 us
    ppermute x10, waiting for transfers between devices, send_by_core(): return lax.ppermute(value, ('chip', 'core'), pairs)  16.4 us
    pallas_call x1, Pallas kernels, attention(): pl.pallas_call(functools.partial(attention_body, parts, rows, tile), grid...  9.93 us
    all_to_all x1, waiting for transfers between devices, per_device(): attended = lax.all_to_all(attended, 'patch', 0, 0, tiled=True)  9.32 us
    dot_general x1, matrix products, per_device(): lax.dot_general(attended, all_out_weight, (((1,), (1,)), ((), ())), prefe...  5.47 us
    ppermute x2, starting transfers between devices, shift(): return lax.ppermute(value, axis, pairs)  5.26 us
    all_to_all x1, starting transfers between devices, per_device(): packed = lax.all_to_all(done[2], 'patch', 0, 0, tiled=True)  4.58 us
  transfers between devices with their start and end apart: 20, of which 14 were waited for; matrix products, arithmetic and copies ran while one was open for 12% of the time, Pallas kernels for 10%

profile of v6, /device:TPU:33, one launch (start us, length us, event | category | flops | bytes accessed | tf_op | source)
XLA Modules:
  0.0 180.5 jit_solution(14925724420713159490)
XLA Ops:
  6.6 0.7 all-gather.2.cloned.1.call-update
  7.3 0.9 constant_dynamic-slice_fusion
  8.2 20.4 %collective-permute-start = (bf16[96,384]{1,0:T(8,128)(2,1)S(1)}, bf16[96,384]{1,0:T(8,128)(2,1)S(1)}, u32[]{:S(2)}, u32[]{:S(2)}) collective-permute-start(bf16[96,384]{1,0:T(8,128)(2,1)S(1)} %constant_dynamic-slice_fusion), channel_id=1, source_target_pairs={{0,4},{4,0},{1,5},{5,1},{2,6},{6,2},{3,7},{7,3},{8,12},{12,8},{9,1... | collective-permute-start | bytes 221192 | tf_op jit(solution)/shard_map/ppermute | solution.py:27
  28.6 0.9 collective-permute-done
  29.5 0.9 broadcast_select_fusion.1
  30.5 3.2 %collective-permute-start.1 = (bf16[192,384]{1,0:T(8,128)(2,1)S(1)}, bf16[192,384]{1,0:T(8,128)(2,1)}, u32[]{:S(2)}, u32[]{:S(2)}) collective-permute-start(bf16[192,384]{1,0:T(8,128)(2,1)S(1)} %pad_maximum_fusion.3.refs_0_), channel_id=1, source_target_pairs={{0,8},{8,16},{16,24},{24,32},{32,40},{40,48},{48,56},{56,64},{64,7... | collective-permute-start | bytes 442376 | tf_op jit(solution)/shard_map/ppermute | solution.py:38
  33.7 1.7 fusion.19
  35.4 0.0 copy-start.6
  35.4 0.5 multiply_reduce_fusion.1
  35.9 0.6 add_sqrt_fusion
  36.4 2.6 %collective-permute-start.2 = (bf16[192,384]{1,0:T(8,128)(2,1)}, bf16[192,384]{1,0:T(8,128)(2,1)}, u32[]{:S(2)}, u32[]{:S(2)}) collective-permute-start(bf16[192,384]{1,0:T(8,128)(2,1)} %collective-permute-done.1.refs_1_), channel_id=1, source_target_pairs={{0,8},{8,16},{16,24},{24,32},{32,40},{40,48},{48,56},{56,64},{64,7... | collective-permute-start | bytes 442376 | tf_op jit(solution)/shard_map/ppermute | solution.py:38
  39.0 3.9 %pack.1 = bf16[4,720,384]{2,1,0:T(8,128)(2,1)} custom-call(bf16[320,1536]{1,0:T(8,128)(2,1)} %bitcast.37, bf16[320,1536]{1,0:T(8,128)(2,1)} %bitcast.38, f32[64,256]{1,0:T(8,128)} %bitcast.41, f32[1,256]{1,0:T(1,128)} %bitcast.47), custom_call_target="tpu_custom_call" | custom-call | flops 1105920 | bytes 4423680 | tf_op jit(solution)/shard_map/pack/pallas_call | solution.py:148
  43.0 0.4 collective-permute-done.2.refs_2_
  43.3 3.4 %collective-permute-start.3 = (bf16[192,384]{1,0:T(8,128)(2,1)}, bf16[192,384]{1,0:T(8,128)(2,1)}, u32[]{:S(2)}, u32[]{:S(2)}) collective-permute-start(bf16[192,384]{1,0:T(8,128)(2,1)} %collective-permute-done.2.refs_2_), channel_id=1, source_target_pairs={{0,8},{8,16},{16,24},{24,32},{32,40},{40,48},{48,56},{56,64},{64,7... | collective-permute-start | bytes 442376 | tf_op jit(solution)/shard_map/ppermute | solution.py:38
  47.4 4.8 %collective-permute-done.3.refs_3_ = bf16[192,384]{1,0:T(8,128)(2,1)} collective-permute-done((bf16[192,384]{1,0:T(8,128)(2,1)}, bf16[192,384]{1,0:T(8,128)(2,1)}, u32[]{:S(2)}, u32[]{:S(2)}) %collective-permute-start.3) | collective-permute-done | bytes 147488 | tf_op jit(solution)/shard_map/ppermute | solution.py:38
  52.1 0.7 select_reduce_fusion
  53.5 3.5 %collective-permute-start.4 = (bf16[192,384]{1,0:T(8,128)(2,1)}, bf16[192,384]{1,0:T(8,128)(2,1)}, u32[]{:S(2)}, u32[]{:S(2)}) collective-permute-start(bf16[192,384]{1,0:T(8,128)(2,1)} %collective-permute-done.3.refs_3_), channel_id=1, source_target_pairs={{0,8},{8,16},{16,24},{24,32},{32,40},{40,48},{48,56},{56,64},{64,7... | collective-permute-start | bytes 442376 | tf_op jit(solution)/shard_map/ppermute | solution.py:38
  57.0 3.8 %fusion.20 = f32[1,9216]{1,0:T(1,128)} fusion(bf16[256,1]{0,1:T(2,128)(2,1)S(1)} %reshape.58, bf16[256,9216]{1,0:T(8,128)(2,1)} %param.18), kind=kOutput, calls=%fused_computation.60 | convolution fusion | flops 4718592 | bytes 4755968 | tf_op jit(solution)/shard_map/dot_general | solution.py:278
  62.0 0.4 collective-permute-done.4.refs_4_
  62.4 3.4 %collective-permute-start.5 = (bf16[192,384]{1,0:T(8,128)(2,1)}, bf16[192,384]{1,0:T(8,128)(2,1)}, u32[]{:S(2)}, u32[]{:S(2)}) collective-permute-start(bf16[192,384]{1,0:T(8,128)(2,1)} %collective-permute-done.4.refs_4_), channel_id=1, source_target_pairs={{0,8},{8,16},{16,24},{24,32},{32,40},{40,48},{48,56},{56,64},{64,7... | collective-permute-start | bytes 442376 | tf_op jit(solution)/shard_map/ppermute | solution.py:38
  65.8 0.1 pad.12.clone
  65.9 4.6 %all-to-all-start = ((bf16[4,720,384]{2,1,0:T(8,128)(2,1)}), bf16[4,720,384]{2,1,0:T(8,128)(2,1)}, u32[]{:S(2)}, u32[]{:S(2)}) async-start(bf16[4,720,384]{2,1,0:T(8,128)(2,1)} %pack.1), calls=%async_computation | async-start | bytes 4423680 | tf_op jit(solution)/shard_map/all_to_all | solution.py:316
  70.4 0.3 collective-permute-done.5.refs_5_
  70.8 0.7 reduce_sum.77
  72.1 3.5 %collective-permute-start.6 = (bf16[192,384]{1,0:T(8,128)(2,1)}, bf16[192,384]{1,0:T(8,128)(2,1)S(1)}, u32[]{:S(2)}, u32[]{:S(2)}) collective-permute-start(bf16[192,384]{1,0:T(8,128)(2,1)} %collective-permute-done.5.refs_5_), channel_id=1, source_target_pairs={{0,8},{8,16},{16,24},{24,32},{32,40},{40,48},{48,56},{56,64},{64,7... | collective-permute-start | bytes 442376 | tf_op jit(solution)/shard_map/ppermute | solution.py:38
  75.6 1.2 convert_reduce_fusion
  76.8 0.7 slice_add_fusion
  77.5 1.1 convert_subtract_fusion
  78.7 0.1 maximum_multiply_fusion
  78.7 0.0 copy-start.7
  78.8 0.2 subtract_convert_fusion
  78.9 0.1 fusion.3
  79.1 1.0 pad_maximum_fusion.source_ref
  80.1 0.9 collective-permute-done.6.refs_6_
  81.0 3.4 %collective-permute-start.7 = (bf16[192,384]{1,0:T(8,128)(2,1)S(1)}, bf16[192,384]{1,0:T(8,128)(2,1)S(1)}, u32[]{:S(2)}, u32[]{:S(2)}) collective-permute-start(bf16[192,384]{1,0:T(8,128)(2,1)S(1)} %collective-permute-done.6.refs_6_), channel_id=1, source_target_pairs={{0,8},{8,16},{16,24},{24,32},{32,40},{40,48},{48,56},{56,64},{64,7... | collective-permute-start | bytes 442376 | tf_op jit(solution)/shard_map/ppermute | solution.py:38
  84.4 2.0 %pad_maximum_fusion.1 = bf16[768,384]{1,0:T(8,128)(2,1)} fusion(bf16[192,384]{1,0:T(8,128)(2,1)} %collective-permute-done.4.refs_4_, bf16[192,384]{1,0:T(8,128)(2,1)} %collective-permute-done.3.refs_3_, bf16[192,384]{1,0:T(8,128)(2,1)} %collective-permute-done.2.refs_2_, bf16[192,384]{1,0:T(8,128)(2,1)} %collective-permute-done.1.refs_1_), kind=kLoop, calls=%fused_computation.15 | loop fusion | flops 2359296 | bytes 1179648 | tf_op jit(solution)/shard_map/concatenate | solution.py:57
  86.4 2.8 %collective-permute-done.7.refs_7_ = bf16[192,384]{1,0:T(8,128)(2,1)S(1)} collective-permute-done((bf16[192,384]{1,0:T(8,128)(2,1)S(1)}, bf16[192,384]{1,0:T(8,128)(2,1)S(1)}, u32[]{:S(2)}, u32[]{:S(2)}) %collective-permute-start.7) | collective-permute-done | bytes 147488 | tf_op jit(solution)/shard_map/ppermute | solution.py:38
  89.2 1.8 pad_maximum_fusion.2
  91.0 3.7 %collective-permute-start.10 = (bf16[576,384]{1,0:T(8,128)(2,1)}, bf16[576,384]{1,0:T(8,128)(2,1)}, u32[]{:S(2)}, u32[]{:S(2)}) collective-permute-start(bf16[576,384]{1,0:T(8,128)(2,1)} %pad_maximum_fusion.2), channel_id=1, source_target_pairs={{0,4},{4,0},{1,5},{5,1},{2,6},{6,2},{3,7},{7,3},{8,12},{12,8},{9,1... | collective-permute-start | bytes 1327112 | tf_op jit(solution)/shard_map/ppermute | solution.py:27
  94.7 0.6 compare_select_fusion.place_ref
  95.2 5.9 %collective-permute-done.8.refs_8_ = bf16[192,384]{1,0:T(8,128)(2,1)} collective-permute-done((bf16[192,384]{1,0:T(8,128)(2,1)}, bf16[192,384]{1,0:T(8,128)(2,1)}, u32[]{:S(2)}, u32[]{:S(2)}) %collective-permute-start.8) | collective-permute-done | bytes 147488 | tf_op jit(solution)/shard_map/ppermute | solution.py:38
  101.1 3.6 %project.1.project_ref = bf16[3,160,256]{2,1,0:T(8,128)(2,1)} custom-call(s32[16]{0:T(128)} %compare_select_fusion.place_ref, bf16[160,3072]{1,0:T(8,128)(2,1)} %pad_maximum_fusion.source_ref, bf16[192,384]{1,0:T(8,128)(2,1)} %copy-done.3, bf16[192,384]{1,0:T(8,128)(2,1)} %collective-permute-done.1.refs_1_, bf16[192,384]{1,0:T(8,128)(2,1)} %collective-permute-done.2.refs_2_, ...), custom_call_target="tpu_custom_call" | custom-call | flops 377487360 | bytes 5701632 | tf_op jit(solution)/shard_map/project/pallas_call | solution.py:100
  104.7 9.9 %attention.1 = bf16[4,256,384]{2,1,0:T(8,128)(2,1)} custom-call(bf16[4,720,384]{2,1,0:T(8,128)(2,1)} %all-to-all-done.packed_ref, bf16[3,160,256]{2,1,0:T(8,128)(2,1)} %project.1.project_ref, f32[1,128]{1,0:T(1,128)} %bitcast.48), custom_call_target="tpu_custom_call" | custom-call | flops 2013265920 | bytes 4325376 | tf_op jit(solution)/shard_map/attention/pallas_call | solution.py:202
  114.7 4.3 %all-to-all-start.1 = ((bf16[4,256,384]{2,1,0:T(8,128)(2,1)}), bf16[4,256,384]{2,1,0:T(8,128)(2,1)}, u32[]{:S(2)}, u32[]{:S(2)}) async-start(bf16[4,256,384]{2,1,0:T(8,128)(2,1)} %attention.1), calls=%async_computation.1 | async-start | bytes 1572864 | tf_op jit(solution)/shard_map/all_to_all | solution.py:320
  118.9 0.7 slice.9
  119.7 9.3 %all-to-all-done.1 = bf16[4,256,384]{2,1,0:T(8,128)(2,1)} async-done(((bf16[4,256,384]{2,1,0:T(8,128)(2,1)}), bf16[4,256,384]{2,1,0:T(8,128)(2,1)}, u32[]{:S(2)}, u32[]{:S(2)}) %all-to-all-start.1) | async-done | bytes 786464 | tf_op jit(solution)/shard_map/all_to_all | solution.py:320
  129.0 2.3 %copy.15 = bf16[256,4,384]{0,2,1:T(8,128)(2,1)} copy(bf16[256,4,384]{2,0,1:T(8,128)(2,1)} %bitcast.12) | data formatting | bytes 1572864 | tf_op jit(solution)/shard_map/transpose | solution.py:321
  131.3 5.5 %fusion.21 = f32[256,3072]{1,0:T(8,128)S(1)} fusion(bf16[256,1536]{0,1:T(8,128)(2,1)} %bitcast.39, bf16[3072,1536]{1,0:T(8,128)(2,1)} %all-gather.2.cloned.1.call-done), kind=kOutput, calls=%fused_computation.61 | convolution fusion | flops 2415919104 | bytes 13369344 | tf_op jit(solution)/shard_map/dot_general | solution.py:322
  136.8 0.8 fusion.18
  137.6 0.0 copy-start.5
  137.6 0.5 multiply_reduce_fusion
  138.1 0.7 bitcast_convert_fusion
  138.8 3.4 %collective-permute-start.11 = (bf16[64,256]{1,0:T(8,128)(2,1)S(1)}, bf16[64,256]{1,0:T(8,128)(2,1)S(1)}, u32[]{:S(2)}, u32[]{:S(2)}) collective-permute-start(bf16[64,256]{1,0:T(8,128)(2,1)S(1)} %get-tuple-element.61), channel_id=1, source_target_pairs={{0,4},{4,0},{1,5},{5,1},{2,6},{6,2},{3,7},{7,3},{8,12},{12,8},{9,1... | collective-permute-start | bytes 98312 | tf_op jit(solution)/shard_map/ppermute | solution.py:27
  142.2 0.9 collective-permute-done.11
  143.1 1.7 collective-permute-start.12
  144.7 1.0 collective-permute-done.12
  145.8 3.6 %collective-permute-start.13 = (bf16[64,256]{1,0:T(8,128)(2,1)S(1)}, bf16[64,256]{1,0:T(8,128)(2,1)S(1)}, u32[]{:S(2)}, u32[]{:S(2)}) collective-permute-start(bf16[64,256]{1,0:T(8,128)(2,1)S(1)} %fusion.10), channel_id=1, source_target_pairs={{0,16},{8,24},{16,32},{24,40},{32,48},{40,56},{48,64},{56,72},{64,... | collective-permute-start | bytes 98312 | tf_op jit(solution)/shard_map/ppermute | solution.py:23
  149.4 1.0 collective-permute-done.13
  150.4 9.7 %collective-permute-start.14 = (bf16[64,256]{1,0:T(8,128)(2,1)S(1)}, bf16[64,256]{1,0:T(8,128)(2,1)S(1)}, u32[]{:S(2)}, u32[]{:S(2)}) collective-permute-start(bf16[64,256]{1,0:T(8,128)(2,1)S(1)} %add_convert_fusion), channel_id=1, source_target_pairs={{0,32},{8,40},{16,48},{24,56},{32,64},{40,72},{48,80},{56,88},{64,... | collective-permute-start | bytes 98312 | tf_op jit(solution)/shard_map/ppermute | solution.py:38
  160.1 1.0 collective-permute-done.14
  161.1 0.7 collective-permute-start.15
  161.8 10.3 %collective-permute-start.16 = (bf16[64,256]{1,0:T(8,128)(2,1)S(1)}, bf16[64,256]{1,0:T(8,128)(2,1)S(1)}, u32[]{:S(2)}, u32[]{:S(2)}) collective-permute-start(bf16[64,256]{1,0:T(8,128)(2,1)S(1)} %fusion.11), channel_id=1, source_target_pairs={{0,4},{4,0},{1,5},{5,1},{2,6},{6,2},{3,7},{7,3},{8,12},{12,8},{9,1... | collective-permute-start | bytes 98312 | tf_op jit(solution)/shard_map/ppermute | solution.py:27
  172.1 0.9 collective-permute-done.16
  173.0 0.7 fusion.9
  (36 shorter events, 0.2 us)
Async XLA Ops:
  6.5 131.5 %copy-start = (bf16[3072,64]{0,1:T(8,128)(2,1)S(1)}, bf16[3072,64]{0,1:T(8,128)(2,1)}, u32[]{:S(2)}) copy-start(bf16[3072,64]{0,1:T(8,128)(2,1)} %param.26) | copy-start | bytes 1179652
  6.6 124.7 %all-gather.2.cloned.1.call-start = ((), (), s32[]{:S(2)}) async-start(), calls=%async_computation.2 | async-start | bytes 9732096 | tf_op jit(solution)/shard_map/all_gather | solution.py:259
  8.2 21.3 %collective-permute-start = (bf16[96,384]{1,0:T(8,128)(2,1)S(1)}, bf16[96,384]{1,0:T(8,128)(2,1)S(1)}, u32[]{:S(2)}, u32[]{:S(2)}) collective-permute-start(bf16[96,384]{1,0:T(8,128)(2,1)S(1)} %constant_dynamic-slice_fusion), channel_id=1, source_target_pairs={{0,4},{4,0},{1,5},{5,1},{2,6},{6,2},{3,7},{7,3},{8,12},{12,8},{9,1... | collective-permute-start | bytes 221192 | tf_op jit(solution)/shard_map/ppermute | solution.py:27
  30.5 5.4 %copy-start.3 = (bf16[192,384]{1,0:T(8,128)(2,1)}, bf16[192,384]{1,0:T(8,128)(2,1)S(1)}, u32[]{:S(2)}) copy-start(bf16[192,384]{1,0:T(8,128)(2,1)S(1)} %pad_maximum_fusion.3.refs_0_) | copy-start | bytes 442372
  30.5 6.0 %collective-permute-start.1 = (bf16[192,384]{1,0:T(8,128)(2,1)S(1)}, bf16[192,384]{1,0:T(8,128)(2,1)}, u32[]{:S(2)}, u32[]{:S(2)}) collective-permute-start(bf16[192,384]{1,0:T(8,128)(2,1)S(1)} %pad_maximum_fusion.3.refs_0_), channel_id=1, source_target_pairs={{0,8},{8,16},{16,24},{24,32},{32,40},{40,48},{48,56},{56,64},{64,7... | collective-permute-start | bytes 442376 | tf_op jit(solution)/shard_map/ppermute | solution.py:38
  35.4 16.8 %copy-start.6 = (f32[1000]{0:T(1024)S(1)}, f32[1000]{0:T(1024)}, u32[]{:S(2)}) copy-start(f32[1000]{0:T(1024)} %param.17) | copy-start | bytes 12004
  36.4 6.9 %collective-permute-start.2 = (bf16[192,384]{1,0:T(8,128)(2,1)}, bf16[192,384]{1,0:T(8,128)(2,1)}, u32[]{:S(2)}, u32[]{:S(2)}) collective-permute-start(bf16[192,384]{1,0:T(8,128)(2,1)} %collective-permute-done.1.refs_1_), channel_id=1, source_target_pairs={{0,8},{8,16},{16,24},{24,32},{32,40},{40,48},{48,56},{56,64},{64,7... | collective-permute-start | bytes 442376 | tf_op jit(solution)/shard_map/ppermute | solution.py:38
  43.3 8.8 %collective-permute-start.3 = (bf16[192,384]{1,0:T(8,128)(2,1)}, bf16[192,384]{1,0:T(8,128)(2,1)}, u32[]{:S(2)}, u32[]{:S(2)}) collective-permute-start(bf16[192,384]{1,0:T(8,128)(2,1)} %collective-permute-done.2.refs_2_), channel_id=1, source_target_pairs={{0,8},{8,16},{16,24},{24,32},{32,40},{40,48},{48,56},{56,64},{64,7... | collective-permute-start | bytes 442376 | tf_op jit(solution)/shard_map/ppermute | solution.py:38
  53.5 8.8 %collective-permute-start.4 = (bf16[192,384]{1,0:T(8,128)(2,1)}, bf16[192,384]{1,0:T(8,128)(2,1)}, u32[]{:S(2)}, u32[]{:S(2)}) collective-permute-start(bf16[192,384]{1,0:T(8,128)(2,1)} %collective-permute-done.3.refs_3_), channel_id=1, source_target_pairs={{0,8},{8,16},{16,24},{24,32},{32,40},{40,48},{48,56},{56,64},{64,7... | collective-permute-start | bytes 442376 | tf_op jit(solution)/shard_map/ppermute | solution.py:38
  60.8 9.9 %copy-start.4 = (f32[3072]{0:T(1024)S(1)}, f32[3072]{0:T(1024)}, u32[]{:S(2)}) copy-start(f32[3072]{0:T(1024)} %param.20) | copy-start | bytes 36868
  62.4 8.4 %collective-permute-start.5 = (bf16[192,384]{1,0:T(8,128)(2,1)}, bf16[192,384]{1,0:T(8,128)(2,1)}, u32[]{:S(2)}, u32[]{:S(2)}) collective-permute-start(bf16[192,384]{1,0:T(8,128)(2,1)} %collective-permute-done.4.refs_4_), channel_id=1, source_target_pairs={{0,8},{8,16},{16,24},{24,32},{32,40},{40,48},{48,56},{56,64},{64,7... | collective-permute-start | bytes 442376 | tf_op jit(solution)/shard_map/ppermute | solution.py:38
  65.9 38.9 %all-to-all-start = ((bf16[4,720,384]{2,1,0:T(8,128)(2,1)}), bf16[4,720,384]{2,1,0:T(8,128)(2,1)}, u32[]{:S(2)}, u32[]{:S(2)}) async-start(bf16[4,720,384]{2,1,0:T(8,128)(2,1)} %pack.1), calls=%async_computation | async-start | bytes 4423680 | tf_op jit(solution)/shard_map/all_to_all | solution.py:316
  72.1 8.9 %collective-permute-start.6 = (bf16[192,384]{1,0:T(8,128)(2,1)}, bf16[192,384]{1,0:T(8,128)(2,1)S(1)}, u32[]{:S(2)}, u32[]{:S(2)}) collective-permute-start(bf16[192,384]{1,0:T(8,128)(2,1)} %collective-permute-done.5.refs_5_), channel_id=1, source_target_pairs={{0,8},{8,16},{16,24},{24,32},{32,40},{40,48},{48,56},{56,64},{64,7... | collective-permute-start | bytes 442376 | tf_op jit(solution)/shard_map/ppermute | solution.py:38
  78.7 15.9 %copy-start.7 = (s32[16]{0:T(128)S(1)}, s32[16]{0:T(128)}, u32[]{:S(2)}) copy-start(s32[16]{0:T(128)} %constant.60.clone) | copy-start | bytes 196
  81.0 8.2 %copy-start.1 = (bf16[192,384]{1,0:T(8,128)(2,1)}, bf16[192,384]{1,0:T(8,128)(2,1)S(1)}, u32[]{:S(2)}) copy-start(bf16[192,384]{1,0:T(8,128)(2,1)S(1)} %collective-permute-done.6.refs_6_) | copy-start | bytes 442372
  81.0 8.2 %collective-permute-start.7 = (bf16[192,384]{1,0:T(8,128)(2,1)S(1)}, bf16[192,384]{1,0:T(8,128)(2,1)S(1)}, u32[]{:S(2)}, u32[]{:S(2)}) collective-permute-start(bf16[192,384]{1,0:T(8,128)(2,1)S(1)} %collective-permute-done.6.refs_6_), channel_id=1, source_target_pairs={{0,8},{8,16},{16,24},{24,32},{32,40},{40,48},{48,56},{56,64},{64,7... | collective-permute-start | bytes 442376 | tf_op jit(solution)/shard_map/ppermute | solution.py:38
  86.4 14.7 %collective-permute-start.9 = (bf16[768,384]{1,0:T(8,128)(2,1)}, bf16[768,384]{1,0:T(8,128)(2,1)}, u32[]{:S(2)}, u32[]{:S(2)}) collective-permute-start(bf16[768,384]{1,0:T(8,128)(2,1)} %pad_maximum_fusion.1), channel_id=1, source_target_pairs={{0,4},{4,0},{1,5},{5,1},{2,6},{6,2},{3,7},{7,3},{8,12},{12,8},{9,1... | collective-permute-start | bytes 1769480 | tf_op jit(solution)/shard_map/ppermute | solution.py:27
  89.2 1.8 copy-start.2
  91.0 10.1 %collective-permute-start.10 = (bf16[576,384]{1,0:T(8,128)(2,1)}, bf16[576,384]{1,0:T(8,128)(2,1)}, u32[]{:S(2)}, u32[]{:S(2)}) collective-permute-start(bf16[576,384]{1,0:T(8,128)(2,1)} %pad_maximum_fusion.2), channel_id=1, source_target_pairs={{0,4},{4,0},{1,5},{5,1},{2,6},{6,2},{3,7},{7,3},{8,12},{12,8},{9,1... | collective-permute-start | bytes 1327112 | tf_op jit(solution)/shard_map/ppermute | solution.py:27
  94.7 6.4 %collective-permute-start.8 = (bf16[192,384]{1,0:T(8,128)(2,1)}, bf16[192,384]{1,0:T(8,128)(2,1)}, u32[]{:S(2)}, u32[]{:S(2)}) collective-permute-start(bf16[192,384]{1,0:T(8,128)(2,1)} %copy-done.2), channel_id=1, source_target_pairs={{0,8},{8,16},{16,24},{24,32},{32,40},{40,48},{48,56},{56,64},{64,7... | collective-permute-start | bytes 442376 | tf_op jit(solution)/shard_map/ppermute | solution.py:38
  114.7 14.3 %all-to-all-start.1 = ((bf16[4,256,384]{2,1,0:T(8,128)(2,1)}), bf16[4,256,384]{2,1,0:T(8,128)(2,1)}, u32[]{:S(2)}, u32[]{:S(2)}) async-start(bf16[4,256,384]{2,1,0:T(8,128)(2,1)} %attention.1), calls=%async_computation.1 | async-start | bytes 1572864 | tf_op jit(solution)/shard_map/all_to_all | solution.py:320
  137.6 35.4 %copy-start.5 = (f32[256,64]{0,1:T(8,128)S(1)}, f32[256,64]{0,1:T(8,128)}, u32[]{:S(2)}) copy-start(f32[256,64]{0,1:T(8,128)} %param.15) | copy-start | bytes 196612
  138.8 4.3 %collective-permute-start.11 = (bf16[64,256]{1,0:T(8,128)(2,1)S(1)}, bf16[64,256]{1,0:T(8,128)(2,1)S(1)}, u32[]{:S(2)}, u32[]{:S(2)}) collective-permute-start(bf16[64,256]{1,0:T(8,128)(2,1)S(1)} %get-tuple-element.61), channel_id=1, source_target_pairs={{0,4},{4,0},{1,5},{5,1},{2,6},{6,2},{3,7},{7,3},{8,12},{12,8},{9,1... | collective-permute-start | bytes 98312 | tf_op jit(solution)/shard_map/ppermute | solution.py:27
  143.1 2.7 %collective-permute-start.12 = (bf16[64,256]{1,0:T(8,128)(2,1)S(1)}, bf16[64,256]{1,0:T(8,128)(2,1)S(1)}, u32[]{:S(2)}, u32[]{:S(2)}) collective-permute-start(bf16[64,256]{1,0:T(8,128)(2,1)S(1)} %fusion.13), channel_id=1, source_target_pairs={{0,8},{8,16},{16,24},{24,32},{32,40},{40,48},{48,56},{56,64},{64,7... | collective-permute-start | bytes 98312 | tf_op jit(solution)/shard_map/ppermute | solution.py:23
  145.8 4.6 %collective-permute-start.13 = (bf16[64,256]{1,0:T(8,128)(2,1)S(1)}, bf16[64,256]{1,0:T(8,128)(2,1)S(1)}, u32[]{:S(2)}, u32[]{:S(2)}) collective-permute-start(bf16[64,256]{1,0:T(8,128)(2,1)S(1)} %fusion.10), channel_id=1, source_target_pairs={{0,16},{8,24},{16,32},{24,40},{32,48},{40,56},{48,64},{56,72},{64,... | collective-permute-start | bytes 98312 | tf_op jit(solution)/shard_map/ppermute | solution.py:23
  150.4 10.7 %collective-permute-start.14 = (bf16[64,256]{1,0:T(8,128)(2,1)S(1)}, bf16[64,256]{1,0:T(8,128)(2,1)S(1)}, u32[]{:S(2)}, u32[]{:S(2)}) collective-permute-start(bf16[64,256]{1,0:T(8,128)(2,1)S(1)} %add_convert_fusion), channel_id=1, source_target_pairs={{0,32},{8,40},{16,48},{24,56},{32,64},{40,72},{48,80},{56,88},{64,... | collective-permute-start | bytes 98312 | tf_op jit(solution)/shard_map/ppermute | solution.py:38
  161.1 0.7 collective-permute-start.15
  161.8 11.2 %collective-permute-start.16 = (bf16[64,256]{1,0:T(8,128)(2,1)S(1)}, bf16[64,256]{1,0:T(8,128)(2,1)S(1)}, u32[]{:S(2)}, u32[]{:S(2)}) collective-permute-start(bf16[64,256]{1,0:T(8,128)(2,1)S(1)} %fusion.11), channel_id=1, source_target_pairs={{0,4},{4,0},{1,5},{5,1},{2,6},{6,2},{3,7},{7,3},{8,12},{12,8},{9,1... | collective-permute-start | bytes 98312 | tf_op jit(solution)/shard_map/ppermute | solution.py:27
Sparse Core Ops, SparseCore 0:
  9.2 99.1 all-gather.1

commit v7 on v6

--- a/solution.py
+++ b/solution.py
@@ -12,6 +12,7 @@
 HEAD = 128
 CORES = 2
 EXTRA = 16
+GATHER_AFTER = 2
 STEP = ("chip", "core")
 REP_STEP = ("rep", "chip", "core")
 epsilon = 1e-06
@@ -256,7 +257,6 @@
 
     core = lax.axis_index("core")
 
-    all_out_weight = lax.all_gather(out_weight, STEP, axis=0, tiled=True)
 
     def embed(latent, embed_weight, embed_bias):
         hidden = lax.dot_general(
@@ -313,6 +313,8 @@
     piece = [jnp.where(core == 0, my_columns, other), jnp.where(core == 0, other, my_columns)]
     own, swapped, done = pass_round(jnp.concatenate(piece), tasks)
     hidden, (modulate, delta), source = done[1][0], done[4], done[6]
+    _, late = lax.optimization_barrier((own[GATHER_AFTER], out_weight))
+    all_out_weight = lax.all_gather(late, STEP, axis=0, tiled=True)
     packed = lax.all_to_all(done[2], "patch", 0, 0, tiled=True)
 
     project = project_latents(source, own, swapped)

time: 182 us -> 177 us (0.973)
  waiting for transfers between devices: 31.1 us -> 23.9 us
  starting transfers between devices: 85.4 us -> 88.3 us
    ppermute x10, waiting for transfers between devices: 16.4 us -> 10.4 us  [send_by_core(): return lax.ppermute(value, ('chip', 'core'), pairs)]
    ppermute x5, starting transfers between devices: 37.8 us -> 43.6 us  [swap_cores(): return lax.ppermute(value, 'core', [(0, 1), (1, 0)])]
    ppermute x10, starting transfers between devices: 33.4 us -> 30.4 us  [send_by_core(): return lax.ppermute(value, ('chip', 'core'), pairs)]
  transfers between devices with their start and end apart: 20 -> 20, of which waited for: 14 -> 11; matrix products, arithmetic and copies ran while one was open for 12% -> 11% of each run, Pallas kernels for 10% -> 10%
where the time goes in v7:
time: 177 us; the launch traced here: 176 us
  starting transfers between devices  88.3 us (50%)
  waiting for transfers between devices  23.9 us (14%)
  Pallas kernels  17.6 us (10%)
  between operations  16.8 us (9%)
  other arithmetic  14.1 us (8%)
  matrix products  11.5 us (6%)
  local copies, waits for them, and re-layouts  4.08 us (2%)
    ppermute x5, starting transfers between devices, swap_cores(): return lax.ppermute(value, 'core', [(0, 1), (1, 0)])  43.6 us
    ppermute x10, starting transfers between devices, send_by_core(): return lax.ppermute(value, ('chip', 'core'), pairs)  30.4 us
    ppermute x10, waiting for transfers between devices, send_by_core(): return lax.ppermute(value, ('chip', 'core'), pairs)  10.4 us
    pallas_call x1, Pallas kernels, attention(): pl.pallas_call(functools.partial(attention_body, parts, rows, tile), grid...  9.96 us
    all_to_all x1, waiting for transfers between devices, per_device(): attended = lax.all_to_all(attended, 'patch', 0, 0, tiled=True)  8.78 us
    dot_general x1, matrix products, per_device(): lax.dot_general(attended, all_out_weight, (((1,), (1,)), ((), ())), prefe...  5.47 us
    ppermute x2, starting transfers between devices, shift(): return lax.ppermute(value, axis, pairs)  5.41 us
    all_to_all x1, starting transfers between devices, per_device(): packed = lax.all_to_all(done[2], 'patch', 0, 0, tiled=True)  4.63 us
  transfers between devices with their start and end apart: 20, of which 11 were waited for; matrix products, arithmetic and copies ran while one was open for 11% of the time, Pallas kernels for 10%

profile of v7, /device:TPU:33, one launch (start us, length us, event | category | flops | bytes accessed | tf_op | source)
XLA Modules:
  0.0 176.3 jit_solution(5670575327398660390)
XLA Ops:
  6.6 0.9 constant_dynamic-slice_fusion
  7.5 20.4 %collective-permute-start = (bf16[96,384]{1,0:T(8,128)(2,1)S(1)}, bf16[96,384]{1,0:T(8,128)(2,1)S(1)}, u32[]{:S(2)}, u32[]{:S(2)}) collective-permute-start(bf16[96,384]{1,0:T(8,128)(2,1)S(1)} %constant_dynamic-slice_fusion), channel_id=1, source_target_pairs={{0,4},{4,0},{1,5},{5,1},{2,6},{6,2},{3,7},{7,3},{8,12},{12,8},{9,1... | collective-permute-start | bytes 221192 | tf_op jit(solution)/shard_map/ppermute | solution.py:28
  27.9 0.9 collective-permute-done
  28.8 0.9 broadcast_select_fusion.1
  29.8 3.2 %collective-permute-start.1 = (bf16[192,384]{1,0:T(8,128)(2,1)S(1)}, bf16[192,384]{1,0:T(8,128)(2,1)}, u32[]{:S(2)}, u32[]{:S(2)}) collective-permute-start(bf16[192,384]{1,0:T(8,128)(2,1)S(1)} %pad_maximum_fusion.3.refs_0_), channel_id=1, source_target_pairs={{0,8},{8,16},{16,24},{24,32},{32,40},{40,48},{48,56},{56,64},{64,7... | collective-permute-start | bytes 442376 | tf_op jit(solution)/shard_map/ppermute | solution.py:39
  33.0 1.7 fusion.19
  34.7 0.0 copy-start.6
  34.7 0.5 multiply_reduce_fusion.1
  35.2 0.6 add_sqrt_fusion
  35.7 2.6 %collective-permute-start.2 = (bf16[192,384]{1,0:T(8,128)(2,1)}, bf16[192,384]{1,0:T(8,128)(2,1)}, u32[]{:S(2)}, u32[]{:S(2)}) collective-permute-start(bf16[192,384]{1,0:T(8,128)(2,1)} %collective-permute-done.1.refs_1_), channel_id=1, source_target_pairs={{0,8},{8,16},{16,24},{24,32},{32,40},{40,48},{48,56},{56,64},{64,7... | collective-permute-start | bytes 442376 | tf_op jit(solution)/shard_map/ppermute | solution.py:39
  38.3 3.9 %pack.1 = bf16[4,720,384]{2,1,0:T(8,128)(2,1)} custom-call(bf16[320,1536]{1,0:T(8,128)(2,1)} %bitcast.37, bf16[320,1536]{1,0:T(8,128)(2,1)} %bitcast.38, f32[64,256]{1,0:T(8,128)} %bitcast.41, f32[1,256]{1,0:T(1,128)} %bitcast.47), custom_call_target="tpu_custom_call" | custom-call | flops 1105920 | bytes 4423680 | tf_op jit(solution)/shard_map/pack/pallas_call | solution.py:149
  42.2 0.1 all-gather.2.cloned.1.call-update
  42.3 1.7 collective-permute-start.3
  44.7 2.1 %collective-permute-done.3.refs_3_ = bf16[192,384]{1,0:T(8,128)(2,1)} collective-permute-done((bf16[192,384]{1,0:T(8,128)(2,1)}, bf16[192,384]{1,0:T(8,128)(2,1)}, u32[]{:S(2)}, u32[]{:S(2)}) %collective-permute-start.3) | collective-permute-done | bytes 147488 | tf_op jit(solution)/shard_map/ppermute | solution.py:39
  46.7 0.7 select_reduce_fusion
  48.1 2.9 %collective-permute-start.4 = (bf16[192,384]{1,0:T(8,128)(2,1)}, bf16[192,384]{1,0:T(8,128)(2,1)}, u32[]{:S(2)}, u32[]{:S(2)}) collective-permute-start(bf16[192,384]{1,0:T(8,128)(2,1)} %collective-permute-done.3.refs_3_), channel_id=1, source_target_pairs={{0,8},{8,16},{16,24},{24,32},{32,40},{40,48},{48,56},{56,64},{64,7... | collective-permute-start | bytes 442376 | tf_op jit(solution)/shard_map/ppermute | solution.py:39
  51.0 3.7 %fusion.20 = f32[1,9216]{1,0:T(1,128)} fusion(bf16[256,1]{0,1:T(2,128)(2,1)S(1)} %reshape.58, bf16[256,9216]{1,0:T(8,128)(2,1)} %param.18), kind=kOutput, calls=%fused_computation.60 | convolution fusion | flops 4718592 | bytes 4755968 | tf_op jit(solution)/shard_map/dot_general | solution.py:278
  55.9 0.0 collective-permute-done.4.refs_4_
  55.9 3.1 %collective-permute-start.5 = (bf16[192,384]{1,0:T(8,128)(2,1)}, bf16[192,384]{1,0:T(8,128)(2,1)}, u32[]{:S(2)}, u32[]{:S(2)}) collective-permute-start(bf16[192,384]{1,0:T(8,128)(2,1)} %collective-permute-done.4.refs_4_), channel_id=1, source_target_pairs={{0,8},{8,16},{16,24},{24,32},{32,40},{40,48},{48,56},{56,64},{64,7... | collective-permute-start | bytes 442376 | tf_op jit(solution)/shard_map/ppermute | solution.py:39
  59.0 0.1 pad.12.clone
  59.1 4.6 %all-to-all-start = ((bf16[4,720,384]{2,1,0:T(8,128)(2,1)}), bf16[4,720,384]{2,1,0:T(8,128)(2,1)}, u32[]{:S(2)}, u32[]{:S(2)}) async-start(bf16[4,720,384]{2,1,0:T(8,128)(2,1)} %pack.1), calls=%async_computation | async-start | bytes 4423680 | tf_op jit(solution)/shard_map/all_to_all | solution.py:318
  63.7 0.2 collective-permute-done.5.refs_5_
  63.9 0.7 reduce_sum.77
  65.3 3.5 %collective-permute-start.6 = (bf16[192,384]{1,0:T(8,128)(2,1)}, bf16[192,384]{1,0:T(8,128)(2,1)S(1)}, u32[]{:S(2)}, u32[]{:S(2)}) collective-permute-start(bf16[192,384]{1,0:T(8,128)(2,1)} %collective-permute-done.5.refs_5_), channel_id=1, source_target_pairs={{0,8},{8,16},{16,24},{24,32},{32,40},{40,48},{48,56},{56,64},{64,7... | collective-permute-start | bytes 442376 | tf_op jit(solution)/shard_map/ppermute | solution.py:39
  68.8 1.2 convert_reduce_fusion
  70.0 0.7 slice_add_fusion
  70.7 1.1 convert_subtract_fusion
  71.8 0.1 maximum_multiply_fusion
  71.9 0.0 copy-start.7
  71.9 0.2 subtract_convert_fusion
  72.1 0.1 fusion.3
  72.2 1.0 pad_maximum_fusion.source_ref
  73.3 0.7 collective-permute-done.6.refs_6_
  74.0 3.4 %collective-permute-start.7 = (bf16[192,384]{1,0:T(8,128)(2,1)S(1)}, bf16[192,384]{1,0:T(8,128)(2,1)S(1)}, u32[]{:S(2)}, u32[]{:S(2)}) collective-permute-start(bf16[192,384]{1,0:T(8,128)(2,1)S(1)} %collective-permute-done.6.refs_6_), channel_id=1, source_target_pairs={{0,8},{8,16},{16,24},{24,32},{32,40},{40,48},{48,56},{56,64},{64,7... | collective-permute-start | bytes 442376 | tf_op jit(solution)/shard_map/ppermute | solution.py:39
  77.4 2.0 %pad_maximum_fusion.1 = bf16[768,384]{1,0:T(8,128)(2,1)} fusion(bf16[192,384]{1,0:T(8,128)(2,1)} %collective-permute-done.4.refs_4_, bf16[192,384]{1,0:T(8,128)(2,1)} %collective-permute-done.3.refs_3_, bf16[192,384]{1,0:T(8,128)(2,1)} %collective-permute-done.2.refs_2_, bf16[192,384]{1,0:T(8,128)(2,1)} %collective-permute-done.1.refs_1_), kind=kLoop, calls=%fused_computation.15 | loop fusion | flops 2359296 | bytes 1179648 | tf_op jit(solution)/shard_map/concatenate | solution.py:58
  79.4 3.3 %collective-permute-start.9 = (bf16[768,384]{1,0:T(8,128)(2,1)}, bf16[768,384]{1,0:T(8,128)(2,1)}, u32[]{:S(2)}, u32[]{:S(2)}) collective-permute-start(bf16[768,384]{1,0:T(8,128)(2,1)} %pad_maximum_fusion.1), channel_id=1, source_target_pairs={{0,4},{4,0},{1,5},{5,1},{2,6},{6,2},{3,7},{7,3},{8,12},{12,8},{9,1... | collective-permute-start | bytes 1769480 | tf_op jit(solution)/shard_map/ppermute | solution.py:28
  82.7 1.8 %pad_maximum_fusion.2 = bf16[576,384]{1,0:T(8,128)(2,1)} fusion(bf16[192,384]{1,0:T(8,128)(2,1)S(1)} %collective-permute-done.7.refs_7_, bf16[192,384]{1,0:T(8,128)(2,1)S(1)} %collective-permute-done.6.refs_6_, bf16[192,384]{1,0:T(8,128)(2,1)} %collective-permute-done.5.refs_5_), kind=kLoop, calls=%fused_computation.16 | loop fusion | flops 1327104 | bytes 884736 | tf_op jit(solution)/shard_map/concatenate | solution.py:58
  84.5 5.8 %collective-permute-start.10 = (bf16[576,384]{1,0:T(8,128)(2,1)}, bf16[576,384]{1,0:T(8,128)(2,1)}, u32[]{:S(2)}, u32[]{:S(2)}) collective-permute-start(bf16[576,384]{1,0:T(8,128)(2,1)} %pad_maximum_fusion.2), channel_id=1, source_target_pairs={{0,4},{4,0},{1,5},{5,1},{2,6},{6,2},{3,7},{7,3},{8,12},{12,8},{9,1... | collective-permute-start | bytes 1327112 | tf_op jit(solution)/shard_map/ppermute | solution.py:28
  90.3 0.0 collective-permute-start.8
  90.3 0.6 compare_select_fusion.place_ref
  90.9 6.3 %collective-permute-done.8.refs_8_ = bf16[192,384]{1,0:T(8,128)(2,1)} collective-permute-done((bf16[192,384]{1,0:T(8,128)(2,1)}, bf16[192,384]{1,0:T(8,128)(2,1)}, u32[]{:S(2)}, u32[]{:S(2)}) %collective-permute-start.8) | collective-permute-done | bytes 147488 | tf_op jit(solution)/shard_map/ppermute | solution.py:39
  97.1 3.7 %project.1.project_ref = bf16[3,160,256]{2,1,0:T(8,128)(2,1)} custom-call(s32[16]{0:T(128)} %compare_select_fusion.place_ref, bf16[160,3072]{1,0:T(8,128)(2,1)} %pad_maximum_fusion.source_ref, bf16[192,384]{1,0:T(8,128)(2,1)} %copy-done.3, bf16[192,384]{1,0:T(8,128)(2,1)} %collective-permute-done.1.refs_1_, bf16[192,384]{1,0:T(8,128)(2,1)} %collective-permute-done.2.refs_2_, ...), custom_call_target="tpu_custom_call" | custom-call | flops 377487360 | bytes 5701632 | tf_op jit(solution)/shard_map/project/pallas_call | solution.py:101
  100.8 10.0 %attention.1 = bf16[4,256,384]{2,1,0:T(8,128)(2,1)} custom-call(bf16[4,720,384]{2,1,0:T(8,128)(2,1)} %all-to-all-done.packed_ref, bf16[3,160,256]{2,1,0:T(8,128)(2,1)} %project.1.project_ref, f32[1,128]{1,0:T(1,128)} %bitcast.48), custom_call_target="tpu_custom_call" | custom-call | flops 2013265920 | bytes 4325376 | tf_op jit(solution)/shard_map/attention/pallas_call | solution.py:203
  110.8 4.3 %all-to-all-start.1 = ((bf16[4,256,384]{2,1,0:T(8,128)(2,1)}), bf16[4,256,384]{2,1,0:T(8,128)(2,1)}, u32[]{:S(2)}, u32[]{:S(2)}) async-start(bf16[4,256,384]{2,1,0:T(8,128)(2,1)} %attention.1), calls=%async_computation.1 | async-start | bytes 1572864 | tf_op jit(solution)/shard_map/all_to_all | solution.py:322
  115.1 0.7 slice.9
  115.8 8.8 %all-to-all-done.1 = bf16[4,256,384]{2,1,0:T(8,128)(2,1)} async-done(((bf16[4,256,384]{2,1,0:T(8,128)(2,1)}), bf16[4,256,384]{2,1,0:T(8,128)(2,1)}, u32[]{:S(2)}, u32[]{:S(2)}) %all-to-all-start.1) | async-done | bytes 786464 | tf_op jit(solution)/shard_map/all_to_all | solution.py:322
  124.6 2.3 %copy.15 = bf16[256,4,384]{0,2,1:T(8,128)(2,1)} copy(bf16[256,4,384]{2,0,1:T(8,128)(2,1)} %bitcast.12) | data formatting | bytes 1572864 | tf_op jit(solution)/shard_map/transpose | solution.py:323
  126.9 5.5 %fusion.21 = f32[256,3072]{1,0:T(8,128)S(1)} fusion(bf16[256,1536]{0,1:T(8,128)(2,1)} %bitcast.39, bf16[3072,1536]{1,0:T(8,128)(2,1)} %all-gather.2.cloned.1.call-done), kind=kOutput, calls=%fused_computation.61 | convolution fusion | flops 2415919104 | bytes 13369344 | tf_op jit(solution)/shard_map/dot_general | solution.py:324
  132.3 0.8 fusion.18
  133.1 0.0 copy-start.5
  133.2 0.5 multiply_reduce_fusion
  133.6 0.7 bitcast_convert_fusion
  134.3 3.9 %collective-permute-start.11 = (bf16[64,256]{1,0:T(8,128)(2,1)S(1)}, bf16[64,256]{1,0:T(8,128)(2,1)S(1)}, u32[]{:S(2)}, u32[]{:S(2)}) collective-permute-start(bf16[64,256]{1,0:T(8,128)(2,1)S(1)} %get-tuple-element.63), channel_id=1, source_target_pairs={{0,4},{4,0},{1,5},{5,1},{2,6},{6,2},{3,7},{7,3},{8,12},{12,8},{9,1... | collective-permute-start | bytes 98312 | tf_op jit(solution)/shard_map/ppermute | solution.py:28
  138.2 0.9 collective-permute-done.11
  139.1 2.0 %collective-permute-start.12 = (bf16[64,256]{1,0:T(8,128)(2,1)S(1)}, bf16[64,256]{1,0:T(8,128)(2,1)S(1)}, u32[]{:S(2)}, u32[]{:S(2)}) collective-permute-start(bf16[64,256]{1,0:T(8,128)(2,1)S(1)} %fusion.13), channel_id=1, source_target_pairs={{0,8},{8,16},{16,24},{24,32},{32,40},{40,48},{48,56},{56,64},{64,7... | collective-permute-start | bytes 98312 | tf_op jit(solution)/shard_map/ppermute | solution.py:24
  141.1 1.0 collective-permute-done.12
  142.1 3.4 %collective-permute-start.13 = (bf16[64,256]{1,0:T(8,128)(2,1)S(1)}, bf16[64,256]{1,0:T(8,128)(2,1)S(1)}, u32[]{:S(2)}, u32[]{:S(2)}) collective-permute-start(bf16[64,256]{1,0:T(8,128)(2,1)S(1)} %fusion.10), channel_id=1, source_target_pairs={{0,16},{8,24},{16,32},{24,40},{32,48},{40,56},{48,64},{56,72},{64,... | collective-permute-start | bytes 98312 | tf_op jit(solution)/shard_map/ppermute | solution.py:24
  145.5 1.0 collective-permute-done.13
  146.6 9.4 %collective-permute-start.14 = (bf16[64,256]{1,0:T(8,128)(2,1)S(1)}, bf16[64,256]{1,0:T(8,128)(2,1)S(1)}, u32[]{:S(2)}, u32[]{:S(2)}) collective-permute-start(bf16[64,256]{1,0:T(8,128)(2,1)S(1)} %add_convert_fusion), channel_id=1, source_target_pairs={{0,32},{8,40},{16,48},{24,56},{32,64},{40,72},{48,80},{56,88},{64,... | collective-permute-start | bytes 98312 | tf_op jit(solution)/shard_map/ppermute | solution.py:39
  155.9 1.2 collective-permute-done.14
  157.1 0.7 collective-permute-start.15
  157.8 10.1 %collective-permute-start.16 = (bf16[64,256]{1,0:T(8,128)(2,1)S(1)}, bf16[64,256]{1,0:T(8,128)(2,1)S(1)}, u32[]{:S(2)}, u32[]{:S(2)}) collective-permute-start(bf16[64,256]{1,0:T(8,128)(2,1)S(1)} %fusion.11), channel_id=1, source_target_pairs={{0,4},{4,0},{1,5},{5,1},{2,6},{6,2},{3,7},{7,3},{8,12},{12,8},{9,1... | collective-permute-start | bytes 98312 | tf_op jit(solution)/shard_map/ppermute | solution.py:28
  167.9 0.9 collective-permute-done.16
  168.8 0.7 fusion.9
  (36 shorter events, 0.2 us)
Async XLA Ops:
  6.5 127.1 %copy-start = (bf16[3072,64]{0,1:T(8,128)(2,1)S(1)}, bf16[3072,64]{0,1:T(8,128)(2,1)}, u32[]{:S(2)}) copy-start(bf16[3072,64]{0,1:T(8,128)(2,1)} %param.26) | copy-start | bytes 1179652
  6.6 120.3 %all-gather.2.cloned.1.call-start = ((), (), s32[]{:S(2)}) async-start(), calls=%async_computation.2 | async-start | bytes 9732096 | tf_op jit(solution)/shard_map/all_gather | solution.py:317
  7.5 21.3 %collective-permute-start = (bf16[96,384]{1,0:T(8,128)(2,1)S(1)}, bf16[96,384]{1,0:T(8,128)(2,1)S(1)}, u32[]{:S(2)}, u32[]{:S(2)}) collective-permute-start(bf16[96,384]{1,0:T(8,128)(2,1)S(1)} %constant_dynamic-slice_fusion), channel_id=1, source_target_pairs={{0,4},{4,0},{1,5},{5,1},{2,6},{6,2},{3,7},{7,3},{8,12},{12,8},{9,1... | collective-permute-start | bytes 221192 | tf_op jit(solution)/shard_map/ppermute | solution.py:28
  29.8 5.4 %copy-start.3 = (bf16[192,384]{1,0:T(8,128)(2,1)}, bf16[192,384]{1,0:T(8,128)(2,1)S(1)}, u32[]{:S(2)}) copy-start(bf16[192,384]{1,0:T(8,128)(2,1)S(1)} %pad_maximum_fusion.3.refs_0_) | copy-start | bytes 442372
  29.8 6.0 %collective-permute-start.1 = (bf16[192,384]{1,0:T(8,128)(2,1)S(1)}, bf16[192,384]{1,0:T(8,128)(2,1)}, u32[]{:S(2)}, u32[]{:S(2)}) collective-permute-start(bf16[192,384]{1,0:T(8,128)(2,1)S(1)} %pad_maximum_fusion.3.refs_0_), channel_id=1, source_target_pairs={{0,8},{8,16},{16,24},{24,32},{32,40},{40,48},{48,56},{56,64},{64,7... | collective-permute-start | bytes 442376 | tf_op jit(solution)/shard_map/ppermute | solution.py:39
  34.7 12.1 %copy-start.6 = (f32[1000]{0:T(1024)S(1)}, f32[1000]{0:T(1024)}, u32[]{:S(2)}) copy-start(f32[1000]{0:T(1024)} %param.17) | copy-start | bytes 12004
  35.7 6.5 %collective-permute-start.2 = (bf16[192,384]{1,0:T(8,128)(2,1)}, bf16[192,384]{1,0:T(8,128)(2,1)}, u32[]{:S(2)}, u32[]{:S(2)}) collective-permute-start(bf16[192,384]{1,0:T(8,128)(2,1)} %collective-permute-done.1.refs_1_), channel_id=1, source_target_pairs={{0,8},{8,16},{16,24},{24,32},{32,40},{40,48},{48,56},{56,64},{64,7... | collective-permute-start | bytes 442376 | tf_op jit(solution)/shard_map/ppermute | solution.py:39
  42.3 4.4 %collective-permute-start.3 = (bf16[192,384]{1,0:T(8,128)(2,1)}, bf16[192,384]{1,0:T(8,128)(2,1)}, u32[]{:S(2)}, u32[]{:S(2)}) collective-permute-start(bf16[192,384]{1,0:T(8,128)(2,1)} %collective-permute-done.2.refs_2_), channel_id=1, source_target_pairs={{0,8},{8,16},{16,24},{24,32},{32,40},{40,48},{48,56},{56,64},{64,7... | collective-permute-start | bytes 442376 | tf_op jit(solution)/shard_map/ppermute | solution.py:39
  48.1 7.8 %collective-permute-start.4 = (bf16[192,384]{1,0:T(8,128)(2,1)}, bf16[192,384]{1,0:T(8,128)(2,1)}, u32[]{:S(2)}, u32[]{:S(2)}) collective-permute-start(bf16[192,384]{1,0:T(8,128)(2,1)} %collective-permute-done.3.refs_3_), channel_id=1, source_target_pairs={{0,8},{8,16},{16,24},{24,32},{32,40},{40,48},{48,56},{56,64},{64,7... | collective-permute-start | bytes 442376 | tf_op jit(solution)/shard_map/ppermute | solution.py:39
  54.7 9.2 %copy-start.4 = (f32[3072]{0:T(1024)S(1)}, f32[3072]{0:T(1024)}, u32[]{:S(2)}) copy-start(f32[3072]{0:T(1024)} %param.20) | copy-start | bytes 36868
  55.9 8.0 %collective-permute-start.5 = (bf16[192,384]{1,0:T(8,128)(2,1)}, bf16[192,384]{1,0:T(8,128)(2,1)}, u32[]{:S(2)}, u32[]{:S(2)}) collective-permute-start(bf16[192,384]{1,0:T(8,128)(2,1)} %collective-permute-done.4.refs_4_), channel_id=1, source_target_pairs={{0,8},{8,16},{16,24},{24,32},{32,40},{40,48},{48,56},{56,64},{64,7... | collective-permute-start | bytes 442376 | tf_op jit(solution)/shard_map/ppermute | solution.py:39
  59.1 41.7 %all-to-all-start = ((bf16[4,720,384]{2,1,0:T(8,128)(2,1)}), bf16[4,720,384]{2,1,0:T(8,128)(2,1)}, u32[]{:S(2)}, u32[]{:S(2)}) async-start(bf16[4,720,384]{2,1,0:T(8,128)(2,1)} %pack.1), calls=%async_computation | async-start | bytes 4423680 | tf_op jit(solution)/shard_map/all_to_all | solution.py:318
  65.3 8.7 %collective-permute-start.6 = (bf16[192,384]{1,0:T(8,128)(2,1)}, bf16[192,384]{1,0:T(8,128)(2,1)S(1)}, u32[]{:S(2)}, u32[]{:S(2)}) collective-permute-start(bf16[192,384]{1,0:T(8,128)(2,1)} %collective-permute-done.5.refs_5_), channel_id=1, source_target_pairs={{0,8},{8,16},{16,24},{24,32},{32,40},{40,48},{48,56},{56,64},{64,7... | collective-permute-start | bytes 442376 | tf_op jit(solution)/shard_map/ppermute | solution.py:39
  71.9 18.4 %copy-start.7 = (s32[16]{0:T(128)S(1)}, s32[16]{0:T(128)}, u32[]{:S(2)}) copy-start(s32[16]{0:T(128)} %constant.60.clone) | copy-start | bytes 196
  74.0 8.7 %copy-start.1 = (bf16[192,384]{1,0:T(8,128)(2,1)}, bf16[192,384]{1,0:T(8,128)(2,1)S(1)}, u32[]{:S(2)}) copy-start(bf16[192,384]{1,0:T(8,128)(2,1)S(1)} %collective-permute-done.6.refs_6_) | copy-start | bytes 442372
  74.0 8.7 %collective-permute-start.7 = (bf16[192,384]{1,0:T(8,128)(2,1)S(1)}, bf16[192,384]{1,0:T(8,128)(2,1)S(1)}, u32[]{:S(2)}, u32[]{:S(2)}) collective-permute-start(bf16[192,384]{1,0:T(8,128)(2,1)S(1)} %collective-permute-done.6.refs_6_), channel_id=1, source_target_pairs={{0,8},{8,16},{16,24},{24,32},{32,40},{40,48},{48,56},{56,64},{64,7... | collective-permute-start | bytes 442376 | tf_op jit(solution)/shard_map/ppermute | solution.py:39
  79.4 17.8 %collective-permute-start.9 = (bf16[768,384]{1,0:T(8,128)(2,1)}, bf16[768,384]{1,0:T(8,128)(2,1)}, u32[]{:S(2)}, u32[]{:S(2)}) collective-permute-start(bf16[768,384]{1,0:T(8,128)(2,1)} %pad_maximum_fusion.1), channel_id=1, source_target_pairs={{0,4},{4,0},{1,5},{5,1},{2,6},{6,2},{3,7},{7,3},{8,12},{12,8},{9,1... | collective-permute-start | bytes 1769480 | tf_op jit(solution)/shard_map/ppermute | solution.py:28
  82.7 1.8 %copy-start.2 = (bf16[192,384]{1,0:T(8,128)(2,1)}, bf16[192,384]{1,0:T(8,128)(2,1)S(1)}, u32[]{:S(2)}) copy-start(bf16[192,384]{1,0:T(8,128)(2,1)S(1)} %collective-permute-done.7.refs_7_) | copy-start | bytes 442372
  84.5 12.7 %collective-permute-start.10 = (bf16[576,384]{1,0:T(8,128)(2,1)}, bf16[576,384]{1,0:T(8,128)(2,1)}, u32[]{:S(2)}, u32[]{:S(2)}) collective-permute-start(bf16[576,384]{1,0:T(8,128)(2,1)} %pad_maximum_fusion.2), channel_id=1, source_target_pairs={{0,4},{4,0},{1,5},{5,1},{2,6},{6,2},{3,7},{7,3},{8,12},{12,8},{9,1... | collective-permute-start | bytes 1327112 | tf_op jit(solution)/shard_map/ppermute | solution.py:28
  90.3 6.8 %collective-permute-start.8 = (bf16[192,384]{1,0:T(8,128)(2,1)}, bf16[192,384]{1,0:T(8,128)(2,1)}, u32[]{:S(2)}, u32[]{:S(2)}) collective-permute-start(bf16[192,384]{1,0:T(8,128)(2,1)} %copy-done.2), channel_id=1, source_target_pairs={{0,8},{8,16},{16,24},{24,32},{32,40},{40,48},{48,56},{56,64},{64,7... | collective-permute-start | bytes 442376 | tf_op jit(solution)/shard_map/ppermute | solution.py:39
  110.8 13.8 %all-to-all-start.1 = ((bf16[4,256,384]{2,1,0:T(8,128)(2,1)}), bf16[4,256,384]{2,1,0:T(8,128)(2,1)}, u32[]{:S(2)}, u32[]{:S(2)}) async-start(bf16[4,256,384]{2,1,0:T(8,128)(2,1)} %attention.1), calls=%async_computation.1 | async-start | bytes 1572864 | tf_op jit(solution)/shard_map/all_to_all | solution.py:322
  133.1 35.6 %copy-start.5 = (f32[256,64]{0,1:T(8,128)S(1)}, f32[256,64]{0,1:T(8,128)}, u32[]{:S(2)}) copy-start(f32[256,64]{0,1:T(8,128)} %param.15) | copy-start | bytes 196612
  134.3 4.7 %collective-permute-start.11 = (bf16[64,256]{1,0:T(8,128)(2,1)S(1)}, bf16[64,256]{1,0:T(8,128)(2,1)S(1)}, u32[]{:S(2)}, u32[]{:S(2)}) collective-permute-start(bf16[64,256]{1,0:T(8,128)(2,1)S(1)} %get-tuple-element.63), channel_id=1, source_target_pairs={{0,4},{4,0},{1,5},{5,1},{2,6},{6,2},{3,7},{7,3},{8,12},{12,8},{9,1... | collective-permute-start | bytes 98312 | tf_op jit(solution)/shard_map/ppermute | solution.py:28
  139.1 3.0 %collective-permute-start.12 = (bf16[64,256]{1,0:T(8,128)(2,1)S(1)}, bf16[64,256]{1,0:T(8,128)(2,1)S(1)}, u32[]{:S(2)}, u32[]{:S(2)}) collective-permute-start(bf16[64,256]{1,0:T(8,128)(2,1)S(1)} %fusion.13), channel_id=1, source_target_pairs={{0,8},{8,16},{16,24},{24,32},{32,40},{40,48},{48,56},{56,64},{64,7... | collective-permute-start | bytes 98312 | tf_op jit(solution)/shard_map/ppermute | solution.py:24
  142.1 4.4 %collective-permute-start.13 = (bf16[64,256]{1,0:T(8,128)(2,1)S(1)}, bf16[64,256]{1,0:T(8,128)(2,1)S(1)}, u32[]{:S(2)}, u32[]{:S(2)}) collective-permute-start(bf16[64,256]{1,0:T(8,128)(2,1)S(1)} %fusion.10), channel_id=1, source_target_pairs={{0,16},{8,24},{16,32},{24,40},{32,48},{40,56},{48,64},{56,72},{64,... | collective-permute-start | bytes 98312 | tf_op jit(solution)/shard_map/ppermute | solution.py:24
  146.6 10.6 %collective-permute-start.14 = (bf16[64,256]{1,0:T(8,128)(2,1)S(1)}, bf16[64,256]{1,0:T(8,128)(2,1)S(1)}, u32[]{:S(2)}, u32[]{:S(2)}) collective-permute-start(bf16[64,256]{1,0:T(8,128)(2,1)S(1)} %add_convert_fusion), channel_id=1, source_target_pairs={{0,32},{8,40},{16,48},{24,56},{32,64},{40,72},{48,80},{56,88},{64,... | collective-permute-start | bytes 98312 | tf_op jit(solution)/shard_map/ppermute | solution.py:39
  157.1 0.7 collective-permute-start.15
  157.8 11.0 %collective-permute-start.16 = (bf16[64,256]{1,0:T(8,128)(2,1)S(1)}, bf16[64,256]{1,0:T(8,128)(2,1)S(1)}, u32[]{:S(2)}, u32[]{:S(2)}) collective-permute-start(bf16[64,256]{1,0:T(8,128)(2,1)S(1)} %fusion.11), channel_id=1, source_target_pairs={{0,4},{4,0},{1,5},{5,1},{2,6},{6,2},{3,7},{7,3},{8,12},{12,8},{9,1... | collective-permute-start | bytes 98312 | tf_op jit(solution)/shard_map/ppermute | solution.py:28
Sparse Core Ops, SparseCore 0:
  42.4 76.6 all-gather.1

commit v8 on v7

--- a/solution.py
+++ b/solution.py
@@ -12,7 +12,7 @@
 HEAD = 128
 CORES = 2
 EXTRA = 16
-GATHER_AFTER = 2
+GATHER_AFTER = 3
 STEP = ("chip", "core")
 REP_STEP = ("rep", "chip", "core")
 epsilon = 1e-06

time: 177 us -> 175 us (0.989)
  starting transfers between devices: 88.3 us -> 82.5 us
  waiting for transfers between devices: 23.9 us -> 27.1 us
    ppermute x10, starting transfers between devices: 30.4 us -> 24.8 us  [send_by_core(): return lax.ppermute(value, ('chip', 'core'), pairs)]
where the time goes in v8:
time: 175 us; the launch traced here: 174 us
  starting transfers between devices  82.5 us (47%)
  waiting for transfers between devices  27.1 us (15%)
  Pallas kernels  17.6 us (10%)
  between operations  16.8 us (10%)
  other arithmetic  14.1 us (8%)
  matrix products  11.5 us (7%)
  local copies, waits for them, and re-layouts  4.08 us (2%)
    ppermute x5, starting transfers between devices, swap_cores(): return lax.ppermute(value, 'core', [(0, 1), (1, 0)])  44.2 us
    ppermute x10, starting transfers between devices, send_by_core(): return lax.ppermute(value, ('chip', 'core'), pairs)  24.8 us
    ppermute x10, waiting for transfers between devices, send_by_core(): return lax.ppermute(value, ('chip', 'core'), pairs)  12.1 us
    all_to_all x1, waiting for transfers between devices, per_device(): attended = lax.all_to_all(attended, 'patch', 0, 0, tiled=True)  10.3 us
    pallas_call x1, Pallas kernels, attention(): pl.pallas_call(functools.partial(attention_body, parts, rows, tile), grid...  10 us
    dot_general x1, matrix products, per_device(): lax.dot_general(attended, all_out_weight, (((1,), (1,)), ((), ())), prefe...  5.47 us
    all_to_all x1, starting transfers between devices, per_device(): packed = lax.all_to_all(done[2], 'patch', 0, 0, tiled=True)  4.57 us
    ppermute x2, starting transfers between devices, shift(): return lax.ppermute(value, axis, pairs)  4.55 us
  transfers between devices with their start and end apart: 20, of which 11 were waited for; matrix products, arithmetic and copies ran while one was open for 11% of the time, Pallas kernels for 10%

profile of v8, /device:TPU:33, one launch (start us, length us, event | category | flops | bytes accessed | tf_op | source)
XLA Modules:
  0.0 173.7 jit_solution(17494319153298665114)
XLA Ops:
  6.6 0.9 constant_dynamic-slice_fusion
  7.5 20.4 %collective-permute-start = (bf16[96,384]{1,0:T(8,128)(2,1)S(1)}, bf16[96,384]{1,0:T(8,128)(2,1)S(1)}, u32[]{:S(2)}, u32[]{:S(2)}) collective-permute-start(bf16[96,384]{1,0:T(8,128)(2,1)S(1)} %constant_dynamic-slice_fusion), channel_id=1, source_target_pairs={{0,4},{4,0},{1,5},{5,1},{2,6},{6,2},{3,7},{7,3},{8,12},{12,8},{9,1... | collective-permute-start | bytes 221192 | tf_op jit(solution)/shard_map/ppermute | solution.py:28
  27.9 0.9 collective-permute-done
  28.8 0.9 broadcast_select_fusion.1
  29.8 3.2 %collective-permute-start.1 = (bf16[192,384]{1,0:T(8,128)(2,1)S(1)}, bf16[192,384]{1,0:T(8,128)(2,1)}, u32[]{:S(2)}, u32[]{:S(2)}) collective-permute-start(bf16[192,384]{1,0:T(8,128)(2,1)S(1)} %pad_maximum_fusion.3.refs_0_), channel_id=1, source_target_pairs={{0,8},{8,16},{16,24},{24,32},{32,40},{40,48},{48,56},{56,64},{64,7... | collective-permute-start | bytes 442376 | tf_op jit(solution)/shard_map/ppermute | solution.py:39
  33.0 1.7 fusion.19
  34.7 0.0 copy-start.6
  34.7 0.5 multiply_reduce_fusion.1
  35.2 0.6 add_sqrt_fusion
  35.7 2.6 %collective-permute-start.2 = (bf16[192,384]{1,0:T(8,128)(2,1)}, bf16[192,384]{1,0:T(8,128)(2,1)}, u32[]{:S(2)}, u32[]{:S(2)}) collective-permute-start(bf16[192,384]{1,0:T(8,128)(2,1)} %collective-permute-done.1.refs_1_), channel_id=1, source_target_pairs={{0,8},{8,16},{16,24},{24,32},{32,40},{40,48},{48,56},{56,64},{64,7... | collective-permute-start | bytes 442376 | tf_op jit(solution)/shard_map/ppermute | solution.py:39
  38.3 3.9 %pack.1 = bf16[4,720,384]{2,1,0:T(8,128)(2,1)} custom-call(bf16[320,1536]{1,0:T(8,128)(2,1)} %bitcast.37, bf16[320,1536]{1,0:T(8,128)(2,1)} %bitcast.38, f32[64,256]{1,0:T(8,128)} %bitcast.41, f32[1,256]{1,0:T(1,128)} %bitcast.47), custom_call_target="tpu_custom_call" | custom-call | flops 1105920 | bytes 4423680 | tf_op jit(solution)/shard_map/pack/pallas_call | solution.py:149
  42.2 1.6 collective-permute-start.3
  43.8 2.7 %collective-permute-done.3.refs_3_ = bf16[192,384]{1,0:T(8,128)(2,1)} collective-permute-done((bf16[192,384]{1,0:T(8,128)(2,1)}, bf16[192,384]{1,0:T(8,128)(2,1)}, u32[]{:S(2)}, u32[]{:S(2)}) %collective-permute-start.3) | collective-permute-done | bytes 147488 | tf_op jit(solution)/shard_map/ppermute | solution.py:39
  46.6 0.1 all-gather.2.cloned.1.call-update
  47.3 0.7 select_reduce_fusion
  48.7 2.9 %collective-permute-start.4 = (bf16[192,384]{1,0:T(8,128)(2,1)}, bf16[192,384]{1,0:T(8,128)(2,1)}, u32[]{:S(2)}, u32[]{:S(2)}) collective-permute-start(bf16[192,384]{1,0:T(8,128)(2,1)} %collective-permute-done.3.refs_3_), channel_id=1, source_target_pairs={{0,8},{8,16},{16,24},{24,32},{32,40},{40,48},{48,56},{56,64},{64,7... | collective-permute-start | bytes 442376 | tf_op jit(solution)/shard_map/ppermute | solution.py:39
  51.6 3.7 %fusion.20 = f32[1,9216]{1,0:T(1,128)} fusion(bf16[256,1]{0,1:T(2,128)(2,1)S(1)} %reshape.58, bf16[256,9216]{1,0:T(8,128)(2,1)} %param.18), kind=kOutput, calls=%fused_computation.60 | convolution fusion | flops 4718592 | bytes 4755968 | tf_op jit(solution)/shard_map/dot_general | solution.py:278
  56.4 0.0 collective-permute-done.4.refs_4_
  56.4 0.6 collective-permute-start.5
  57.1 0.1 pad.12.clone
  57.2 4.6 %all-to-all-start = ((bf16[4,720,384]{2,1,0:T(8,128)(2,1)}), bf16[4,720,384]{2,1,0:T(8,128)(2,1)}, u32[]{:S(2)}, u32[]{:S(2)}) async-start(bf16[4,720,384]{2,1,0:T(8,128)(2,1)} %pack.1), calls=%async_computation | async-start | bytes 4423680 | tf_op jit(solution)/shard_map/all_to_all | solution.py:318
  61.7 1.3 collective-permute-done.5.refs_5_
  63.0 0.7 reduce_sum.77
  64.4 2.3 %collective-permute-start.6 = (bf16[192,384]{1,0:T(8,128)(2,1)}, bf16[192,384]{1,0:T(8,128)(2,1)S(1)}, u32[]{:S(2)}, u32[]{:S(2)}) collective-permute-start(bf16[192,384]{1,0:T(8,128)(2,1)} %collective-permute-done.5.refs_5_), channel_id=1, source_target_pairs={{0,8},{8,16},{16,24},{24,32},{32,40},{40,48},{48,56},{56,64},{64,7... | collective-permute-start | bytes 442376 | tf_op jit(solution)/shard_map/ppermute | solution.py:39
  66.7 1.1 convert_reduce_fusion
  67.9 0.7 slice_add_fusion
  68.6 1.1 convert_subtract_fusion
  69.7 0.1 maximum_multiply_fusion
  69.8 0.0 copy-start.7
  69.8 0.2 subtract_convert_fusion
  70.0 0.1 fusion.3
  70.1 1.0 pad_maximum_fusion.source_ref
  71.2 0.3 collective-permute-done.6.refs_6_
  71.4 3.4 %collective-permute-start.7 = (bf16[192,384]{1,0:T(8,128)(2,1)S(1)}, bf16[192,384]{1,0:T(8,128)(2,1)S(1)}, u32[]{:S(2)}, u32[]{:S(2)}) collective-permute-start(bf16[192,384]{1,0:T(8,128)(2,1)S(1)} %collective-permute-done.6.refs_6_), channel_id=1, source_target_pairs={{0,8},{8,16},{16,24},{24,32},{32,40},{40,48},{48,56},{56,64},{64,7... | collective-permute-start | bytes 442376 | tf_op jit(solution)/shard_map/ppermute | solution.py:39
  74.8 2.0 %pad_maximum_fusion.1 = bf16[768,384]{1,0:T(8,128)(2,1)} fusion(bf16[192,384]{1,0:T(8,128)(2,1)} %collective-permute-done.4.refs_4_, bf16[192,384]{1,0:T(8,128)(2,1)} %collective-permute-done.3.refs_3_, bf16[192,384]{1,0:T(8,128)(2,1)} %collective-permute-done.2.refs_2_, bf16[192,384]{1,0:T(8,128)(2,1)} %collective-permute-done.1.refs_1_), kind=kLoop, calls=%fused_computation.15 | loop fusion | flops 2359296 | bytes 1179648 | tf_op jit(solution)/shard_map/concatenate | solution.py:58
  76.9 4.8 %collective-permute-start.9 = (bf16[768,384]{1,0:T(8,128)(2,1)}, bf16[768,384]{1,0:T(8,128)(2,1)}, u32[]{:S(2)}, u32[]{:S(2)}) collective-permute-start(bf16[768,384]{1,0:T(8,128)(2,1)} %pad_maximum_fusion.1), channel_id=1, source_target_pairs={{0,4},{4,0},{1,5},{5,1},{2,6},{6,2},{3,7},{7,3},{8,12},{12,8},{9,1... | collective-permute-start | bytes 1769480 | tf_op jit(solution)/shard_map/ppermute | solution.py:28
  81.7 1.8 %pad_maximum_fusion.2 = bf16[576,384]{1,0:T(8,128)(2,1)} fusion(bf16[192,384]{1,0:T(8,128)(2,1)S(1)} %collective-permute-done.7.refs_7_, bf16[192,384]{1,0:T(8,128)(2,1)S(1)} %collective-permute-done.6.refs_6_, bf16[192,384]{1,0:T(8,128)(2,1)} %collective-permute-done.5.refs_5_), kind=kLoop, calls=%fused_computation.16 | loop fusion | flops 1327104 | bytes 884736 | tf_op jit(solution)/shard_map/concatenate | solution.py:58
  83.5 6.5 %collective-permute-start.10 = (bf16[576,384]{1,0:T(8,128)(2,1)}, bf16[576,384]{1,0:T(8,128)(2,1)}, u32[]{:S(2)}, u32[]{:S(2)}) collective-permute-start(bf16[576,384]{1,0:T(8,128)(2,1)} %pad_maximum_fusion.2), channel_id=1, source_target_pairs={{0,4},{4,0},{1,5},{5,1},{2,6},{6,2},{3,7},{7,3},{8,12},{12,8},{9,1... | collective-permute-start | bytes 1327112 | tf_op jit(solution)/shard_map/ppermute | solution.py:28
  90.0 0.0 collective-permute-start.8
  90.0 0.6 compare_select_fusion.place_ref
  90.6 6.8 %collective-permute-done.8.refs_8_ = bf16[192,384]{1,0:T(8,128)(2,1)} collective-permute-done((bf16[192,384]{1,0:T(8,128)(2,1)}, bf16[192,384]{1,0:T(8,128)(2,1)}, u32[]{:S(2)}, u32[]{:S(2)}) %collective-permute-start.8) | collective-permute-done | bytes 147488 | tf_op jit(solution)/shard_map/ppermute | solution.py:39
  97.4 3.7 %project.1.project_ref = bf16[3,160,256]{2,1,0:T(8,128)(2,1)} custom-call(s32[16]{0:T(128)} %compare_select_fusion.place_ref, bf16[160,3072]{1,0:T(8,128)(2,1)} %pad_maximum_fusion.source_ref, bf16[192,384]{1,0:T(8,128)(2,1)} %copy-done.3, bf16[192,384]{1,0:T(8,128)(2,1)} %collective-permute-done.1.refs_1_, bf16[192,384]{1,0:T(8,128)(2,1)} %collective-permute-done.2.refs_2_, ...), custom_call_target="tpu_custom_call" | custom-call | flops 377487360 | bytes 5701632 | tf_op jit(solution)/shard_map/project/pallas_call | solution.py:101
  101.0 10.0 %attention.1 = bf16[4,256,384]{2,1,0:T(8,128)(2,1)} custom-call(bf16[4,720,384]{2,1,0:T(8,128)(2,1)} %all-to-all-done.packed_ref, bf16[3,160,256]{2,1,0:T(8,128)(2,1)} %project.1.project_ref, f32[1,128]{1,0:T(1,128)} %bitcast.48), custom_call_target="tpu_custom_call" | custom-call | flops 2013265920 | bytes 4325376 | tf_op jit(solution)/shard_map/attention/pallas_call | solution.py:203
  111.1 4.3 %all-to-all-start.1 = ((bf16[4,256,384]{2,1,0:T(8,128)(2,1)}), bf16[4,256,384]{2,1,0:T(8,128)(2,1)}, u32[]{:S(2)}, u32[]{:S(2)}) async-start(bf16[4,256,384]{2,1,0:T(8,128)(2,1)} %attention.1), calls=%async_computation.1 | async-start | bytes 1572864 | tf_op jit(solution)/shard_map/all_to_all | solution.py:322
  115.4 0.7 slice.9
  116.1 10.3 %all-to-all-done.1 = bf16[4,256,384]{2,1,0:T(8,128)(2,1)} async-done(((bf16[4,256,384]{2,1,0:T(8,128)(2,1)}), bf16[4,256,384]{2,1,0:T(8,128)(2,1)}, u32[]{:S(2)}, u32[]{:S(2)}) %all-to-all-start.1) | async-done | bytes 786464 | tf_op jit(solution)/shard_map/all_to_all | solution.py:322
  126.4 2.3 %copy.15 = bf16[256,4,384]{0,2,1:T(8,128)(2,1)} copy(bf16[256,4,384]{2,0,1:T(8,128)(2,1)} %bitcast.12) | data formatting | bytes 1572864 | tf_op jit(solution)/shard_map/transpose | solution.py:323
  128.7 5.5 %fusion.21 = f32[256,3072]{1,0:T(8,128)S(1)} fusion(bf16[256,1536]{0,1:T(8,128)(2,1)} %bitcast.39, bf16[3072,1536]{1,0:T(8,128)(2,1)} %all-gather.2.cloned.1.call-done), kind=kOutput, calls=%fused_computation.61 | convolution fusion | flops 2415919104 | bytes 13369344 | tf_op jit(solution)/shard_map/dot_general | solution.py:324
  134.2 0.8 fusion.18
  135.0 0.0 copy-start.5
  135.0 0.5 multiply_reduce_fusion
  135.5 0.7 bitcast_convert_fusion
  136.2 2.4 %collective-permute-start.11 = (bf16[64,256]{1,0:T(8,128)(2,1)S(1)}, bf16[64,256]{1,0:T(8,128)(2,1)S(1)}, u32[]{:S(2)}, u32[]{:S(2)}) collective-permute-start(bf16[64,256]{1,0:T(8,128)(2,1)S(1)} %get-tuple-element.63), channel_id=1, source_target_pairs={{0,4},{4,0},{1,5},{5,1},{2,6},{6,2},{3,7},{7,3},{8,12},{12,8},{9,1... | collective-permute-start | bytes 98312 | tf_op jit(solution)/shard_map/ppermute | solution.py:28
  138.5 0.9 collective-permute-done.11
  139.4 1.3 collective-permute-start.12
  140.7 1.0 collective-permute-done.12
  141.7 3.2 %collective-permute-start.13 = (bf16[64,256]{1,0:T(8,128)(2,1)S(1)}, bf16[64,256]{1,0:T(8,128)(2,1)S(1)}, u32[]{:S(2)}, u32[]{:S(2)}) collective-permute-start(bf16[64,256]{1,0:T(8,128)(2,1)S(1)} %fusion.10), channel_id=1, source_target_pairs={{0,16},{8,24},{16,32},{24,40},{32,48},{40,56},{48,64},{56,72},{64,... | collective-permute-start | bytes 98312 | tf_op jit(solution)/shard_map/ppermute | solution.py:24
  145.0 1.0 collective-permute-done.13
  146.0 7.5 %collective-permute-start.14 = (bf16[64,256]{1,0:T(8,128)(2,1)S(1)}, bf16[64,256]{1,0:T(8,128)(2,1)S(1)}, u32[]{:S(2)}, u32[]{:S(2)}) collective-permute-start(bf16[64,256]{1,0:T(8,128)(2,1)S(1)} %add_convert_fusion), channel_id=1, source_target_pairs={{0,32},{8,40},{16,48},{24,56},{32,64},{40,72},{48,80},{56,88},{64,... | collective-permute-start | bytes 98312 | tf_op jit(solution)/shard_map/ppermute | solution.py:39
  153.5 1.0 collective-permute-done.14
  154.5 0.7 collective-permute-start.15
  155.2 10.1 %collective-permute-start.16 = (bf16[64,256]{1,0:T(8,128)(2,1)S(1)}, bf16[64,256]{1,0:T(8,128)(2,1)S(1)}, u32[]{:S(2)}, u32[]{:S(2)}) collective-permute-start(bf16[64,256]{1,0:T(8,128)(2,1)S(1)} %fusion.11), channel_id=1, source_target_pairs={{0,4},{4,0},{1,5},{5,1},{2,6},{6,2},{3,7},{7,3},{8,12},{12,8},{9,1... | collective-permute-start | bytes 98312 | tf_op jit(solution)/shard_map/ppermute | solution.py:28
  165.3 0.9 collective-permute-done.16
  166.2 0.7 fusion.9
  (36 shorter events, 0.2 us)
Async XLA Ops:
  6.5 128.9 %copy-start = (bf16[3072,64]{0,1:T(8,128)(2,1)S(1)}, bf16[3072,64]{0,1:T(8,128)(2,1)}, u32[]{:S(2)}) copy-start(bf16[3072,64]{0,1:T(8,128)(2,1)} %param.26) | copy-start | bytes 1179652
  6.6 122.1 %all-gather.2.cloned.1.call-start = ((), (), s32[]{:S(2)}) async-start(), calls=%async_computation.2 | async-start | bytes 9732096 | tf_op jit(solution)/shard_map/all_gather | solution.py:317
  7.5 21.3 %collective-permute-start = (bf16[96,384]{1,0:T(8,128)(2,1)S(1)}, bf16[96,384]{1,0:T(8,128)(2,1)S(1)}, u32[]{:S(2)}, u32[]{:S(2)}) collective-permute-start(bf16[96,384]{1,0:T(8,128)(2,1)S(1)} %constant_dynamic-slice_fusion), channel_id=1, source_target_pairs={{0,4},{4,0},{1,5},{5,1},{2,6},{6,2},{3,7},{7,3},{8,12},{12,8},{9,1... | collective-permute-start | bytes 221192 | tf_op jit(solution)/shard_map/ppermute | solution.py:28
  29.8 5.4 %copy-start.3 = (bf16[192,384]{1,0:T(8,128)(2,1)}, bf16[192,384]{1,0:T(8,128)(2,1)S(1)}, u32[]{:S(2)}) copy-start(bf16[192,384]{1,0:T(8,128)(2,1)S(1)} %pad_maximum_fusion.3.refs_0_) | copy-start | bytes 442372
  29.8 6.0 %collective-permute-start.1 = (bf16[192,384]{1,0:T(8,128)(2,1)S(1)}, bf16[192,384]{1,0:T(8,128)(2,1)}, u32[]{:S(2)}, u32[]{:S(2)}) collective-permute-start(bf16[192,384]{1,0:T(8,128)(2,1)S(1)} %pad_maximum_fusion.3.refs_0_), channel_id=1, source_target_pairs={{0,8},{8,16},{16,24},{24,32},{32,40},{40,48},{48,56},{56,64},{64,7... | collective-permute-start | bytes 442376 | tf_op jit(solution)/shard_map/ppermute | solution.py:39
  34.7 12.6 %copy-start.6 = (f32[1000]{0:T(1024)S(1)}, f32[1000]{0:T(1024)}, u32[]{:S(2)}) copy-start(f32[1000]{0:T(1024)} %param.17) | copy-start | bytes 12004
  35.7 6.5 %collective-permute-start.2 = (bf16[192,384]{1,0:T(8,128)(2,1)}, bf16[192,384]{1,0:T(8,128)(2,1)}, u32[]{:S(2)}, u32[]{:S(2)}) collective-permute-start(bf16[192,384]{1,0:T(8,128)(2,1)} %collective-permute-done.1.refs_1_), channel_id=1, source_target_pairs={{0,8},{8,16},{16,24},{24,32},{32,40},{40,48},{48,56},{56,64},{64,7... | collective-permute-start | bytes 442376 | tf_op jit(solution)/shard_map/ppermute | solution.py:39
  42.2 4.3 %collective-permute-start.3 = (bf16[192,384]{1,0:T(8,128)(2,1)}, bf16[192,384]{1,0:T(8,128)(2,1)}, u32[]{:S(2)}, u32[]{:S(2)}) collective-permute-start(bf16[192,384]{1,0:T(8,128)(2,1)} %collective-permute-done.2.refs_2_), channel_id=1, source_target_pairs={{0,8},{8,16},{16,24},{24,32},{32,40},{40,48},{48,56},{56,64},{64,7... | collective-permute-start | bytes 442376 | tf_op jit(solution)/shard_map/ppermute | solution.py:39
  48.7 7.8 %collective-permute-start.4 = (bf16[192,384]{1,0:T(8,128)(2,1)}, bf16[192,384]{1,0:T(8,128)(2,1)}, u32[]{:S(2)}, u32[]{:S(2)}) collective-permute-start(bf16[192,384]{1,0:T(8,128)(2,1)} %collective-permute-done.3.refs_3_), channel_id=1, source_target_pairs={{0,8},{8,16},{16,24},{24,32},{32,40},{40,48},{48,56},{56,64},{64,7... | collective-permute-start | bytes 442376 | tf_op jit(solution)/shard_map/ppermute | solution.py:39
  55.2 7.8 %copy-start.4 = (f32[3072]{0:T(1024)S(1)}, f32[3072]{0:T(1024)}, u32[]{:S(2)}) copy-start(f32[3072]{0:T(1024)} %param.20) | copy-start | bytes 36868
  56.4 6.6 %collective-permute-start.5 = (bf16[192,384]{1,0:T(8,128)(2,1)}, bf16[192,384]{1,0:T(8,128)(2,1)}, u32[]{:S(2)}, u32[]{:S(2)}) collective-permute-start(bf16[192,384]{1,0:T(8,128)(2,1)} %collective-permute-done.4.refs_4_), channel_id=1, source_target_pairs={{0,8},{8,16},{16,24},{24,32},{32,40},{40,48},{48,56},{56,64},{64,7... | collective-permute-start | bytes 442376 | tf_op jit(solution)/shard_map/ppermute | solution.py:39
  57.2 43.9 %all-to-all-start = ((bf16[4,720,384]{2,1,0:T(8,128)(2,1)}), bf16[4,720,384]{2,1,0:T(8,128)(2,1)}, u32[]{:S(2)}, u32[]{:S(2)}) async-start(bf16[4,720,384]{2,1,0:T(8,128)(2,1)} %pack.1), calls=%async_computation | async-start | bytes 4423680 | tf_op jit(solution)/shard_map/all_to_all | solution.py:318
  64.4 7.0 %collective-permute-start.6 = (bf16[192,384]{1,0:T(8,128)(2,1)}, bf16[192,384]{1,0:T(8,128)(2,1)S(1)}, u32[]{:S(2)}, u32[]{:S(2)}) collective-permute-start(bf16[192,384]{1,0:T(8,128)(2,1)} %collective-permute-done.5.refs_5_), channel_id=1, source_target_pairs={{0,8},{8,16},{16,24},{24,32},{32,40},{40,48},{48,56},{56,64},{64,7... | collective-permute-start | bytes 442376 | tf_op jit(solution)/shard_map/ppermute | solution.py:39
  69.8 20.2 %copy-start.7 = (s32[16]{0:T(128)S(1)}, s32[16]{0:T(128)}, u32[]{:S(2)}) copy-start(s32[16]{0:T(128)} %constant.60.clone) | copy-start | bytes 196
  71.4 10.3 %copy-start.1 = (bf16[192,384]{1,0:T(8,128)(2,1)}, bf16[192,384]{1,0:T(8,128)(2,1)S(1)}, u32[]{:S(2)}) copy-start(bf16[192,384]{1,0:T(8,128)(2,1)S(1)} %collective-permute-done.6.refs_6_) | copy-start | bytes 442372
  71.4 10.3 %collective-permute-start.7 = (bf16[192,384]{1,0:T(8,128)(2,1)S(1)}, bf16[192,384]{1,0:T(8,128)(2,1)S(1)}, u32[]{:S(2)}, u32[]{:S(2)}) collective-permute-start(bf16[192,384]{1,0:T(8,128)(2,1)S(1)} %collective-permute-done.6.refs_6_), channel_id=1, source_target_pairs={{0,8},{8,16},{16,24},{24,32},{32,40},{40,48},{48,56},{56,64},{64,7... | collective-permute-start | bytes 442376 | tf_op jit(solution)/shard_map/ppermute | solution.py:39
  76.9 20.5 %collective-permute-start.9 = (bf16[768,384]{1,0:T(8,128)(2,1)}, bf16[768,384]{1,0:T(8,128)(2,1)}, u32[]{:S(2)}, u32[]{:S(2)}) collective-permute-start(bf16[768,384]{1,0:T(8,128)(2,1)} %pad_maximum_fusion.1), channel_id=1, source_target_pairs={{0,4},{4,0},{1,5},{5,1},{2,6},{6,2},{3,7},{7,3},{8,12},{12,8},{9,1... | collective-permute-start | bytes 1769480 | tf_op jit(solution)/shard_map/ppermute | solution.py:28
  81.7 1.8 %copy-start.2 = (bf16[192,384]{1,0:T(8,128)(2,1)}, bf16[192,384]{1,0:T(8,128)(2,1)S(1)}, u32[]{:S(2)}) copy-start(bf16[192,384]{1,0:T(8,128)(2,1)S(1)} %collective-permute-done.7.refs_7_) | copy-start | bytes 442372
  83.5 13.9 %collective-permute-start.10 = (bf16[576,384]{1,0:T(8,128)(2,1)}, bf16[576,384]{1,0:T(8,128)(2,1)}, u32[]{:S(2)}, u32[]{:S(2)}) collective-permute-start(bf16[576,384]{1,0:T(8,128)(2,1)} %pad_maximum_fusion.2), channel_id=1, source_target_pairs={{0,4},{4,0},{1,5},{5,1},{2,6},{6,2},{3,7},{7,3},{8,12},{12,8},{9,1... | collective-permute-start | bytes 1327112 | tf_op jit(solution)/shard_map/ppermute | solution.py:28
  90.0 7.4 %collective-permute-start.8 = (bf16[192,384]{1,0:T(8,128)(2,1)}, bf16[192,384]{1,0:T(8,128)(2,1)}, u32[]{:S(2)}, u32[]{:S(2)}) collective-permute-start(bf16[192,384]{1,0:T(8,128)(2,1)} %copy-done.2), channel_id=1, source_target_pairs={{0,8},{8,16},{16,24},{24,32},{32,40},{40,48},{48,56},{56,64},{64,7... | collective-permute-start | bytes 442376 | tf_op jit(solution)/shard_map/ppermute | solution.py:39
  111.1 15.3 %all-to-all-start.1 = ((bf16[4,256,384]{2,1,0:T(8,128)(2,1)}), bf16[4,256,384]{2,1,0:T(8,128)(2,1)}, u32[]{:S(2)}, u32[]{:S(2)}) async-start(bf16[4,256,384]{2,1,0:T(8,128)(2,1)} %attention.1), calls=%async_computation.1 | async-start | bytes 1572864 | tf_op jit(solution)/shard_map/all_to_all | solution.py:322
  135.0 31.2 %copy-start.5 = (f32[256,64]{0,1:T(8,128)S(1)}, f32[256,64]{0,1:T(8,128)}, u32[]{:S(2)}) copy-start(f32[256,64]{0,1:T(8,128)} %param.15) | copy-start | bytes 196612
  136.2 3.2 %collective-permute-start.11 = (bf16[64,256]{1,0:T(8,128)(2,1)S(1)}, bf16[64,256]{1,0:T(8,128)(2,1)S(1)}, u32[]{:S(2)}, u32[]{:S(2)}) collective-permute-start(bf16[64,256]{1,0:T(8,128)(2,1)S(1)} %get-tuple-element.63), channel_id=1, source_target_pairs={{0,4},{4,0},{1,5},{5,1},{2,6},{6,2},{3,7},{7,3},{8,12},{12,8},{9,1... | collective-permute-start | bytes 98312 | tf_op jit(solution)/shard_map/ppermute | solution.py:28
  139.4 2.3 %collective-permute-start.12 = (bf16[64,256]{1,0:T(8,128)(2,1)S(1)}, bf16[64,256]{1,0:T(8,128)(2,1)S(1)}, u32[]{:S(2)}, u32[]{:S(2)}) collective-permute-start(bf16[64,256]{1,0:T(8,128)(2,1)S(1)} %fusion.13), channel_id=1, source_target_pairs={{0,8},{8,16},{16,24},{24,32},{32,40},{40,48},{48,56},{56,64},{64,7... | collective-permute-start | bytes 98312 | tf_op jit(solution)/shard_map/ppermute | solution.py:24
  141.7 4.3 %collective-permute-start.13 = (bf16[64,256]{1,0:T(8,128)(2,1)S(1)}, bf16[64,256]{1,0:T(8,128)(2,1)S(1)}, u32[]{:S(2)}, u32[]{:S(2)}) collective-permute-start(bf16[64,256]{1,0:T(8,128)(2,1)S(1)} %fusion.10), channel_id=1, source_target_pairs={{0,16},{8,24},{16,32},{24,40},{32,48},{40,56},{48,64},{56,72},{64,... | collective-permute-start | bytes 98312 | tf_op jit(solution)/shard_map/ppermute | solution.py:24
  146.0 8.5 %collective-permute-start.14 = (bf16[64,256]{1,0:T(8,128)(2,1)S(1)}, bf16[64,256]{1,0:T(8,128)(2,1)S(1)}, u32[]{:S(2)}, u32[]{:S(2)}) collective-permute-start(bf16[64,256]{1,0:T(8,128)(2,1)S(1)} %add_convert_fusion), channel_id=1, source_target_pairs={{0,32},{8,40},{16,48},{24,56},{32,64},{40,72},{48,80},{56,88},{64,... | collective-permute-start | bytes 98312 | tf_op jit(solution)/shard_map/ppermute | solution.py:39
  154.5 0.7 collective-permute-start.15
  155.2 11.0 %collective-permute-start.16 = (bf16[64,256]{1,0:T(8,128)(2,1)S(1)}, bf16[64,256]{1,0:T(8,128)(2,1)S(1)}, u32[]{:S(2)}, u32[]{:S(2)}) collective-permute-start(bf16[64,256]{1,0:T(8,128)(2,1)S(1)} %fusion.11), channel_id=1, source_target_pairs={{0,4},{4,0},{1,5},{5,1},{2,6},{6,2},{3,7},{7,3},{8,12},{12,8},{9,1... | collective-permute-start | bytes 98312 | tf_op jit(solution)/shard_map/ppermute | solution.py:28
Sparse Core Ops, SparseCore 0:
  46.7 78.3 all-gather.1
